TPU v7x, 32 devices: a whole 2x2x4 slice. The times are simulated.
32 devices in a mesh: wide: 8 (over z, y), narrow: 4 (over x, core).
Axes of the slice: x: 2, y: 2, z: 4, core: 2. Of those that a mesh axis runs over, the one named last changes fastest.
Arguments:
- tokens: bfloat16 [8192, 2304], P(('wide', 'narrow')), may hold values from -6 to 6
- norm_attn: bfloat16 [2304], replicated, may hold values from 0.25 to 1.75
- norm_ffn: bfloat16 [2304], replicated, may hold values from 0.25 to 1.75
- w_query: bfloat16 [2304, 2304], P('wide', 'narrow'), may hold values from -0.125 to 0.125
- w_key: bfloat16 [2304, 2304], P('wide', 'narrow'), may hold values from -0.125 to 0.125
- w_value: bfloat16 [2304, 2304], P('wide', 'narrow'), may hold values from -0.125 to 0.125
- w_out: bfloat16 [2304, 2304], P('narrow', 'wide'), may hold values from -3 to 3
- w_gate: bfloat16 [2304, 5760], P('wide', 'narrow'), may hold values from -0.125 to 0.125
- w_up: bfloat16 [2304, 5760], P('wide', 'narrow'), may hold values from -0.125 to 0.125
- w_down: bfloat16 [5760, 2304], P('narrow', 'wide'), may hold values from -0.625 to 0.625
- cotangent: bfloat16 [8192, 2304], P(('wide', 'narrow')), may hold values from -6 to 6
- lengths: int32 [2, 8], replicated, may hold values from 0 to 1024, as said below
- deal: int32 [1024], replicated, may hold values from 0 to 1023, as said below
Outputs:
- output: bfloat16 [8192, 2304], P(('wide', 'narrow'))
- grad_tokens: bfloat16 [8192, 2304], P(('wide', 'narrow'))
- grad_norm_attn: float32 [2304], replicated
- grad_norm_ffn: float32 [2304], replicated
- grad_query: float32 [2304, 2304], P('wide', 'narrow')
- grad_key: float32 [2304, 2304], P('wide', 'narrow')
- grad_value: float32 [2304, 2304], P('wide', 'narrow')
- grad_out: float32 [2304, 2304], P('narrow', 'wide')
- grad_gate: float32 [2304, 5760], P('wide', 'narrow')
- grad_up: float32 [2304, 5760], P('wide', 'narrow')
- grad_down: float32 [5760, 2304], P('narrow', 'wide')
Inputs may be any that keep to these rules, and one draw needn't show every extreme that they name: Micro-batch 0: for each p, sequences 2p and 2p+1 fill stream rows 2p 512 to 2p 512 + 2 * 512 - 1 (their extents add up to 1024); sequence 0 has length 1024 and sequence 1 length 0. Micro-batch 1: sequence 0 has extent 512; for each p from 0 to 2, sequences 2p+1 and 2p+2 fill stream rows (2p+1) * 512 to (2p+3) * 512 - 1; the last sequence has extent 512; sequences 3 and 4 have lengths 1024 and 0. In both, the first sequence of each such pair has a length that is a multiple of 64. deal is a permutation of 0 .. 1023. Dealt block g and source block deal[g] lie on devices with the same index of narrow. For every two indices of wide, exactly 4 blocks of one device goes to the device with the other index of wide and the same index of narrow.
All inputs are finite; a program needn't handle non-finite values.
Results may differ from a plain program's by a relative error of at most 0.019.
Values may be sent and summed in bfloat16 or wider, within the bound.
A program may use at most 160 MiB of HBM per device.

v0:
```python
import math

import jax
import jax.numpy as jnp
from jax import lax
from jax.sharding import PartitionSpec as P

HEAD_DIM = 64
MB = 2
BLK = 8
UNIT = 64


BRANCH = 1.4 / math.sqrt(40.0)
EPSILON = 1e-05
NEGATIVE = -1e30


def passed_along(block, axis, distance):
    devices = range(lax.axis_size(axis))
    route = [(i - distance, i) for i in devices if i - distance in devices]
    return lax.ppermute(block, axis, route)


def rotate(field_in, position, direction):
    head_count = field_in.shape[1] // HEAD_DIM
    half_dim = HEAD_DIM // 2
    counter = jnp.arange(half_dim, dtype=jnp.float32)
    frequency = jnp.exp(counter * (-2.0 * math.log(10000.0) / HEAD_DIM))
    phase_angle = position.astype(jnp.float32)[:, None] * frequency[None, :]
    cosine = jnp.concatenate([jnp.cos(phase_angle), jnp.cos(phase_angle)], axis=1)[:, None, :]
    sine_table = jnp.concatenate([jnp.sin(phase_angle), jnp.sin(phase_angle)], axis=1)[:, None, :]
    shaped = field_in.reshape(field_in.shape[0], head_count, HEAD_DIM)
    turned = jnp.concatenate([-shaped[:, :, half_dim:], shaped[:, :, :half_dim]], axis=2)
    return (shaped * cosine + direction * turned * sine_table).reshape(field_in.shape)


def contract_rows(left, right):
    return lax.dot_general(
        left, right, (((0,), (0,)), ((), ())), preferred_element_type=jnp.float32
    )


def times_transpose(left, right):
    return lax.dot_general(
        left, right, (((1,), (1,)), ((), ())), preferred_element_type=jnp.float32
    )


def norm_rate(resid):
    return lax.rsqrt(jnp.mean(resid * resid, axis=1, keepdims=True) + EPSILON)


def norm_backward(grad_in, resid, rate, gain):
    scaled_grad = grad_in * gain[None, :]
    return rate * scaled_grad - resid * rate**3 * jnp.mean(
        scaled_grad * resid, axis=1, keepdims=True
    )


def invert_order(placing):
    counter = jnp.arange(placing.shape[0], dtype=jnp.int32)
    return jnp.sum(jnp.where(placing[None, :] == counter[:, None], counter[None, :], 0), axis=1)


def deal_routes(deal, my_rank, my_lane, rank_count, lane_count, block_count):
    per_pair = block_count // rank_count
    base_block = (my_rank * lane_count + my_lane) * block_count
    counter = jnp.arange(block_count, dtype=jnp.int32)
    every_block = jnp.arange(deal.shape[0], dtype=jnp.int32)
    owned = base_block + counter
    target = jnp.sum(jnp.where(deal[None, :] == owned[:, None], every_block[None, :], 0), axis=1)
    target_rank = target // (lane_count * block_count)
    target_slot = target % block_count
    earlier = (target_rank[None, :] == target_rank[:, None]) & (
        target_slot[None, :] < target_slot[:, None]
    )
    send_place = target_rank * per_pair + jnp.sum(earlier.astype(jnp.int32), axis=1)
    mine = lax.dynamic_slice_in_dim(deal, base_block, block_count)
    source_rank = mine // (lane_count * block_count)
    before = (source_rank[None, :] == source_rank[:, None]) & (counter[None, :] < counter[:, None])
    recv_place = source_rank * per_pair + jnp.sum(before.astype(jnp.int32), axis=1)
    return (send_place, recv_place)


def stream_layout(length_row, my_rank, slot_rows):
    extent = (length_row + UNIT - 1) // UNIT * UNIT
    begin = jnp.cumsum(extent) - extent
    places = my_rank * slot_rows - slot_rows + jnp.arange(2 * slot_rows, dtype=jnp.int32)
    ending = begin + length_row
    inside = (places[:, None] >= begin[None, :]) & (places[:, None] < ending[None, :])
    number = jnp.arange(length_row.shape[0], dtype=jnp.int32) + 1
    segment = jnp.sum(jnp.where(inside, number[None, :], 0), axis=1) - 1
    position = places - jnp.sum(jnp.where(inside, begin[None, :], 0), axis=1)
    return (segment, position)


def score_block(queries, keys_all, segment, slot_rows, head_count):
    query_three = queries.reshape(slot_rows, head_count, HEAD_DIM)
    key_three = keys_all.reshape(2 * slot_rows, head_count, HEAD_DIM)
    scores = jnp.einsum(
        "qhd,khd->hqk", query_three, key_three, preferred_element_type=jnp.float32
    ) * (1.0 / math.sqrt(HEAD_DIM))
    query_index = slot_rows + jnp.arange(slot_rows, dtype=jnp.int32)
    key_index = jnp.arange(2 * slot_rows, dtype=jnp.int32)
    query_segment = segment[slot_rows:]
    allowed = (query_segment[:, None] == segment[None, :]) & (query_segment[:, None] >= 0) & (
        key_index[None, :] <= query_index[:, None]
    ) | (key_index[None, :] == query_index[:, None])
    return jnp.where(allowed[None, :, :], scores, NEGATIVE)


def body(
    tokens,
    norm_attn,
    norm_ffn,
    w_query,
    w_key,
    w_value,
    w_out,
    w_gate,
    w_up,
    w_down,
    cotangent,
    lengths,
    deal,
):
    rank_count = lax.axis_size("wide")
    lane_count = lax.axis_size("narrow")
    my_rank = lax.axis_index("wide")
    my_lane = lax.axis_index("narrow")
    row_count = tokens.shape[0]
    width = tokens.shape[1]
    block_count = row_count // BLK
    per_pair = block_count // rank_count
    micro_rows = row_count // MB
    slot_rows = lane_count * micro_rows
    head_count = w_query.shape[1] // HEAD_DIM
    score_scale = 1.0 / math.sqrt(HEAD_DIM)
    send_place, recv_place = deal_routes(
        deal, my_rank, my_lane, rank_count, lane_count, block_count
    )
    send_order = invert_order(send_place)
    back_order = invert_order(recv_place)

    def pack_out(flat_rows):
        return flat_rows.reshape(block_count, BLK, width)[send_order].reshape(
            rank_count, per_pair * BLK, width
        )

    got_x, got_cot = (
        lax.all_to_all(pack_out(tokens), "wide", split_axis=0, concat_axis=0, tiled=True),
        lax.all_to_all(pack_out(cotangent), "wide", split_axis=0, concat_axis=0, tiled=True),
    )
    dealt_x = got_x.reshape(block_count, BLK, width)[recv_place].reshape(row_count, width)
    dealt_cot = got_cot.reshape(block_count, BLK, width)[recv_place].reshape(row_count, width)
    gain_attn = norm_attn.astype(jnp.float32)
    gain_ffn = norm_ffn.astype(jnp.float32)
    totals = None
    gain_total_attn = jnp.zeros((width,), jnp.float32)
    gain_total_ffn = jnp.zeros((width,), jnp.float32)
    out_parts = []
    grad_parts = []
    for micro in range(MB):
        weights_full = (
            lax.all_gather(w_query, "wide", axis=0, tiled=True),
            lax.all_gather(w_key, "wide", axis=0, tiled=True),
            lax.all_gather(w_value, "wide", axis=0, tiled=True),
            lax.all_gather(w_out, "wide", axis=1, tiled=True),
            lax.all_gather(w_gate, "wide", axis=0, tiled=True),
            lax.all_gather(w_up, "wide", axis=0, tiled=True),
            lax.all_gather(w_down, "wide", axis=1, tiled=True),
        )
        wq_full, wk_full, wv_full, wo_full, wg_full, wu_full, wd_full = weights_full
        segment, position = stream_layout(lengths[micro], my_rank, slot_rows)
        own_segment = lax.dynamic_slice_in_dim(
            segment, slot_rows + my_lane * micro_rows, micro_rows
        )
        validity = (own_segment >= 0).astype(jnp.float32)[:, None]
        query_pos = position[slot_rows:]
        x_rows = dealt_x[micro * micro_rows : (micro + 1) * micro_rows]
        cot_rows = dealt_cot[micro * micro_rows : (micro + 1) * micro_rows]
        resid = x_rows.astype(jnp.float32) * validity
        rate_attn = norm_rate(resid)
        attn_in = (resid * rate_attn * gain_attn[None, :]).astype(jnp.bfloat16)
        attn_rows, cot_all = (
            lax.all_gather(attn_in, "narrow", axis=0, tiled=True),
            lax.all_gather(cot_rows, "narrow", axis=0, tiled=True),
        )
        queries = rotate(
            jnp.dot(attn_rows, wq_full, preferred_element_type=jnp.float32), query_pos, 1.0
        ).astype(jnp.bfloat16)
        keys_own = rotate(
            jnp.dot(attn_rows, wk_full, preferred_element_type=jnp.float32), query_pos, 1.0
        ).astype(jnp.bfloat16)
        values_own = jnp.dot(attn_rows, wv_full, preferred_element_type=jnp.float32).astype(
            jnp.bfloat16
        )
        keys_prev, values_prev = passed_along((keys_own, values_own), "wide", 1)
        keys_all = jnp.concatenate([keys_prev, keys_own], axis=0)
        values_all = jnp.concatenate([values_prev, values_own], axis=0)
        scores = score_block(queries, keys_all, segment, slot_rows, head_count)
        top_score = jnp.max(scores, axis=2, keepdims=True)
        weights_exp = jnp.exp(scores - top_score)
        total_exp = jnp.sum(weights_exp, axis=2, keepdims=True)
        probs = weights_exp / total_exp
        log_total = top_score + jnp.log(total_exp)
        values_three = values_all.reshape(2 * slot_rows, head_count, HEAD_DIM)
        mixed = jnp.einsum(
            "hqk,khd->qhd",
            probs.astype(jnp.bfloat16),
            values_three,
            preferred_element_type=jnp.float32,
        )
        attn_out = mixed.reshape(slot_rows, head_count * HEAD_DIM).astype(jnp.bfloat16)
        branch_attn = lax.psum_scatter(
            jnp.dot(attn_out, wo_full, preferred_element_type=jnp.float32),
            "narrow",
            scatter_dimension=0,
            tiled=True,
        )
        middle = resid + BRANCH * branch_attn
        rate_ffn = norm_rate(middle)
        ffn_in = (middle * rate_ffn * gain_ffn[None, :]).astype(jnp.bfloat16)
        ffn_rows = lax.all_gather(ffn_in, "narrow", axis=0, tiled=True)
        gate = jnp.dot(ffn_rows, wg_full, preferred_element_type=jnp.float32)
        upward = jnp.dot(ffn_rows, wu_full, preferred_element_type=jnp.float32)
        sigma = jax.nn.sigmoid(gate)
        hidden = (gate * sigma * upward).astype(jnp.bfloat16)
        branch_ffn = lax.psum_scatter(
            jnp.dot(hidden, wd_full, preferred_element_type=jnp.float32).astype(jnp.bfloat16),
            "narrow",
            scatter_dimension=0,
            tiled=True,
        ).astype(jnp.float32)
        out_parts.append((middle + BRANCH * branch_ffn).astype(jnp.bfloat16))
        cot_branch = (BRANCH * cot_all.astype(jnp.float32)).astype(jnp.bfloat16)
        grad_wd = contract_rows(hidden, cot_branch)
        grad_hidden = times_transpose(cot_branch, wd_full)
        grad_gate = (grad_hidden * upward * sigma * (1.0 + gate * (1.0 - sigma))).astype(
            jnp.bfloat16
        )
        grad_upward = (grad_hidden * gate * sigma).astype(jnp.bfloat16)
        grad_wg = contract_rows(ffn_rows, grad_gate)
        grad_wu = contract_rows(ffn_rows, grad_upward)
        grad_ffn_in = lax.psum_scatter(
            times_transpose(grad_gate, wg_full) + times_transpose(grad_upward, wu_full),
            "narrow",
            scatter_dimension=0,
            tiled=True,
        )
        gain_total_ffn = gain_total_ffn + jnp.sum(grad_ffn_in * middle * rate_ffn, axis=0)
        grad_middle = cot_rows.astype(jnp.float32) + norm_backward(
            grad_ffn_in, middle, rate_ffn, gain_ffn
        )
        grad_branch = (BRANCH * grad_middle).astype(jnp.bfloat16)
        grad_branch_all = lax.all_gather(grad_branch, "narrow", axis=0, tiled=True)
        grad_wo = contract_rows(attn_out, grad_branch_all)
        grad_mixed = times_transpose(grad_branch_all, wo_full).astype(jnp.bfloat16)
        probs_again = jnp.exp(
            score_block(queries, keys_all, segment, slot_rows, head_count) - log_total
        )
        grad_three = grad_mixed.reshape(slot_rows, head_count, HEAD_DIM)
        grad_probs = jnp.einsum(
            "qhd,khd->hqk", grad_three, values_three, preferred_element_type=jnp.float32
        )
        grad_scores = (
            probs_again * (grad_probs - jnp.sum(probs_again * grad_probs, axis=2, keepdims=True))
        ).astype(jnp.bfloat16)
        key_three = keys_all.reshape(2 * slot_rows, head_count, HEAD_DIM)
        query_three = queries.reshape(slot_rows, head_count, HEAD_DIM)
        grad_queries = (
            jnp.einsum("hqk,khd->qhd", grad_scores, key_three, preferred_element_type=jnp.float32)
            * score_scale
        ).reshape(slot_rows, head_count * HEAD_DIM)
        grad_keys = (
            jnp.einsum("hqk,qhd->khd", grad_scores, query_three, preferred_element_type=jnp.float32)
            * score_scale
        ).reshape(2 * slot_rows, head_count * HEAD_DIM)
        grad_values = jnp.einsum(
            "hqk,qhd->khd",
            probs_again.astype(jnp.bfloat16),
            grad_three,
            preferred_element_type=jnp.float32,
        ).reshape(2 * slot_rows, head_count * HEAD_DIM)
        keys_back, values_back = (
            passed_along(grad_keys[:slot_rows].astype(jnp.bfloat16), "wide", -1).astype(
                jnp.float32
            ),
            passed_along(grad_values[:slot_rows].astype(jnp.bfloat16), "wide", -1).astype(
                jnp.float32
            ),
        )
        grad_q = rotate(grad_queries, query_pos, -1.0).astype(jnp.bfloat16)
        grad_k = rotate(grad_keys[slot_rows:] + keys_back, query_pos, -1.0).astype(jnp.bfloat16)
        grad_v = (grad_values[slot_rows:] + values_back).astype(jnp.bfloat16)
        grad_wq = contract_rows(attn_rows, grad_q)
        grad_wk = contract_rows(attn_rows, grad_k)
        grad_wv = contract_rows(attn_rows, grad_v)
        grad_attn_in = lax.psum_scatter(
            (
                times_transpose(grad_q, wq_full)
                + times_transpose(grad_k, wk_full)
                + times_transpose(grad_v, wv_full)
            ).astype(jnp.bfloat16),
            "narrow",
            scatter_dimension=0,
            tiled=True,
        ).astype(jnp.float32)
        gain_total_attn = gain_total_attn + jnp.sum(grad_attn_in * resid * rate_attn, axis=0)
        grad_resid = grad_middle + norm_backward(grad_attn_in, resid, rate_attn, gain_attn)
        grad_parts.append((validity * grad_resid).astype(jnp.bfloat16))
        local_grads = (grad_wq, grad_wk, grad_wv, grad_wo, grad_wg, grad_wu, grad_wd)
        if totals is None:
            totals = local_grads
        else:
            totals = tuple(
                (earlier_sum + newer_sum for earlier_sum, newer_sum in zip(totals, local_grads))
            )
    totals = (
        lax.psum_scatter(
            totals[0].astype(jnp.bfloat16), "wide", scatter_dimension=0, tiled=True
        ).astype(jnp.float32),
        lax.psum_scatter(
            totals[1].astype(jnp.bfloat16), "wide", scatter_dimension=0, tiled=True
        ).astype(jnp.float32),
        lax.psum_scatter(
            totals[2].astype(jnp.bfloat16), "wide", scatter_dimension=0, tiled=True
        ).astype(jnp.float32),
        lax.psum_scatter(
            totals[3].astype(jnp.bfloat16), "wide", scatter_dimension=1, tiled=True
        ).astype(jnp.float32),
        lax.psum_scatter(
            totals[4].astype(jnp.bfloat16), "wide", scatter_dimension=0, tiled=True
        ).astype(jnp.float32),
        lax.psum_scatter(
            totals[5].astype(jnp.bfloat16), "wide", scatter_dimension=0, tiled=True
        ).astype(jnp.float32),
        lax.psum_scatter(
            totals[6].astype(jnp.bfloat16), "wide", scatter_dimension=1, tiled=True
        ).astype(jnp.float32),
    )
    gain_sum_attn, gain_sum_ffn = lax.psum((gain_total_attn, gain_total_ffn), ("wide", "narrow"))
    out_dealt = jnp.concatenate(out_parts, axis=0)
    grad_dealt = jnp.concatenate(grad_parts, axis=0)

    def pack_back(flat_rows):
        return flat_rows.reshape(block_count, BLK, width)[back_order].reshape(
            rank_count, per_pair * BLK, width
        )

    got_out, got_grad = (
        lax.all_to_all(pack_back(out_dealt), "wide", split_axis=0, concat_axis=0, tiled=True),
        lax.all_to_all(pack_back(grad_dealt), "wide", split_axis=0, concat_axis=0, tiled=True),
    )
    output = got_out.reshape(block_count, BLK, width)[send_place].reshape(row_count, width)
    grad_tokens = got_grad.reshape(block_count, BLK, width)[send_place].reshape(row_count, width)
    return (
        output,
        grad_tokens,
        gain_sum_attn,
        gain_sum_ffn,
        totals[0],
        totals[1],
        totals[2],
        totals[3],
        totals[4],
        totals[5],
        totals[6],
    )


def solution(mesh):
    placed = (
        P(("wide", "narrow"), None),
        P(),
        P(),
        P("wide", "narrow"),
        P("wide", "narrow"),
        P("wide", "narrow"),
        P("narrow", "wide"),
        P("wide", "narrow"),
        P("wide", "narrow"),
        P("narrow", "wide"),
        P(("wide", "narrow"), None),
        P(),
        P(),
    )
    return jax.shard_map(
        body,
        mesh=mesh,
        in_specs=placed,
        out_specs=(
            P(("wide", "narrow"), None),
            P(("wide", "narrow"), None),
            P(),
            P(),
            P("wide", "narrow"),
            P("wide", "narrow"),
            P("wide", "narrow"),
            P("narrow", "wide"),
            P("wide", "narrow"),
            P("wide", "narrow"),
            P("narrow", "wide"),
        ),
        check_vma=False,
    )
```

profile of v0, /device:TPU:0, one launch (start us, length us, event | category | flops | bytes accessed | tf_op | source)
XLA Modules:
  0.0 2090.4 jit_solution(11321917345078120002)
XLA Ops:
  21.8 37.2 %all-to-all-done = bf16[8,32,2304]{2,1,0:T(8,128)(2,1)S(1)} async-done(((bf16[8,32,2304]{2,1,0:T(8,128)(2,1)}), bf16[8,32,2304]{2,1,0:T(8,128)(2,1)S(1)}, u32[]{:S(2)}, u32[]{:S(2)}) %all-to-all-start) | async-done | bytes 1179680 | tf_op jit(solution)/shard_map/all_to_all | solution.py:152
  87.6 24.9 %all-gather.34.cloned.1.call-done = bf16[512,2304]{1,0:T(8,128)(2,1)} async-done(((bf16[128,2304]{1,0:T(8,128)(2,1)}), bf16[512,2304]{1,0:T(8,128)(2,1)}) %all-gather.34.cloned.1.call-update) | async-done | bytes 2359312 | tf_op jit(solution)/shard_map/all_gather | solution.py:187
  118.7 54.3 %all-gather.22.cloned.1.call-done = bf16[2304,576]{1,0:T(8,128)(2,1)} async-done(((bf16[288,576]{1,0:T(8,128)(2,1)}), bf16[2304,576]{1,0:T(8,128)(2,1)}) %all-gather.22.cloned.1.call-update) | async-done | bytes 2654224 | tf_op jit(solution)/shard_map/all_gather | solution.py:167
  186.5 54.4 %all-gather.18.cloned.1.call-done = bf16[2304,576]{1,0:T(8,128)(2,1)} async-done(((bf16[288,576]{1,0:T(8,128)(2,1)}), bf16[2304,576]{1,0:T(8,128)(2,1)}) %all-gather.18.cloned.1.call-update) | async-done | bytes 2654224 | tf_op jit(solution)/shard_map/all_gather | solution.py:168
  281.0 25.7 %all-gather.24.cloned.1.call-done = bf16[576,2304]{0,1:T(8,128)(2,1)} async-done(((bf16[576,288]{0,1:T(8,128)(2,1)}), bf16[576,2304]{0,1:T(8,128)(2,1)}) %all-gather.24.cloned.1.call-update) | async-done | bytes 2654224 | tf_op jit(solution)/shard_map/all_gather | solution.py:169
  397.1 48.1 %reduce-scatter.16.cloned.1.call-done = f32[128,2304]{1,0:T(8,128)} async-done(((f32[512,2304]{1,0:T(8,128)}), f32[128,2304]{1,0:T(8,128)}) %reduce-scatter.16.cloned.1.call-update) | async-done | bytes 1179664 | tf_op jit(solution)/shard_map/reduce_scatter | solution.py:216
  452.3 60.8 %all_to_all.20 = bf16[8,32,2304]{2,1,0:T(8,128)(2,1)} all-to-all(bf16[8,32,2304]{2,1,0:T(8,128)(2,1)S(1)} %bitcast.321), channel_id=1, replica_groups=mesh['wide'=8,'narrow'=4] {'wide'}, dimensions={0} | all-to-all | bytes 2359296 | tf_op jit(solution)/shard_map/all_to_all | solution.py:153
  517.2 64.1 %all-gather.30.cloned.1.call-done = bf16[2304,1440]{1,0:T(8,128)(2,1)} async-done(((bf16[288,1440]{1,0:T(8,128)(2,1)}), bf16[2304,1440]{1,0:T(8,128)(2,1)}) %all-gather.30.cloned.1.call-update) | async-done | bytes 6635536 | tf_op jit(solution)/shard_map/all_gather | solution.py:171
  581.4 24.3 %all-gather.26.cloned.1.call-done = bf16[512,2304]{1,0:T(8,128)(2,1)} async-done(((bf16[128,2304]{1,0:T(8,128)(2,1)}), bf16[512,2304]{1,0:T(8,128)(2,1)}) %all-gather.26.cloned.1.call-update) | async-done | bytes 2359312 | tf_op jit(solution)/shard_map/all_gather | solution.py:225
  614.8 101.9 %all-gather.28.cloned.1.call-done = bf16[2304,1440]{1,0:T(8,128)(2,1)} async-done(((bf16[288,1440]{1,0:T(8,128)(2,1)}), bf16[2304,1440]{1,0:T(8,128)(2,1)}) %all-gather.28.cloned.1.call-update) | async-done | bytes 6635536 | tf_op jit(solution)/shard_map/all_gather | solution.py:170
  741.0 111.0 %all-gather.32.cloned.1.call-done = bf16[1440,2304]{0,1:T(8,128)(2,1)} async-done(((bf16[1440,288]{0,1:T(8,128)(2,1)}), bf16[1440,2304]{0,1:T(8,128)(2,1)}) %all-gather.32.cloned.1.call-update) | async-done | bytes 6635536 | tf_op jit(solution)/shard_map/all_gather | solution.py:172
  878.0 44.9 %reduce-scatter.24.cloned.1.call-done = f32[128,2304]{1,0:T(8,128)} async-done(((f32[512,2304]{1,0:T(8,128)}), f32[128,2304]{1,0:T(8,128)}) %reduce-scatter.24.cloned.1.call-update) | async-done | bytes 1179664 | tf_op jit(solution)/shard_map/reduce_scatter | solution.py:246
  1024.3 27.9 %reduce-scatter.28.cloned.1.call-done = f32[128,2304]{1,0:T(8,128)} async-done(((f32[512,2304]{1,0:T(8,128)}), f32[128,2304]{1,0:T(8,128)}) %reduce-scatter.28.cloned.1.call-update) | async-done | bytes 1179664 | tf_op jit(solution)/shard_map/reduce_scatter | solution.py:246
  1055.0 32.7 %reduce-scatter.18.cloned.1.call-done = bf16[128,2304]{1,0:T(8,128)(2,1)} async-done(((bf16[512,2304]{1,0:T(8,128)(2,1)}), bf16[128,2304]{1,0:T(8,128)(2,1)}) %reduce-scatter.18.cloned.1.call-update) | async-done | bytes 589840 | tf_op jit(solution)/shard_map/reduce_scatter | solution.py:230
  1087.8 35.8 %reduce-scatter.22.cloned.1.call-done = bf16[128,2304]{1,0:T(8,128)(2,1)} async-done(((bf16[512,2304]{1,0:T(8,128)(2,1)}), bf16[128,2304]{1,0:T(8,128)(2,1)}) %reduce-scatter.22.cloned.1.call-update) | async-done | bytes 589840 | tf_op jit(solution)/shard_map/reduce_scatter | solution.py:230
  1284.1 25.0 %collective-permute-done.6 = bf16[512,576]{0,1:T(8,128)(2,1)S(1)} collective-permute-done((bf16[512,576]{0,1:T(8,128)(2,1)S(1)}, bf16[512,576]{0,1:T(8,128)(2,1)S(1)}, u32[]{:S(2)}, u32[]{:S(2)}) %collective-permute-start.6) | collective-permute-done | bytes 589856 | tf_op jit(solution)/shard_map/ppermute | solution.py:22
  1456.6 56.9 %reduce-scatter.44.cloned.1.call-done = bf16[1440,288]{0,1:T(8,128)(2,1)} async-done(((bf16[1440,2304]{0,1:T(8,128)(2,1)}), bf16[1440,288]{0,1:T(8,128)(2,1)}) %reduce-scatter.44.cloned.1.call-update) | async-done | bytes 829456 | tf_op jit(solution)/shard_map/reduce_scatter | solution.py:339
  1516.1 129.2 %reduce-scatter.42.cloned.1.call-done = bf16[288,1440]{1,0:T(8,128)(2,1)} async-done(((bf16[2304,1440]{1,0:T(8,128)(2,1)}), bf16[288,1440]{1,0:T(8,128)(2,1)}) %reduce-scatter.42.cloned.1.call-update) | async-done | bytes 829456 | tf_op jit(solution)/shard_map/reduce_scatter | solution.py:336
  1647.9 129.1 %reduce-scatter.40.cloned.1.call-done = bf16[288,1440]{1,0:T(8,128)(2,1)} async-done(((bf16[2304,1440]{1,0:T(8,128)(2,1)}), bf16[288,1440]{1,0:T(8,128)(2,1)}) %reduce-scatter.40.cloned.1.call-update) | async-done | bytes 829456 | tf_op jit(solution)/shard_map/reduce_scatter | solution.py:333
  1779.5 72.9 %reduce-scatter.38.cloned.1.call-done = bf16[576,288]{0,1:T(8,128)(2,1)} async-done(((bf16[576,2304]{0,1:T(8,128)(2,1)}), bf16[576,288]{0,1:T(8,128)(2,1)}) %reduce-scatter.38.cloned.1.call-update) | async-done | bytes 331792 | tf_op jit(solution)/shard_map/reduce_scatter | solution.py:330
  1854.3 41.5 %all-reduce = (f32[2304]{0:T(1024)}, f32[2304]{0:T(1024)}) all-reduce(f32[2304]{0:T(1024)S(1)} %add.499, f32[2304]{0:T(1024)S(1)} %add.500), channel_id=1, replica_groups=mesh['wide'=8,'narrow'=4] {'wide','narrow'}, use_global_device_ids=true, to_apply=%region_35.36 | all-reduce | flops 4608 | bytes 36864 | tf_op jit(solution)/shard_map/psum | solution.py:343
  1895.8 33.2 %reduce-scatter.36.cloned.1.call-done = bf16[288,576]{1,0:T(8,128)(2,1)} async-done(((bf16[2304,576]{1,0:T(8,128)(2,1)}), bf16[288,576]{1,0:T(8,128)(2,1)}) %reduce-scatter.36.cloned.1.call-update) | async-done | bytes 331792 | tf_op jit(solution)/shard_map/reduce_scatter | solution.py:327
  1931.0 73.6 %reduce-scatter.34.cloned.1.call-done = bf16[288,576]{1,0:T(8,128)(2,1)} async-done(((bf16[2304,576]{1,0:T(8,128)(2,1)}), bf16[288,576]{1,0:T(8,128)(2,1)}) %reduce-scatter.34.cloned.1.call-update) | async-done | bytes 331792 | tf_op jit(solution)/shard_map/reduce_scatter | solution.py:324
  2006.5 73.2 %reduce-scatter.32.cloned.1.call-done = bf16[288,576]{1,0:T(8,128)(2,1)} async-done(((bf16[2304,576]{1,0:T(8,128)(2,1)}), bf16[288,576]{1,0:T(8,128)(2,1)}) %reduce-scatter.32.cloned.1.call-update) | async-done | bytes 331792 | tf_op jit(solution)/shard_map/reduce_scatter | solution.py:321
  (536 shorter events, 691.3 us)
Async XLA Ops:
  61.8 111.3 %all-gather.22.cloned.1.call-start = ((), (), s32[]{:S(2)}) async-start(), calls=%async_computation.22 | async-start | bytes 3317760 | tf_op jit(solution)/shard_map/all_gather | solution.py:167
  62.5 178.3 %all-gather.18.cloned.1.call-start = ((), (), s32[]{:S(2)}) async-start(), calls=%async_computation.20 | async-start | bytes 3317760 | tf_op jit(solution)/shard_map/all_gather | solution.py:168
  63.1 243.6 %all-gather.24.cloned.1.call-start = ((), (), s32[]{:S(2)}) async-start(), calls=%async_computation.23 | async-start | bytes 3317760 | tf_op jit(solution)/shard_map/all_gather | solution.py:169
  63.7 267.7 %all-gather.16.cloned.1.call-start = ((), (), s32[]{:S(2)}) async-start(), calls=%async_computation.19 | async-start | bytes 2949120 | tf_op jit(solution)/shard_map/all_gather | solution.py:187
  186.4 210.6 %reduce-scatter.20.cloned.1.call-start = ((), (), s32[]{:S(2)}) async-start(), calls=%async_computation.31 | async-start | bytes 5898240 | tf_op jit(solution)/shard_map/reduce_scatter | solution.py:216
  312.7 132.5 %reduce-scatter.16.cloned.1.call-start = ((), (), s32[]{:S(2)}) async-start(), calls=%async_computation.24 | async-start | bytes 5898240 | tf_op jit(solution)/shard_map/reduce_scatter | solution.py:216
  396.2 185.1 %all-gather.30.cloned.1.call-start = ((), (), s32[]{:S(2)}) async-start(), calls=%async_computation.27 | async-start | bytes 7962624 | tf_op jit(solution)/shard_map/all_gather | solution.py:171
  397.0 208.7 %all-gather.26.cloned.1.call-start = ((), (), s32[]{:S(2)}) async-start(), calls=%async_computation.25 | async-start | bytes 2949120 | tf_op jit(solution)/shard_map/all_gather | solution.py:225
  449.5 267.2 %all-gather.28.cloned.1.call-start = ((), (), s32[]{:S(2)}) async-start(), calls=%async_computation.26 | async-start | bytes 7962624 | tf_op jit(solution)/shard_map/all_gather | solution.py:170
  450.3 290.7 %all-gather.38.cloned.1.call-start = ((), (), s32[]{:S(2)}) async-start(), calls=%async_computation.34 | async-start | bytes 2949120 | tf_op jit(solution)/shard_map/all_gather | solution.py:188
  516.3 335.7 %all-gather.32.cloned.1.call-start = ((), (), s32[]{:S(2)}) async-start(), calls=%async_computation.28 | async-start | bytes 7962624 | tf_op jit(solution)/shard_map/all_gather | solution.py:172
  517.0 405.9 %reduce-scatter.24.cloned.1.call-start = ((), (), s32[]{:S(2)}) async-start(), calls=%async_computation.35 | async-start | bytes 5898240 | tf_op jit(solution)/shard_map/reduce_scatter | solution.py:246
  926.6 125.6 %reduce-scatter.28.cloned.1.call-start = ((), (), s32[]{:S(2)}) async-start(), calls=%async_computation.39 | async-start | bytes 5898240 | tf_op jit(solution)/shard_map/reduce_scatter | solution.py:246
  1022.9 130.1 %all-gather.40.cloned.1.call-start = ((), (), s32[]{:S(2)}) async-start(), calls=%async_computation.36 | async-start | bytes 2949120 | tf_op jit(solution)/shard_map/all_gather | solution.py:257
  1131.0 290.8 %reduce-scatter.26.cloned.1.call-start = ((), (), s32[]{:S(2)}) async-start(), calls=%async_computation.37 | async-start | bytes 2949120 | tf_op jit(solution)/shard_map/reduce_scatter | solution.py:300
  1260.1 161.7 %reduce-scatter.30.cloned.1.call-start = ((), (), s32[]{:S(2)}) async-start(), calls=%async_computation.41 | async-start | bytes 2949120 | tf_op jit(solution)/shard_map/reduce_scatter | solution.py:300
  1320.7 192.8 %reduce-scatter.44.cloned.1.call-start = ((), (), s32[]{:S(2)}) async-start(), calls=%async_computation.48 | async-start | bytes 7962624 | tf_op jit(solution)/shard_map/reduce_scatter | solution.py:339
  1340.6 304.6 %reduce-scatter.42.cloned.1.call-start = ((), (), s32[]{:S(2)}) async-start(), calls=%async_computation.47 | async-start | bytes 7962624 | tf_op jit(solution)/shard_map/reduce_scatter | solution.py:336
  1360.0 417.0 %reduce-scatter.40.cloned.1.call-start = ((), (), s32[]{:S(2)}) async-start(), calls=%async_computation.46 | async-start | bytes 7962624 | tf_op jit(solution)/shard_map/reduce_scatter | solution.py:333
  1378.2 474.2 %reduce-scatter.38.cloned.1.call-start = ((), (), s32[]{:S(2)}) async-start(), calls=%async_computation.45 | async-start | bytes 3317760 | tf_op jit(solution)/shard_map/reduce_scatter | solution.py:330
  1386.0 543.0 %reduce-scatter.36.cloned.1.call-start = ((), (), s32[]{:S(2)}) async-start(), calls=%async_computation.44 | async-start | bytes 3317760 | tf_op jit(solution)/shard_map/reduce_scatter | solution.py:327
  1393.6 611.0 %reduce-scatter.34.cloned.1.call-start = ((), (), s32[]{:S(2)}) async-start(), calls=%async_computation.43 | async-start | bytes 3317760 | tf_op jit(solution)/shard_map/reduce_scatter | solution.py:324
  1402.3 677.4 %reduce-scatter.32.cloned.1.call-start = ((), (), s32[]{:S(2)}) async-start(), calls=%async_computation.42 | async-start | bytes 3317760 | tf_op jit(solution)/shard_map/reduce_scatter | solution.py:321
  1451.3 630.4 %all-to-all-start.3 = ((bf16[8,32,2304]{2,1,0:T(8,128)(2,1)}), bf16[8,32,2304]{2,1,0:T(8,128)(2,1)S(1)}, u32[]{:S(2)}, u32[]{:S(2)}) async-start(bf16[8,32,2304]{2,1,0:T(8,128)(2,1)} %bitcast.68), calls=%async_computation.11 | async-start | bytes 2359296 | tf_op jit(solution)/shard_map/all_to_all | solution.py:354
  (151 other events, 3541.0 us)
Sparse Core Ops, SparseCore 0:
  10.2 77.3 all-gather.19
  114.6 58.3 all-gather.21
  175.1 65.6 all-gather.17
  242.8 63.7 all-gather.23
  333.9 47.8 reduce-scatter.19
  396.4 48.7 reduce-scatter.15
  447.4 133.9 all-gather.29
  607.8 108.7 all-gather.27
  743.1 108.7 all-gather.31
  876.9 45.9 reduce-scatter.23
  926.2 24.0 all-gather.35
  1004.4 47.8 reduce-scatter.27
  1054.7 33.0 reduce-scatter.17
  1090.5 33.0 reduce-scatter.21
  1155.1 24.0 all-gather.43
  1260.2 37.0 reduce-scatter.25
  1320.8 34.5 reduce-scatter.29
  1359.0 154.4 reduce-scatter.43
  1517.6 127.6 reduce-scatter.41
  1648.8 128.0 reduce-scatter.39
  1780.7 71.5 reduce-scatter.37
  1856.0 73.0 reduce-scatter.35
  1933.0 71.5 reduce-scatter.33
  2008.0 71.6 reduce-scatter.31
  (6 shorter events, 137.7 us)
where the time goes:
time: 2100 us; the launch traced here: 2090 us
  waiting for transfers between devices  1430 us (68%)
  matrix products  338 us (16%)
  other arithmetic  117 us (6%)
  blocking collectives  102 us (5%)
  local copies, waits for them, and re-layouts  42.6 us (2%)
  starting transfers between devices  39.2 us (2%)
    reduce_scatter x1, waiting for transfers between devices, body(): lax.psum_scatter(totals[5].astype(jnp.bfloat16), 'wide', scatter_dimensio...  129 us
    reduce_scatter x1, waiting for transfers between devices, body(): lax.psum_scatter(totals[4].astype(jnp.bfloat16), 'wide', scatter_dimensio...  129 us
    all_gather x1, waiting for transfers between devices, body(): lax.all_gather(w_down, 'wide', axis=1, tiled=True)  111 us
    all_gather x1, waiting for transfers between devices, body(): lax.all_gather(w_gate, 'wide', axis=0, tiled=True)  102 us
    dot_general x14, matrix products, contract_rows(): lax.dot_general(left, right, (((0,), (0,)), ((), ())), preferred_element_...  80.8 us
    dot_general x14, matrix products, times_transpose(): lax.dot_general(left, right, (((1,), (1,)), ((), ())), preferred_element_...  76.3 us
    reduce_scatter x1, waiting for transfers between devices, body(): lax.psum_scatter(totals[1].astype(jnp.bfloat16), 'wide', scatter_dimensio...  73.6 us
    reduce_scatter x1, waiting for transfers between devices, body(): lax.psum_scatter(totals[0].astype(jnp.bfloat16), 'wide', scatter_dimensio...  73.2 us
  transfers between devices with their start and end apart: 41, of which 32 were waited for; matrix products, arithmetic and copies ran while one was open for 19% of the time, Pallas kernels for 0%

commit v1 on v0

v1 whole, which is shorter than its diff:
```python
import math

import jax
import jax.numpy as jnp
from jax import lax
from jax.experimental import pallas as pl
from jax.experimental.pallas import tpu as pltpu
from jax.sharding import PartitionSpec as P

HEAD_DIM = 64
MB = 2
BLK = 8
UNIT = 64


BRANCH = 1.4 / math.sqrt(40.0)
EPSILON = 1e-05
NEGATIVE = -1e30
RING_MAX = 8


def ring_rank(place, count):
    place = lax.rem(place + 2 * count, count)
    return jnp.where(place < count // 2, 2 * place, 2 * count - 1 - 2 * place)


def ring_place(rank, count):
    return jnp.where(rank % 2 == 0, rank // 2, count - 1 - rank // 2)


def ring_send(block, count, direction):
    order = list(range(0, count, 2)) + list(range(count - 1, 0, -2))
    route = [(order[i], order[(i + direction) % count]) for i in range(count)]
    return lax.ppermute(block, "wide", route)


def after(value, *others):
    return lax.optimization_barrier((value,) + others)[0]


def ring_gather(block, count, gate=None):
    rank = lax.axis_index("wide")
    place = ring_place(rank, count)
    rows = block.shape[0]
    half = rows // 16 * 8
    found = [(rank, 0, block)]
    if gate is not None:
        block = after(block, *gate)
    up = down = block
    for step in range(1, count // 2):
        up = ring_send(up, count, 1)
        down = ring_send(down, count, -1)
        found.append((ring_rank(place - step, count), 0, up))
        found.append((ring_rank(place + step, count), 0, down))
    last = (up, down)
    far = ring_rank(place + count // 2, count)
    found.append((far, 0, ring_send(up[:half], count, 1)))
    found.append((far, half, ring_send(down[half:], count, -1)))
    return found, last


def assemble(found, count, rows, first=0):
    width = found[0][2].shape[1]
    full = jnp.zeros((count * rows, width), found[0][2].dtype)
    for rank, start, piece in found:
        low = max(first - start, 0)
        high = min(first + rows - start, piece.shape[0])
        if low < high:
            full = lax.dynamic_update_slice(
                full, piece[low:high], (rank * rows + start + low - first, 0)
            )
    return full


def gather_weights(groups, count):
    if count > RING_MAX:
        return [lax.all_gather(one, "wide", axis=0, tiled=True) for group in groups for one in group]
    fulls = []
    gate = None
    for group in groups:
        rows = group[0].shape[0]
        block = jnp.concatenate(group, axis=0) if len(group) > 1 else group[0]
        found, gate = ring_gather(block, count, gate)
        fulls += [assemble(found, count, rows, index * rows) for index in range(len(group))]
    return fulls


def ring_scatter(fulls, count):
    if count > RING_MAX:
        return [
            lax.psum_scatter(full, "wide", scatter_dimension=0, tiled=True).astype(jnp.float32)
            for full in fulls
        ]
    rank = lax.axis_index("wide")
    place = ring_place(rank, count)
    rows = fulls[0].shape[0] // count
    total = rows * len(fulls)
    half = total // 16 * 8

    def local(where):
        owner = ring_rank(where, count)
        return jnp.concatenate(
            [lax.dynamic_slice_in_dim(full, owner * rows, rows, axis=0) for full in fulls], axis=0
        ).astype(jnp.float32)

    far = local(place + count // 2).astype(jnp.bfloat16)
    up = ring_send(far[:half], count, 1)
    down = ring_send(far[half:], count, -1)
    for step in range(2, count // 2 + 1):
        mine_up = local(place + count // 2 - step + 1)
        mine_down = local(place - count // 2 + step - 1)
        if step == 2:
            sum_up = jnp.concatenate([up.astype(jnp.float32) + mine_up[:half], mine_up[half:]], axis=0)
            sum_down = jnp.concatenate(
                [mine_down[:half], down.astype(jnp.float32) + mine_down[half:]], axis=0
            )
        else:
            sum_up = up.astype(jnp.float32) + mine_up
            sum_down = down.astype(jnp.float32) + mine_down
        up = ring_send(sum_up.astype(jnp.bfloat16), count, 1)
        down = ring_send(sum_down.astype(jnp.bfloat16), count, -1)
    done = local(place) + up.astype(jnp.float32) + down.astype(jnp.float32)
    return [done[i * rows : (i + 1) * rows] for i in range(len(fulls))]


def swap_chip(block):
    return lax.ppermute(block, "narrow", [(0, 2), (1, 3), (2, 0), (3, 1)])


def swap_core(block):
    return lax.ppermute(block, "narrow", [(0, 1), (1, 0), (2, 3), (3, 2)])


def narrow_gather(block):
    lane = lax.axis_index("narrow")
    chip = swap_chip(block)
    core = swap_core(block)
    both = swap_core(chip)
    full = jnp.zeros((4,) + block.shape, block.dtype)
    for piece, owner in ((block, lane), (core, lane ^ 1), (chip, lane ^ 2), (both, lane ^ 3)):
        full = lax.dynamic_update_slice(full, piece[None], (owner,) + (0,) * block.ndim)
    return full


def narrow_scatter(parts):
    lane = lax.axis_index("narrow")

    def pick(owner):
        return lax.dynamic_index_in_dim(parts, owner, 0, keepdims=False)

    far = swap_core(pick(lane ^ 3))
    near = swap_core(pick(lane ^ 1))
    across = swap_chip(
        (pick(lane ^ 2).astype(jnp.float32) + far.astype(jnp.float32)).astype(jnp.bfloat16)
    )
    return pick(lane).astype(jnp.float32) + near.astype(jnp.float32) + across.astype(jnp.float32)


def angles(position):
    lane = jnp.arange(2 * HEAD_DIM, dtype=jnp.int32) % HEAD_DIM
    counter = (lane % (HEAD_DIM // 2)).astype(jnp.float32)
    frequency = jnp.exp(counter * (-2.0 * math.log(10000.0) / HEAD_DIM))
    phase_angle = position.astype(jnp.float32)[:, None] * frequency[None, :]
    sign = jnp.where(lane < HEAD_DIM // 2, -1.0, 1.0)
    return jnp.cos(phase_angle), jnp.sin(phase_angle) * sign[None, :]


def turn(field_in, cosine, sine, direction):
    rows, width = field_in.shape
    parts = []
    for low in range(0, width, 2 * HEAD_DIM):
        size = min(2 * HEAD_DIM, width - low)
        piece = field_in[:, low : low + size]
        if size < 2 * HEAD_DIM:
            piece = jnp.concatenate([piece, piece], axis=1)
        lane = lax.broadcasted_iota(jnp.int32, piece.shape, 1)
        swapped = jnp.where(
            lane % HEAD_DIM < HEAD_DIM // 2,
            pltpu.roll(piece, 2 * HEAD_DIM - HEAD_DIM // 2, 1),
            pltpu.roll(piece, HEAD_DIM // 2, 1),
        )
        parts.append((piece * cosine + direction * (swapped * sine))[:, :size])
    return jnp.concatenate(parts, axis=1)


def contract_rows(left, right):
    return lax.dot_general(
        left, right, (((0,), (0,)), ((), ())), preferred_element_type=jnp.float32
    ).astype(jnp.bfloat16)


def times(left, right):
    return jnp.dot(left, right, preferred_element_type=jnp.float32)


def times_transpose(left, right):
    return lax.dot_general(
        left, right, (((1,), (1,)), ((), ())), preferred_element_type=jnp.float32
    )


def norm_rate(resid):
    return lax.rsqrt(jnp.mean(resid * resid, axis=1, keepdims=True) + EPSILON)


def norm_backward(grad_in, resid, rate, gain):
    scaled_grad = grad_in * gain[None, :]
    return rate * scaled_grad - resid * rate**3 * jnp.mean(
        scaled_grad * resid, axis=1, keepdims=True
    )


def invert_order(placing):
    counter = jnp.arange(placing.shape[0], dtype=jnp.int32)
    return jnp.sum(jnp.where(placing[None, :] == counter[:, None], counter[None, :], 0), axis=1)


def deal_routes(deal, my_rank, my_lane, rank_count, lane_count, block_count):
    per_pair = block_count // rank_count
    base_block = (my_rank * lane_count + my_lane) * block_count
    counter = jnp.arange(block_count, dtype=jnp.int32)
    every_block = jnp.arange(deal.shape[0], dtype=jnp.int32)
    owned = base_block + counter
    target = jnp.sum(jnp.where(deal[None, :] == owned[:, None], every_block[None, :], 0), axis=1)
    target_rank = target // (lane_count * block_count)
    target_slot = target % block_count
    earlier = (target_rank[None, :] == target_rank[:, None]) & (
        target_slot[None, :] < target_slot[:, None]
    )
    send_place = target_rank * per_pair + jnp.sum(earlier.astype(jnp.int32), axis=1)
    mine = lax.dynamic_slice_in_dim(deal, base_block, block_count)
    source_rank = mine // (lane_count * block_count)
    before = (source_rank[None, :] == source_rank[:, None]) & (counter[None, :] < counter[:, None])
    recv_place = source_rank * per_pair + jnp.sum(before.astype(jnp.int32), axis=1)
    return (send_place, recv_place)


def stream_layout(length_row, my_rank, slot_rows):
    extent = (length_row + UNIT - 1) // UNIT * UNIT
    begin = jnp.cumsum(extent) - extent
    places = my_rank * slot_rows - slot_rows + jnp.arange(2 * slot_rows, dtype=jnp.int32)
    ending = begin + length_row
    inside = (places[:, None] >= begin[None, :]) & (places[:, None] < ending[None, :])
    number = jnp.arange(length_row.shape[0], dtype=jnp.int32) + 1
    segment = jnp.sum(jnp.where(inside, number[None, :], 0), axis=1) - 1
    position = places - jnp.sum(jnp.where(inside, begin[None, :], 0), axis=1)
    return (segment, position)


VMEM_LIMIT = 60 * 1024 * 1024


def dot_nn(left, right):
    return jnp.dot(left, right, preferred_element_type=jnp.float32)


def dot_nt(left, right):
    return times_transpose(left, right)


def dot_tn(left, right):
    return lax.dot_general(
        left, right, (((0,), (0,)), ((), ())), preferred_element_type=jnp.float32
    )


def project_kernel(rows_ref, weight_ref, cos_ref, sin_ref, q_ref, k_ref, v_ref):
    width = q_ref.shape[1]
    z = dot_nn(rows_ref[...], weight_ref[...])
    turned = turn(z[:, : 2 * width], cos_ref[...], sin_ref[...], 1.0).astype(jnp.bfloat16)
    q_ref[...] = turned[:, :width]
    k_ref[...] = turned[:, width:]
    v_ref[...] = z[:, 2 * width :].astype(jnp.bfloat16)


def project(rows, weight, cosine, sine):
    count, depth = rows.shape
    width = weight.shape[1] // 3
    block = 256
    out = jax.ShapeDtypeStruct((count, width), jnp.bfloat16)
    row_spec = pl.BlockSpec((block, width), lambda i: (i, 0))
    angle_spec = pl.BlockSpec((block, 2 * HEAD_DIM), lambda i: (i, 0))
    return pl.pallas_call(
        project_kernel,
        out_shape=(out, out, out),
        grid=(count // block,),
        in_specs=[
            pl.BlockSpec((block, depth), lambda i: (i, 0)),
            pl.BlockSpec(weight.shape, lambda i: (0, 0), pipeline_mode=pl.Buffered(1)),
            angle_spec,
            angle_spec,
        ],
        out_specs=(row_spec, row_spec, row_spec),
        compiler_params=pltpu.CompilerParams(vmem_limit_bytes=VMEM_LIMIT),
        cost_estimate=pl.CostEstimate(
            flops=2 * count * depth * 3 * width,
            bytes_accessed=2 * (count * depth + 3 * depth * width + 3 * count * width),
            transcendentals=0,
        ),
        name="project",
    )(rows, weight, cosine, sine)


def fill_bias(seg_col_ref, seg_row_ref, bias_own, bias_prev):
    slot = bias_own.shape[0]
    query = seg_row_ref[...]
    key = lax.broadcasted_iota(jnp.int32, (slot, slot), 0)
    place = lax.broadcasted_iota(jnp.int32, (slot, slot), 1)
    own = seg_col_ref[slot:, :]
    allowed = (own == query) & (query >= 0) & (key <= place) | (key == place)
    bias_own[...] = jnp.where(allowed, 0.0, NEGATIVE)
    bias_prev[...] = jnp.where((seg_col_ref[:slot, :] == query) & (query >= 0), 0.0, NEGATIVE)


def over_pairs(width, body):
    pairs = width // (2 * HEAD_DIM)

    def step(index, carry):
        body(pl.multiple_of(index * 2 * HEAD_DIM, 2 * HEAD_DIM), index * 2, 2)
        return carry

    lax.fori_loop(0, pairs, step, 0)
    if width % (2 * HEAD_DIM):
        body(pairs * 2 * HEAD_DIM, pairs * 2, 1)


def head_mask(lanes, head, value):
    lane = lax.broadcasted_iota(jnp.int32, (1, lanes), 1)
    return jnp.where(lane // HEAD_DIM == head, value, 0.0).astype(jnp.bfloat16)


def flat(ref, low, lanes):
    value = ref[:, :, pl.ds(low, lanes)]
    return value.reshape(value.shape[0] * value.shape[1], lanes)


def attend_kernel(
    flag_ref, seg_col_ref, seg_row_ref, q_ref, k_ref, v_ref, kp_ref, vp_ref,
    o_ref, lse_ref, bias_own, bias_prev,
):
    fill_bias(seg_col_ref, seg_row_ref, bias_own, bias_prev)
    slot = bias_own.shape[0]
    part = slot // 2

    def pair(with_prev, low, head, heads):
        lanes = heads * HEAD_DIM
        q, k, v = (flat(ref, low, lanes) for ref in (q_ref, k_ref, v_ref))
        if with_prev:
            kp, vp = kp_ref[:, pl.ds(low, lanes)], vp_ref[:, pl.ds(low, lanes)]
        for half in range(2):
            first, keys = half * part, (half + 1) * part
            mixed = []
            for one in range(heads):
                qm = q[first : first + part] * head_mask(lanes, one, 1.0 / math.sqrt(HEAD_DIM))
                s = dot_nt(k[:keys], qm) + bias_own[:keys, first : first + part]
                top = jnp.max(s, axis=0, keepdims=True)
                if with_prev:
                    sp = dot_nt(kp, qm) + bias_prev[:, first : first + part]
                    top = jnp.maximum(top, jnp.max(sp, axis=0, keepdims=True))
                p = jnp.exp(s - top)
                total = jnp.sum(p, axis=0, keepdims=True)
                o = dot_tn(v[:keys], p.astype(jnp.bfloat16))
                if with_prev:
                    pp = jnp.exp(sp - top)
                    total = total + jnp.sum(pp, axis=0, keepdims=True)
                    o = o + dot_tn(vp, pp.astype(jnp.bfloat16))
                mixed.append(o[one * HEAD_DIM : (one + 1) * HEAD_DIM] / total)
                lse_ref[pl.ds(head + one, 1), first : first + part] = top + jnp.log(total)
            o = jnp.concatenate(mixed, axis=0).T
            quarter = o_ref.shape[1]
            o_ref[first // quarter : (first + part) // quarter, :, pl.ds(low, lanes)] = (
                o.astype(jnp.bfloat16).reshape(part // quarter, quarter, lanes)
            )

    width = q_ref.shape[2]
    shared = flag_ref[pl.program_id(0)] == 1

    @pl.when(shared)
    def _():
        over_pairs(width, lambda *args: pair(True, *args))

    @pl.when(jnp.logical_not(shared))
    def _():
        over_pairs(width, lambda *args: pair(False, *args))


def attention_specs(lanes, rows, width):
    block = pl.BlockSpec((lanes, None, rows, width), lambda u, flag: (0, u, 0, 0))
    slot = lanes * rows
    key_before = pl.BlockSpec((None, None, slot, width), lambda u, flag: (u, 0, 0, 0))
    value_before = pl.BlockSpec((None, None, slot, width), lambda u, flag: (u, 1, 0, 0))
    col = pl.BlockSpec((None, 2 * slot, 1), lambda u, flag: (u, 0, 0))
    row = pl.BlockSpec((None, 1, slot), lambda u, flag: (u, 0, 0))
    lse = pl.BlockSpec((None, 16, slot), lambda u, flag: (u, 0, 0))
    return block, key_before, value_before, col, row, lse


def attend(flags, seg_col, seg_row, q, k, v, before):
    lanes, micros, rows, width = q.shape
    slot = lanes * rows
    block, key_before, value_before, col, row, lse = attention_specs(lanes, rows, width)
    heads = width // HEAD_DIM
    return pl.pallas_call(
        attend_kernel,
        out_shape=(
            jax.ShapeDtypeStruct(q.shape, jnp.bfloat16),
            jax.ShapeDtypeStruct((micros, 16, slot), jnp.float32),
        ),
        grid_spec=pltpu.PrefetchScalarGridSpec(
            num_scalar_prefetch=1,
            grid=(micros,),
            in_specs=[col, row, block, block, block, key_before, value_before],
            out_specs=(block, lse),
            scratch_shapes=[
                pltpu.VMEM((slot, slot), jnp.float32),
                pltpu.VMEM((slot, slot), jnp.float32),
            ],
        ),
        compiler_params=pltpu.CompilerParams(vmem_limit_bytes=VMEM_LIMIT),
        cost_estimate=pl.CostEstimate(
            flops=4 * micros * heads * slot * slot * 256,
            bytes_accessed=12 * micros * slot * width,
            transcendentals=micros * heads * slot * slot,
        ),
        name="attend",
    )(flags, seg_col, seg_row, q, k, v, before, before)


def attend_back_kernel(
    flag_ref, seg_col_ref, seg_row_ref, q_ref, k_ref, v_ref, kp_ref, vp_ref, o_ref, do_ref, lse_ref,
    dq_ref, dk_ref, dv_ref, back_ref, bias_own, bias_prev,
):
    fill_bias(seg_col_ref, seg_row_ref, bias_own, bias_prev)
    slot = bias_own.shape[0]
    part = slot // 2
    quarter = q_ref.shape[1]
    scale = 1.0 / math.sqrt(HEAD_DIM)

    def pair(with_prev, low, head, heads):
        lanes = heads * HEAD_DIM
        q, k, v, o, do = (flat(ref, low, lanes) for ref in (q_ref, k_ref, v_ref, o_ref, do_ref))
        if with_prev:
            kp, vp = kp_ref[:, pl.ds(low, lanes)], vp_ref[:, pl.ds(low, lanes)]
        product = (do.astype(jnp.float32) * o.astype(jnp.float32)).T
        dk = [0.0, 0.0]
        dv = [0.0, 0.0]
        dkp = dvp = 0.0
        for half in range(2):
            first, keys = half * part, (half + 1) * part
            turned = []
            for one in range(heads):
                span = slice(one * HEAD_DIM, (one + 1) * HEAD_DIM)
                delta = jnp.sum(product[span, first : first + part], axis=0, keepdims=True)
                lse = lse_ref[pl.ds(head + one, 1), first : first + part]
                qm = q[first : first + part] * head_mask(lanes, one, scale)
                dm = do[first : first + part] * head_mask(lanes, one, 1.0)
                p = jnp.exp(dot_nt(k[:keys], qm) + bias_own[:keys, first : first + part] - lse)
                ds = (p * (dot_nt(v[:keys], dm) - delta)).astype(jnp.bfloat16)
                new_dv = dot_nn(p.astype(jnp.bfloat16), dm)
                new_dk = dot_nn(ds, qm)
                for index in range(half + 1):
                    rows = slice(index * part, (index + 1) * part)
                    dv[index] = dv[index] + new_dv[rows]
                    dk[index] = dk[index] + new_dk[rows]
                dq = dot_tn(k[:keys], ds)
                if with_prev:
                    p = jnp.exp(dot_nt(kp, qm) + bias_prev[:, first : first + part] - lse)
                    ds = (p * (dot_nt(vp, dm) - delta)).astype(jnp.bfloat16)
                    dvp = dvp + dot_nn(p.astype(jnp.bfloat16), dm)
                    dkp = dkp + dot_nn(ds, qm)
                    dq = dq + dot_tn(kp, ds)
                turned.append(dq[span])
            dq = jnp.concatenate(turned, axis=0).T * scale
            dq_ref[first // quarter : (first + part) // quarter, :, pl.ds(low, lanes)] = dq.reshape(
                part // quarter, quarter, lanes
            )
        for index in range(2):
            span = slice(index * part // quarter, (index + 1) * part // quarter)
            shape = (part // quarter, quarter, lanes)
            dk_ref[span, :, pl.ds(low, lanes)] = dk[index].reshape(shape)
            dv_ref[span, :, pl.ds(low, lanes)] = dv[index].reshape(shape)
        if with_prev:
            back_ref[0, :, pl.ds(low, lanes)] = dkp.astype(jnp.bfloat16)
            back_ref[1, :, pl.ds(low, lanes)] = dvp.astype(jnp.bfloat16)

    width = q_ref.shape[2]
    shared = flag_ref[pl.program_id(0)] == 1

    @pl.when(shared)
    def _():
        over_pairs(width, lambda *args: pair(True, *args))

    @pl.when(jnp.logical_not(shared))
    def _():
        over_pairs(width, lambda *args: pair(False, *args))
        back_ref[...] = jnp.zeros_like(back_ref)


def attend_back(flags, seg_col, seg_row, q, k, v, before, o, do, lse_in):
    lanes, micros, rows, width = q.shape
    slot = lanes * rows
    block, key_before, value_before, col, row, lse = attention_specs(lanes, rows, width)
    both = pl.BlockSpec((None, 2, slot, width), lambda u, flag: (u, 0, 0, 0))
    wide = jax.ShapeDtypeStruct(q.shape, jnp.float32)
    heads = width // HEAD_DIM
    return pl.pallas_call(
        attend_back_kernel,
        out_shape=(
            wide,
            wide,
            wide,
            jax.ShapeDtypeStruct((micros, 2, slot, width), jnp.bfloat16),
        ),
        grid_spec=pltpu.PrefetchScalarGridSpec(
            num_scalar_prefetch=1,
            grid=(micros,),
            in_specs=[col, row, block, block, block, key_before, value_before, block, block, lse],
            out_specs=(block, block, block, both),
            scratch_shapes=[
                pltpu.VMEM((slot, slot), jnp.float32),
                pltpu.VMEM((slot, slot), jnp.float32),
            ],
        ),
        compiler_params=pltpu.CompilerParams(vmem_limit_bytes=VMEM_LIMIT),
        cost_estimate=pl.CostEstimate(
            flops=10 * micros * heads * slot * slot * 256,
            bytes_accessed=30 * micros * slot * width,
            transcendentals=micros * heads * slot * slot,
        ),
        name="attend_back",
    )(flags, seg_col, seg_row, q, k, v, before, before, o, do, lse_in)


def join_kernel(dq_ref, dk_ref, dv_ref, back_ref, cos_ref, sin_ref, out_ref):
    width = dq_ref.shape[1]
    cosine, sine = cos_ref[...], sin_ref[...]
    dk = dk_ref[...] + back_ref[0].astype(jnp.float32)
    dv = dv_ref[...] + back_ref[1].astype(jnp.float32)
    out_ref[...] = jnp.concatenate(
        [turn(dq_ref[...], cosine, sine, -1.0), turn(dk, cosine, sine, -1.0), dv], axis=1
    ).astype(jnp.bfloat16)


def join_grads(dq, dk, dv, back, cosine, sine):
    lanes, micros, rows, width = dq.shape
    block = pl.BlockSpec((None, None, rows, width), lambda j, u: (j, u, 0, 0))
    both = pl.BlockSpec((None, 2, rows, width), lambda j, u: (u, 0, j, 0))
    angle = pl.BlockSpec((None, None, rows, 2 * HEAD_DIM), lambda j, u: (j, u, 0, 0))
    return pl.pallas_call(
        join_kernel,
        out_shape=jax.ShapeDtypeStruct((lanes, micros, rows, 3 * width), jnp.bfloat16),
        grid=(lanes, micros),
        in_specs=[block, block, block, both, angle, angle],
        out_specs=pl.BlockSpec((None, None, rows, 3 * width), lambda j, u: (j, u, 0, 0)),
        compiler_params=pltpu.CompilerParams(vmem_limit_bytes=VMEM_LIMIT),
        cost_estimate=pl.CostEstimate(
            flops=8 * lanes * micros * rows * width,
            bytes_accessed=22 * lanes * micros * rows * width,
            transcendentals=0,
        ),
        name="join_grads",
    )(dq, dk, dv, back, cosine, sine)


def pair_route(micro, count, direction):
    route = [(low, low + 1) for low in range(micro, count - 1, 2)]
    return [(b, a) for a, b in route] if direction < 0 else route


def body(
    tokens,
    norm_attn,
    norm_ffn,
    w_query,
    w_key,
    w_value,
    w_out,
    w_gate,
    w_up,
    w_down,
    cotangent,
    lengths,
    deal,
):
    rank_count = lax.axis_size("wide")
    lane_count = lax.axis_size("narrow")
    my_rank = lax.axis_index("wide")
    my_lane = lax.axis_index("narrow")
    row_count = tokens.shape[0]
    width = tokens.shape[1]
    block_count = row_count // BLK
    per_pair = block_count // rank_count
    micro_rows = row_count // MB
    slot_rows = lane_count * micro_rows
    all_rows = lane_count * row_count
    features = w_query.shape[1]
    shard = w_query.shape[0]
    send_place, recv_place = deal_routes(
        deal, my_rank, my_lane, rank_count, lane_count, block_count
    )
    send_order = invert_order(send_place)
    back_order = invert_order(recv_place)

    def exchange(flat_rows, order, placing):
        packed = flat_rows.reshape(block_count, BLK, width)[order].reshape(
            rank_count, per_pair * BLK, width
        )
        got = lax.all_to_all(packed, "wide", split_axis=0, concat_axis=0, tiled=True)
        return got.reshape(block_count, BLK, width)[placing].reshape(row_count, width)

    dealt_x = exchange(tokens, send_order, recv_place)
    dealt_cot = exchange(cotangent, send_order, recv_place)

    wqkv, wo, wg, wu, wd = gather_weights(
        [
            [jnp.concatenate([w_query, w_key, w_value], axis=1)],
            [w_out.T],
            [w_gate, w_up],
            [w_down.T],
        ],
        rank_count,
    )

    gain_attn = norm_attn.astype(jnp.float32)
    gain_ffn = norm_ffn.astype(jnp.float32)
    layouts = [stream_layout(lengths[micro], my_rank, slot_rows) for micro in range(MB)]
    segments = [one[0] for one in layouts]
    own_segment = jnp.concatenate(
        [
            lax.dynamic_slice_in_dim(segment, slot_rows + my_lane * micro_rows, micro_rows)
            for segment in segments
        ]
    )
    validity = (own_segment >= 0).astype(jnp.float32)[:, None]
    by_lane = (lane_count, MB, micro_rows)
    row_position = jnp.stack(
        [one[1][slot_rows:].reshape(lane_count, micro_rows) for one in layouts], axis=1
    ).reshape(all_rows)
    cosine, sine = angles(row_position)
    seg_col = jnp.stack(segments)[:, :, None]
    seg_row = jnp.stack(segments)[:, None, slot_rows:]
    parity = jnp.arange(MB, dtype=jnp.int32)
    flags = ((my_rank > 0) & ((my_rank + parity) % 2 == 1)).astype(jnp.int32)

    resid = dealt_x.astype(jnp.float32) * validity
    rate_attn = norm_rate(resid)
    attn_in = (resid * rate_attn * gain_attn[None, :]).astype(jnp.bfloat16)
    attn_rows = narrow_gather(attn_in).reshape(all_rows, width)
    cot_all = narrow_gather(dealt_cot).reshape(all_rows, width)
    queries, keys, values = (
        one.reshape(by_lane + (features,)) for one in project(attn_rows, wqkv, cosine, sine)
    )
    before = jnp.stack(
        [
            lax.ppermute(
                jnp.stack([keys[:, micro], values[:, micro]]).reshape(2, slot_rows, features),
                "wide",
                pair_route(micro, rank_count, 1),
            )
            for micro in range(MB)
        ]
    )
    mixed, log_total = attend(flags, seg_col, seg_row, queries, keys, values, before)
    attn_out = mixed.reshape(all_rows, features)
    branch_attn = narrow_scatter(
        times_transpose(attn_out, wo).astype(jnp.bfloat16).reshape(lane_count, row_count, width)
    )
    middle = resid + BRANCH * branch_attn
    rate_ffn = norm_rate(middle)
    ffn_in = (middle * rate_ffn * gain_ffn[None, :]).astype(jnp.bfloat16)
    ffn_rows = narrow_gather(ffn_in).reshape(all_rows, width)
    gate = times(ffn_rows, wg)
    upward = times(ffn_rows, wu)
    sigma = jax.nn.sigmoid(gate)
    hidden = (gate * sigma * upward).astype(jnp.bfloat16)
    cot_branch = (BRANCH * cot_all.astype(jnp.float32)).astype(jnp.bfloat16)
    grad_wd = contract_rows(cot_branch, hidden)
    (sum_wd,) = ring_scatter([grad_wd], rank_count)
    grad_hidden = times(cot_branch, wd)
    grad_gate = (grad_hidden * upward * sigma * (1.0 + gate * (1.0 - sigma))).astype(jnp.bfloat16)
    grad_upward = (grad_hidden * gate * sigma).astype(jnp.bfloat16)
    grad_ffn_in = narrow_scatter(
        (times_transpose(grad_gate, wg) + times_transpose(grad_upward, wu))
        .astype(jnp.bfloat16)
        .reshape(lane_count, row_count, width)
    )
    grad_wg = contract_rows(ffn_rows, grad_gate)
    grad_wu = contract_rows(ffn_rows, grad_upward)
    sum_wg, sum_wu = ring_scatter([grad_wg, grad_wu], rank_count)
    branch_ffn = narrow_scatter(
        times_transpose(hidden, wd).astype(jnp.bfloat16).reshape(lane_count, row_count, width)
    )
    output = exchange(
        (middle + BRANCH * branch_ffn).astype(jnp.bfloat16), back_order, send_place
    )
    gain_total_ffn = jnp.sum(grad_ffn_in * middle * rate_ffn, axis=0)
    grad_middle = dealt_cot.astype(jnp.float32) + norm_backward(
        grad_ffn_in, middle, rate_ffn, gain_ffn
    )
    grad_branch = narrow_gather((BRANCH * grad_middle).astype(jnp.bfloat16)).reshape(
        all_rows, width
    )
    grad_mixed = times(grad_branch, wo).astype(jnp.bfloat16)
    grad_wo = contract_rows(grad_branch, attn_out)
    (sum_wo,) = ring_scatter([grad_wo], rank_count)

    grad_q, grad_k, grad_v, shared = attend_back(
        flags, seg_col, seg_row, queries, keys, values, before, mixed,
        grad_mixed.reshape(by_lane + (features,)), log_total,
    )
    back = jnp.stack(
        [
            lax.ppermute(shared[micro], "wide", pair_route(micro, rank_count, -1))
            for micro in range(MB)
        ]
    )
    angle_shape = by_lane + (2 * HEAD_DIM,)
    grad_qkv = join_grads(
        grad_q, grad_k, grad_v, back, cosine.reshape(angle_shape), sine.reshape(angle_shape)
    ).reshape(all_rows, 3 * features)
    grad_wqkv = contract_rows(attn_rows, grad_qkv)
    (sum_wqkv,) = ring_scatter([grad_wqkv], rank_count)
    grad_attn_in = narrow_scatter(
        times_transpose(grad_qkv, wqkv).astype(jnp.bfloat16).reshape(lane_count, row_count, width)
    )
    gain_total_attn = jnp.sum(grad_attn_in * resid * rate_attn, axis=0)
    grad_resid = grad_middle + norm_backward(grad_attn_in, resid, rate_attn, gain_attn)
    grad_tokens = exchange(
        (validity * grad_resid).astype(jnp.bfloat16), back_order, send_place
    )
    gain_sum_attn, gain_sum_ffn = lax.psum((gain_total_attn, gain_total_ffn), ("wide", "narrow"))
    return (
        output,
        grad_tokens,
        gain_sum_attn,
        gain_sum_ffn,
        sum_wqkv[:, :features],
        sum_wqkv[:, features : 2 * features],
        sum_wqkv[:, 2 * features :],
        sum_wo.T,
        sum_wg,
        sum_wu,
        sum_wd.T,
    )


def solution(mesh):
    placed = (
        P(("wide", "narrow"), None),
        P(),
        P(),
        P("wide", "narrow"),
        P("wide", "narrow"),
        P("wide", "narrow"),
        P("narrow", "wide"),
        P("wide", "narrow"),
        P("wide", "narrow"),
        P("narrow", "wide"),
        P(("wide", "narrow"), None),
        P(),
        P(),
    )
    return jax.shard_map(
        body,
        mesh=mesh,
        in_specs=placed,
        out_specs=(
            P(("wide", "narrow"), None),
            P(("wide", "narrow"), None),
            P(),
            P(),
            P("wide", "narrow"),
            P("wide", "narrow"),
            P("wide", "narrow"),
            P("narrow", "wide"),
            P("wide", "narrow"),
            P("wide", "narrow"),
            P("narrow", "wide"),
        ),
        check_vma=False,
    )
```

time: 2100 us -> 1050 us (0.50)
  waiting for transfers between devices: 1430 us -> 351 us
  matrix products: 338 us -> 159 us
  starting transfers between devices: 39.2 us -> 155 us
  local copies, waits for them, and re-layouts: 42.6 us -> 153 us
  Pallas kernels: 0 us -> 61.8 us
  blocking collectives: 102 us -> 50.9 us
    reduce_scatter x15 -> x0, waiting for transfers between devices: 758 us -> none  [the longest x1 129 us: body(): lax.psum_scatter(totals[5].astype(jnp.bfloat16), 'wide', scatter_dimensio...]
    all_gather x15 -> x0, waiting for transfers between devices: 564 us -> none  [the longest x1 111 us: body(): lax.all_gather(w_down, 'wide', axis=1, tiled=True)]
    ppermute x8 -> x92, waiting for transfers between devices: 47.3 us -> 337 us  [the longest x64 322 us: ring_send(): return lax.ppermute(block, 'wide', route)]
    dot_general x26 -> x4, matrix products: 181 us -> 45.3 us  [times(): return jnp.dot(left, right, preferred_element_type=jnp.float32)]
    ppermute x8 -> x92, starting transfers between devices: 19.1 us -> 138 us  [the longest x64 115 us: ring_send(): return lax.ppermute(block, 'wide', route)]
    pallas_call x0 -> x4, Pallas kernels: none -> 61.8 us  [the longest x1 19.4 us: attend_back(): pl.pallas_call(attend_back_kernel, out_shape=(wide, wide, wide, jax.Shape...]
    all_to_all x1 -> x0, blocking collectives: 60.8 us -> none  [body(): lax.all_to_all(pack_out(cotangent), 'wide', split_axis=0, concat_axis=0,...]
    dynamic_update_slice x0 -> x49, local copies, waits for them, and re-layouts: none -> 55.9 us  [the longest x36 41.1 us: assemble(): lax.dynamic_update_slice(full, piece[low:high], (rank * rows + start + lo...]
  transfers between devices with their start and end apart: 41 -> 96, of which waited for: 32 -> 33; matrix products, arithmetic and copies ran while one was open for 19% -> 30% of each run, Pallas kernels for 0% -> 6%
where the time goes in v1:
time: 1050 us; the launch traced here: 1040 us
  waiting for transfers between devices  351 us (33%)
  matrix products  159 us (15%)
  starting transfers between devices  155 us (15%)
  local copies, waits for them, and re-layouts  153 us (15%)
  other arithmetic  104 us (10%)
  Pallas kernels  61.8 us (6%)
  blocking collectives  50.9 us (5%)
    ppermute x64, waiting for transfers between devices, ring_send(): return lax.ppermute(block, 'wide', route)  322 us
    ppermute x64, starting transfers between devices, ring_send(): return lax.ppermute(block, 'wide', route)  115 us
    dot_general x5, matrix products, times_transpose(): lax.dot_general(left, right, (((1,), (1,)), ((), ())), preferred_element_...  64.1 us
    psum x1, blocking collectives, body(): lax.psum((gain_total_attn, gain_total_ffn), ('wide', 'narrow'))  50.9 us
    dot_general x5, matrix products, contract_rows(): lax.dot_general(left, right, (((0,), (0,)), ((), ())), preferred_element_...  49.5 us
    dot_general x4, matrix products, times(): return jnp.dot(left, right, preferred_element_type=jnp.float32)  45.3 us
    dynamic_update_slice x36, local copies, waits for them, and re-layouts, assemble(): lax.dynamic_update_slice(full, piece[low:high], (rank * rows + start + lo...  41.1 us
    convert_element_type x8, other arithmetic, ring_scatter(): up = ring_send(sum_up.astype(jnp.bfloat16), count, 1)  23.7 us
  transfers between devices with their start and end apart: 96, of which 33 were waited for; matrix products, arithmetic and copies ran while one was open for 30% of the time, Pallas kernels for 6%

profile of v1, /device:TPU:0, one launch (start us, length us, event | category | flops | bytes accessed | tf_op | source)
XLA Modules:
  0.0 1037.2 jit_solution(1504511327757430872)
XLA Ops:
  73.0 13.6 %collective-permute-start.7 = (bf16[288,1728]{1,0:T(8,128)(2,1)}, bf16[288,1728]{1,0:T(8,128)(2,1)}, u32[]{:S(2)}, u32[]{:S(2)}) collective-permute-start(bf16[288,1728]{1,0:T(8,128)(2,1)} %collective-permute-done.5), channel_id=1, source_target_pairs={{0,8},{8,16},{16,24},{24,28},{28,20},{20,12},{12,4},{4,0},{1,9},{9... | collective-permute-start | bytes 2985992 | tf_op jit(solution)/shard_map/ppermute | solution.py:34
  158.4 13.9 %project.1 = (bf16[1024,576]{1,0:T(8,128)(2,1)}, bf16[1024,576]{1,0:T(8,128)(2,1)}, bf16[1024,576]{1,0:T(8,128)(2,1)}) custom-call(bf16[1024,2304]{1,0:T(8,128)(2,1)} %bitcast.19.rows_ref, bf16[2304,1728]{1,0:T(8,128)(2,1)} %constant_dynamic-update-slice_fusion.24.weight_ref, f32[1024,128]{1,0:T(8,128)} %get-tuple-element.195.cos_ref, ...), custom_call_target="tpu_custom_call" | custom-call | flops 8153726976 | bytes 16220160 | tf_op jit(solution)/shard_map/project/pallas_call | solution.py:283
  205.3 12.2 %collective-permute-done.18 = bf16[288,576]{1,0:T(8,128)(2,1)S(1)} collective-permute-done((bf16[288,576]{1,0:T(8,128)(2,1)}, bf16[288,576]{1,0:T(8,128)(2,1)S(1)}, u32[]{:S(2)}, u32[]{:S(2)}) %collective-permute-start.18) | collective-permute-done | bytes 331808 | tf_op jit(solution)/shard_map/ppermute | solution.py:34
  238.5 18.5 %attend.1 = (bf16[4,2,128,576]{3,2,1,0:T(8,128)(2,1)}, f32[2,16,512]{2,1,0:T(8,128)}) custom-call(s32[2]{0:T(128)} %and_convert_fusion.flag_ref, s32[2,1024,1]{2,1,0:T(8,128)} %copy.186.seg_col_ref, s32[2,1,512]{2,1,0:T(1,128)} %broadcast_in_dim.181.seg_row_ref, bf16[4,2,128,576]{3,2,1,0:T(8,128)(2,1)} %bitcast.330, bf16[4,2,128,576]{3,2,1,0:T(8,128)(2,1)} %bitcast.310, ...), custom_call_target="tpu_custom_call" | custom-call | flops 4831838208 | bytes 7077888 | tf_op jit(solution)/shard_map/attend/pallas_call | solution.py:403
  280.8 34.1 %collective-permute-done.29 = bf16[576,1440]{1,0:T(8,128)(2,1)S(1)} collective-permute-done((bf16[576,1440]{1,0:T(8,128)(2,1)}, bf16[576,1440]{1,0:T(8,128)(2,1)S(1)}, u32[]{:S(2)}, u32[]{:S(2)}) %collective-permute-start.29) | collective-permute-done | bytes 1658912 | tf_op jit(solution)/shard_map/ppermute | solution.py:34
  322.0 33.3 %collective-permute-done.31 = bf16[576,1440]{1,0:T(8,128)(2,1)S(1)} collective-permute-done((bf16[576,1440]{1,0:T(8,128)(2,1)S(1)}, bf16[576,1440]{1,0:T(8,128)(2,1)S(1)}, u32[]{:S(2)}, u32[]{:S(2)}) %collective-permute-start.31) | collective-permute-done | bytes 1658912 | tf_op jit(solution)/shard_map/ppermute | solution.py:34
  360.3 17.8 %collective-permute-done.35 = bf16[288,1440]{1,0:T(8,128)(2,1)S(1)} collective-permute-done((bf16[288,1440]{1,0:T(8,128)(2,1)S(1)}, bf16[288,1440]{1,0:T(8,128)(2,1)S(1)}, u32[]{:S(2)}, u32[]{:S(2)}) %collective-permute-start.35) | collective-permute-done | bytes 829472 | tf_op jit(solution)/shard_map/ppermute | solution.py:34
  382.0 15.0 %collective-permute-done.33 = bf16[288,1440]{1,0:T(8,128)(2,1)S(1)} collective-permute-done((bf16[288,1440]{1,0:T(8,128)(2,1)S(1)}, bf16[288,1440]{1,0:T(8,128)(2,1)S(1)}, u32[]{:S(2)}, u32[]{:S(2)}) %collective-permute-start.33) | collective-permute-done | bytes 829472 | tf_op jit(solution)/shard_map/ppermute | solution.py:34
  400.1 13.9 %collective-permute-done.37 = bf16[288,1440]{1,0:T(8,128)(2,1)} collective-permute-done((bf16[288,1440]{1,0:T(8,128)(2,1)S(1)}, bf16[288,1440]{1,0:T(8,128)(2,1)}, u32[]{:S(2)}, u32[]{:S(2)}) %collective-permute-start.37) | collective-permute-done | bytes 829472 | tf_op jit(solution)/shard_map/ppermute | solution.py:34
  456.5 18.7 %multiply_convert_fusion.2 = (bf16[1024,1440]{0,1:T(8,128)(2,1)}, bf16[1024,1440]{0,1:T(8,128)(2,1)}, bf16[1024,1440]{0,1:T(8,128)(2,1)}) fusion(f32[1024,1440]{0,1:T(8,128)} %fusion.60, f32[1024,1440]{0,1:T(8,128)} %fusion.59, bf16[1024,2304]{1,0:T(8,128)(2,1)} %bitcast.297, bf16[2304,1440]{1,0:T(8,128)(2,1)} %copy-done.13), kind=kOutput, calls=%fused_computation.15 | convolution fusion | flops 6818365440 | bytes 31997952 | tf_op jit(solution)/shard_map/dot_general | solution.py:193
  486.6 14.9 %convolution_convert_fusion.6 = bf16[1024,2304]{1,0:T(8,128)(2,1)} fusion(bf16[1024,1440]{0,1:T(8,128)(2,1)S(1)} %copy-done.57, bf16[2304,1440]{1,0:T(8,128)(2,1)} %constant_dynamic-update-slice_fusion), kind=kOutput, calls=%fused_computation.20 | convolution fusion | flops 6797131776 | bytes 14303232 | tf_op jit(solution)/shard_map/dot_general | solution.py:197
  511.9 12.8 %fusion.61 = f32[1024,2304]{1,0:T(8,128)} fusion(bf16[1024,1440]{0,1:T(8,128)(2,1)} %get-tuple-element.113, bf16[2304,1440]{1,0:T(8,128)(2,1)S(1)} %bitcast.271), kind=kOutput, calls=%fused_computation.320 | convolution fusion | flops 6794772480 | bytes 19021824 | tf_op jit(solution)/shard_map/dot_general | solution.py:197
  549.2 13.1 %add_convert_fusion = bf16[1024,2304]{1,0:T(8,128)(2,1)S(1)} fusion(f32[1024,2304]{1,0:T(8,128)} %fusion.61, bf16[1024,1440]{0,1:T(8,128)(2,1)} %get-tuple-element.111, bf16[2304,1440]{1,0:T(8,128)(2,1)} %copy-done.13), kind=kOutput, calls=%fused_computation.12 | convolution fusion | flops 6799491072 | bytes 23740416 | tf_op jit(solution)/shard_map/dot_general | solution.py:197
  568.4 17.6 %collective-permute-done.89 = bf16[288,1440]{1,0:T(8,128)(2,1)S(1)} collective-permute-done((bf16[288,1440]{1,0:T(8,128)(2,1)S(1)}, bf16[288,1440]{1,0:T(8,128)(2,1)S(1)}, u32[]{:S(2)}, u32[]{:S(2)}) %collective-permute-start.89) | collective-permute-done | bytes 829472 | tf_op jit(solution)/shard_map/ppermute | solution.py:34
  592.4 17.1 %collective-permute-done.86 = bf16[288,1440]{1,0:T(8,128)(2,1)S(1)} collective-permute-done((bf16[288,1440]{1,0:T(8,128)(2,1)S(1)}, bf16[288,1440]{1,0:T(8,128)(2,1)S(1)}, u32[]{:S(2)}, u32[]{:S(2)}) %collective-permute-start.86) | collective-permute-done | bytes 829472 | tf_op jit(solution)/shard_map/ppermute | solution.py:34
  614.8 16.0 %collective-permute-done.90 = bf16[288,1440]{1,0:T(8,128)(2,1)S(1)} collective-permute-done((bf16[288,1440]{1,0:T(8,128)(2,1)S(1)}, bf16[288,1440]{1,0:T(8,128)(2,1)S(1)}, u32[]{:S(2)}, u32[]{:S(2)}) %collective-permute-start.90) | collective-permute-done | bytes 829472 | tf_op jit(solution)/shard_map/ppermute | solution.py:34
  658.8 13.8 %collective-permute-done.77 = bf16[576,1440]{1,0:T(8,128)(2,1)} collective-permute-done((bf16[576,1440]{1,0:T(8,128)(2,1)}, bf16[576,1440]{1,0:T(8,128)(2,1)}, u32[]{:S(2)}, u32[]{:S(2)}) %collective-permute-start.77) | collective-permute-done | bytes 1658912 | tf_op jit(solution)/shard_map/ppermute | solution.py:34
  681.9 12.1 %collective-permute-done.87 = bf16[288,1440]{1,0:T(8,128)(2,1)} collective-permute-done((bf16[288,1440]{1,0:T(8,128)(2,1)}, bf16[288,1440]{1,0:T(8,128)(2,1)}, u32[]{:S(2)}, u32[]{:S(2)}) %collective-permute-start.87) | collective-permute-done | bytes 829472 | tf_op jit(solution)/shard_map/ppermute | solution.py:34
  714.8 19.4 %attend_back.1 = (f32[4,2,128,576]{3,2,1,0:T(8,128)}, f32[4,2,128,576]{3,2,1,0:T(8,128)}, f32[4,2,128,576]{3,2,1,0:T(8,128)}, bf16[2,2,512,576]{3,2,1,0:T(8,128)(2,1)}) custom-call(s32[2]{0:T(128)} %and_convert_fusion.flag_ref, s32[2,1024,1]{2,1,0:T(8,128)} %copy.186.seg_col_ref, s32[2,1,512]{2,1,0:T(1,128)} %broadcast_in_dim.181.seg_row_ref, ...), custom_call_target="tpu_custom_call" | custom-call | flops 12079595520 | bytes 17694720 | tf_op jit(solution)/shard_map/attend_back/pallas_call | solution.py:506
  751.7 13.8 %collective-permute-start.68 = (bf16[144,576]{0,1:T(8,128)(2,1)S(1)}, bf16[144,576]{0,1:T(8,128)(2,1)S(1)}, u32[]{:S(2)}, u32[]{:S(2)}) collective-permute-start(bf16[144,576]{0,1:T(8,128)(2,1)S(1)} %get-tuple-element.164), channel_id=1, source_target_pairs={{0,8},{8,16},{16,24},{24,28},{28,20},{20,12},{12,4},{4,0},{1,9},{9... | collective-permute-start | bytes 497672 | tf_op jit(solution)/shard_map/ppermute | solution.py:34
  768.6 15.4 %collective-permute-done.68 = bf16[144,576]{0,1:T(8,128)(2,1)S(1)} collective-permute-done((bf16[144,576]{0,1:T(8,128)(2,1)S(1)}, bf16[144,576]{0,1:T(8,128)(2,1)S(1)}, u32[]{:S(2)}, u32[]{:S(2)}) %collective-permute-start.68) | collective-permute-done | bytes 165920 | tf_op jit(solution)/shard_map/ppermute | solution.py:34
  825.5 17.2 %convolution_convert_fusion.4 = bf16[1024,2304]{1,0:T(8,128)(2,1)} fusion(bf16[1024,1728]{1,0:T(8,128)(2,1)} %bitcast.304, bf16[2304,1728]{1,0:T(8,128)(2,1)} %constant_dynamic-update-slice_fusion.24.weight_ref), kind=kOutput, calls=%fused_computation.18 | convolution fusion | flops 8156086272 | bytes 16220160 | tf_op jit(solution)/shard_map/dot_general | solution.py:197
  913.0 45.9 %collective-permute-done.62 = bf16[288,1728]{1,0:T(8,128)(2,1)} collective-permute-done((bf16[288,1728]{1,0:T(8,128)(2,1)}, bf16[288,1728]{1,0:T(8,128)(2,1)}, u32[]{:S(2)}, u32[]{:S(2)}) %collective-permute-start.62) | collective-permute-done | bytes 995360 | tf_op jit(solution)/shard_map/ppermute | solution.py:34
  980.4 50.9 %all-reduce = (f32[2304]{0:T(1024)}, f32[2304]{0:T(1024)}) all-reduce(f32[2304]{0:T(1024)S(1)} %copy-done.43, f32[2304]{0:T(1024)S(1)} %get-tuple-element.90), channel_id=1, replica_groups=mesh['wide'=8,'narrow'=4] {'wide','narrow'}, use_global_device_ids=true, to_apply=%region_16.17 | all-reduce | flops 4608 | bytes 36864 | tf_op jit(solution)/shard_map/psum | solution.py:731
  (529 shorter events, 564.3 us)
Async XLA Ops:
  149.9 113.5 %collective-permute-start.48 = (bf16[256,2304]{1,0:T(8,128)(2,1)}, bf16[256,2304]{1,0:T(8,128)(2,1)}, u32[]{:S(2)}, u32[]{:S(2)}) collective-permute-start(bf16[256,2304]{1,0:T(8,128)(2,1)} %collective-permute-done.47), channel_id=1, source_target_pairs={{0,1},{1,0},{2,3},{3,2},{4,5},{5,4},{6,7},{7,6},{8,9},{9,8},{10,11... | collective-permute-start | bytes 3538952 | tf_op jit(solution)/shard_map/ppermute | solution.py:131
  179.6 51.6 %collective-permute-start.11 = (bf16[2,512,576]{1,2,0:T(8,128)(2,1)}, bf16[2,512,576]{1,2,0:T(8,128)(2,1)}, u32[]{:S(2)}, u32[]{:S(2)}) collective-permute-start(bf16[2,512,576]{1,2,0:T(8,128)(2,1)} %pad_maximum_fusion.5), channel_id=1, source_target_pairs={{0,4},{8,12},{16,20},{24,28},{1,5},{9,13},{17,21},{25,29},{2,6},{1... | collective-permute-start | bytes 3538952 | tf_op jit(solution)/shard_map/ppermute | solution.py:655
  269.7 47.6 %collective-permute-start.21 = (bf16[256,2304]{1,0:T(8,128)(2,1)S(1)}, bf16[256,2304]{1,0:T(8,128)(2,1)S(1)}, u32[]{:S(2)}, u32[]{:S(2)}) collective-permute-start(bf16[256,2304]{1,0:T(8,128)(2,1)S(1)} %get-tuple-element.154), channel_id=1, source_target_pairs={{0,1},{1,0},{2,3},{3,2},{4,5},{5,4},{6,7},{7,6},{8,9},{9,8},{10,11... | collective-permute-start | bytes 3538952 | tf_op jit(solution)/shard_map/ppermute | solution.py:131
  566.3 68.5 %collective-permute-start.43 = (bf16[256,2304]{1,0:T(8,128)(2,1)S(1)}, bf16[256,2304]{1,0:T(8,128)(2,1)S(1)}, u32[]{:S(2)}, u32[]{:S(2)}) collective-permute-start(bf16[256,2304]{1,0:T(8,128)(2,1)S(1)} %copy-done.33), channel_id=1, source_target_pairs={{0,1},{1,0},{2,3},{3,2},{4,5},{5,4},{6,7},{7,6},{8,9},{9,8},{10,11... | collective-permute-start | bytes 3538952 | tf_op jit(solution)/shard_map/ppermute | solution.py:131
  586.9 49.0 %collective-permute-start.49 = (bf16[256,2304]{1,0:T(8,128)(2,1)S(1)}, bf16[256,2304]{1,0:T(8,128)(2,1)S(1)}, u32[]{:S(2)}, u32[]{:S(2)}) collective-permute-start(bf16[256,2304]{1,0:T(8,128)(2,1)S(1)} %get-tuple-element.150), channel_id=1, source_target_pairs={{0,1},{1,0},{2,3},{3,2},{4,5},{5,4},{6,7},{7,6},{8,9},{9,8},{10,11... | collective-permute-start | bytes 3538952 | tf_op jit(solution)/shard_map/ppermute | solution.py:131
  591.7 51.7 %collective-permute-start.51 = (bf16[256,2304]{1,0:T(8,128)(2,1)S(1)}, bf16[256,2304]{1,0:T(8,128)(2,1)S(1)}, u32[]{:S(2)}, u32[]{:S(2)}) collective-permute-start(bf16[256,2304]{1,0:T(8,128)(2,1)S(1)} %fusion.24), channel_id=1, source_target_pairs={{0,2},{1,3},{2,0},{3,1},{4,6},{5,7},{6,4},{7,5},{8,10},{9,11},{10,... | collective-permute-start | bytes 3538952 | tf_op jit(solution)/shard_map/ppermute | solution.py:127
  635.9 58.2 %collective-permute-start.87 = (bf16[288,1440]{1,0:T(8,128)(2,1)}, bf16[288,1440]{1,0:T(8,128)(2,1)}, u32[]{:S(2)}, u32[]{:S(2)}) collective-permute-start(bf16[288,1440]{1,0:T(8,128)(2,1)} %get-tuple-element.124), channel_id=1, source_target_pairs={{0,8},{8,16},{16,24},{24,28},{28,20},{20,12},{12,4},{4,0},{1,9},{9... | collective-permute-start | bytes 2488328 | tf_op jit(solution)/shard_map/ppermute | solution.py:34
  636.8 61.4 %collective-permute-start.91 = (bf16[288,1440]{1,0:T(8,128)(2,1)}, bf16[288,1440]{1,0:T(8,128)(2,1)}, u32[]{:S(2)}, u32[]{:S(2)}) collective-permute-start(bf16[288,1440]{1,0:T(8,128)(2,1)} %get-tuple-element.125), channel_id=1, source_target_pairs={{0,4},{8,0},{16,8},{24,16},{28,24},{20,28},{12,20},{4,12},{1,5},{9... | collective-permute-start | bytes 2488328 | tf_op jit(solution)/shard_map/ppermute | solution.py:34
  652.0 49.4 %collective-permute-start.52 = (bf16[256,2304]{1,0:T(8,128)(2,1)}, bf16[256,2304]{1,0:T(8,128)(2,1)}, u32[]{:S(2)}, u32[]{:S(2)}) collective-permute-start(bf16[256,2304]{1,0:T(8,128)(2,1)} %get-tuple-element.103), channel_id=1, source_target_pairs={{0,1},{1,0},{2,3},{3,2},{4,5},{5,4},{6,7},{7,6},{8,9},{9,8},{10,11... | collective-permute-start | bytes 3538952 | tf_op jit(solution)/shard_map/ppermute | solution.py:131
  655.1 216.7 %all-to-all-start.1 = ((bf16[8,32,2304]{2,1,0:T(8,128)(2,1)}), bf16[8,32,2304]{2,1,0:T(8,128)(2,1)S(1)}, u32[]{:S(2)}, u32[]{:S(2)}) async-start(bf16[8,32,2304]{2,1,0:T(8,128)(2,1)} %bitcast.287), calls=%async_computation.1 | async-start | bytes 2359296 | tf_op jit(solution)/shard_map/all_to_all | solution.py:608
  677.7 87.7 %collective-permute-start.78 = (bf16[576,1440]{1,0:T(8,128)(2,1)}, bf16[576,1440]{1,0:T(8,128)(2,1)}, u32[]{:S(2)}, u32[]{:S(2)}) collective-permute-start(bf16[576,1440]{1,0:T(8,128)(2,1)} %add_convert_fusion.4), channel_id=1, source_target_pairs={{0,8},{8,16},{16,24},{24,28},{28,20},{20,12},{12,4},{4,0},{1,9},{9... | collective-permute-start | bytes 4976648 | tf_op jit(solution)/shard_map/ppermute | solution.py:34
  694.0 172.2 %collective-permute-start.82 = (bf16[576,1440]{1,0:T(8,128)(2,1)}, bf16[576,1440]{1,0:T(8,128)(2,1)}, u32[]{:S(2)}, u32[]{:S(2)}) collective-permute-start(bf16[576,1440]{1,0:T(8,128)(2,1)} %add_convert_fusion.2), channel_id=1, source_target_pairs={{0,4},{8,0},{16,8},{24,16},{28,24},{20,28},{12,20},{4,12},{1,5},{9... | collective-permute-start | bytes 4976648 | tf_op jit(solution)/shard_map/ppermute | solution.py:34
  740.1 54.9 %collective-permute-start.55 = (bf16[2,512,576]{1,2,0:T(8,128)(2,1)}, bf16[2,512,576]{1,2,0:T(8,128)(2,1)}, u32[]{:S(2)}, u32[]{:S(2)}) collective-permute-start(bf16[2,512,576]{1,2,0:T(8,128)(2,1)} %copy.189), channel_id=1, source_target_pairs={{4,0},{12,8},{20,16},{28,24},{5,1},{13,9},{21,17},{29,25},{6,2},{1... | collective-permute-start | bytes 3538952 | tf_op jit(solution)/shard_map/ppermute | solution.py:713
  743.7 54.0 %collective-permute-start.56 = (bf16[2,512,576]{1,2,0:T(8,128)(2,1)}, bf16[2,512,576]{1,2,0:T(8,128)(2,1)}, u32[]{:S(2)}, u32[]{:S(2)}) collective-permute-start(bf16[2,512,576]{1,2,0:T(8,128)(2,1)} %copy.191), channel_id=1, source_target_pairs={{8,4},{16,12},{24,20},{9,5},{17,13},{25,21},{10,6},{18,14},{26,22}... | collective-permute-start | bytes 3538952 | tf_op jit(solution)/shard_map/ppermute | solution.py:713
  792.0 55.8 %collective-permute-start.73 = (bf16[288,576]{0,1:T(8,128)(2,1)}, bf16[288,576]{0,1:T(8,128)(2,1)}, u32[]{:S(2)}, u32[]{:S(2)}) collective-permute-start(bf16[288,576]{0,1:T(8,128)(2,1)} %pad_maximum_fusion.12), channel_id=1, source_target_pairs={{0,4},{8,0},{16,8},{24,16},{28,24},{20,28},{12,20},{4,12},{1,5},{9... | collective-permute-start | bytes 995336 | tf_op jit(solution)/shard_map/ppermute | solution.py:34
  794.3 53.5 %collective-permute-start.69 = (bf16[288,576]{0,1:T(8,128)(2,1)}, bf16[288,576]{0,1:T(8,128)(2,1)}, u32[]{:S(2)}, u32[]{:S(2)}) collective-permute-start(bf16[288,576]{0,1:T(8,128)(2,1)} %pad_maximum_fusion.11), channel_id=1, source_target_pairs={{0,8},{8,16},{16,24},{24,28},{28,20},{20,12},{12,4},{4,0},{1,9},{9... | collective-permute-start | bytes 995336 | tf_op jit(solution)/shard_map/ppermute | solution.py:34
  873.5 92.5 %collective-permute-start.79 = (bf16[576,1440]{1,0:T(8,128)(2,1)}, bf16[576,1440]{1,0:T(8,128)(2,1)}, u32[]{:S(2)}, u32[]{:S(2)}) collective-permute-start(bf16[576,1440]{1,0:T(8,128)(2,1)} %add_convert_fusion.3), channel_id=1, source_target_pairs={{0,8},{8,16},{16,24},{24,28},{28,20},{20,12},{12,4},{4,0},{1,9},{9... | collective-permute-start | bytes 4976648 | tf_op jit(solution)/shard_map/ppermute | solution.py:34
  890.1 78.6 %collective-permute-start.83 = (bf16[576,1440]{1,0:T(8,128)(2,1)}, bf16[576,1440]{1,0:T(8,128)(2,1)}, u32[]{:S(2)}, u32[]{:S(2)}) collective-permute-start(bf16[576,1440]{1,0:T(8,128)(2,1)} %add_convert_fusion.1), channel_id=1, source_target_pairs={{0,4},{8,0},{16,8},{24,16},{28,24},{20,28},{12,20},{4,12},{1,5},{9... | collective-permute-start | bytes 4976648 | tf_op jit(solution)/shard_map/ppermute | solution.py:34
  891.5 81.8 %collective-permute-start.71 = (bf16[288,576]{0,1:T(8,128)(2,1)}, bf16[288,576]{0,1:T(8,128)(2,1)}, u32[]{:S(2)}, u32[]{:S(2)}) collective-permute-start(bf16[288,576]{0,1:T(8,128)(2,1)} %get-tuple-element.158), channel_id=1, source_target_pairs={{0,8},{8,16},{16,24},{24,28},{28,20},{20,12},{12,4},{4,0},{1,9},{9... | collective-permute-start | bytes 995336 | tf_op jit(solution)/shard_map/ppermute | solution.py:34
  896.1 62.8 %collective-permute-start.62 = (bf16[288,1728]{1,0:T(8,128)(2,1)}, bf16[288,1728]{1,0:T(8,128)(2,1)}, u32[]{:S(2)}, u32[]{:S(2)}) collective-permute-start(bf16[288,1728]{1,0:T(8,128)(2,1)} %get-tuple-element.116), channel_id=1, source_target_pairs={{0,8},{8,16},{16,24},{24,28},{28,20},{20,12},{12,4},{4,0},{1,9},{9... | collective-permute-start | bytes 2985992 | tf_op jit(solution)/shard_map/ppermute | solution.py:34
  897.9 63.7 %collective-permute-start.66 = (bf16[288,1728]{1,0:T(8,128)(2,1)}, bf16[288,1728]{1,0:T(8,128)(2,1)}, u32[]{:S(2)}, u32[]{:S(2)}) collective-permute-start(bf16[288,1728]{1,0:T(8,128)(2,1)} %get-tuple-element.117), channel_id=1, source_target_pairs={{0,4},{8,0},{16,8},{24,16},{28,24},{20,28},{12,20},{4,12},{1,5},{9... | collective-permute-start | bytes 2985992 | tf_op jit(solution)/shard_map/ppermute | solution.py:34
  909.1 126.1 %all-to-all-start.3 = ((bf16[8,32,2304]{2,1,0:T(8,128)(2,1)}), bf16[8,32,2304]{2,1,0:T(8,128)(2,1)S(1)}, u32[]{:S(2)}, u32[]{:S(2)}) async-start(bf16[8,32,2304]{2,1,0:T(8,128)(2,1)} %bitcast.90), calls=%async_computation.3 | async-start | bytes 2359296 | tf_op jit(solution)/shard_map/all_to_all | solution.py:608
  965.1 66.2 %collective-permute-start.63 = (bf16[288,1728]{1,0:T(8,128)(2,1)}, bf16[288,1728]{1,0:T(8,128)(2,1)}, u32[]{:S(2)}, u32[]{:S(2)}) collective-permute-start(bf16[288,1728]{1,0:T(8,128)(2,1)} %get-tuple-element.114), channel_id=1, source_target_pairs={{0,8},{8,16},{16,24},{24,28},{28,20},{20,12},{12,4},{4,0},{1,9},{9... | collective-permute-start | bytes 2985992 | tf_op jit(solution)/shard_map/ppermute | solution.py:34
  966.0 65.3 %collective-permute-start.67 = (bf16[288,1728]{1,0:T(8,128)(2,1)S(1)}, bf16[288,1728]{1,0:T(8,128)(2,1)}, u32[]{:S(2)}, u32[]{:S(2)}) collective-permute-start(bf16[288,1728]{1,0:T(8,128)(2,1)S(1)} %get-tuple-element.115), channel_id=1, source_target_pairs={{0,4},{8,0},{16,8},{24,16},{28,24},{20,28},{12,20},{4,12},{1,5},{9... | collective-permute-start | bytes 2985992 | tf_op jit(solution)/shard_map/ppermute | solution.py:34
  (142 other events, 3796.7 us)

commit v2 on v1

v2 whole, which is shorter than its diff:
```python
import math

import jax
import jax.numpy as jnp
from jax import lax
from jax.experimental import pallas as pl
from jax.experimental.layout import Layout, with_layout_constraint
from jax.experimental.pallas import tpu as pltpu
from jax.sharding import PartitionSpec as P

HEAD_DIM = 64
MB = 2
BLK = 8
UNIT = 64


BRANCH = 1.4 / math.sqrt(40.0)
EPSILON = 1e-05
NEGATIVE = -1e30
RING_MAX = 8
RING_MAX = 8


def ring_rank(place, count):
    place = lax.rem(place + 2 * count, count)
    return jnp.where(place < count // 2, 2 * place, 2 * count - 1 - 2 * place)


def ring_place(rank, count):
    return jnp.where(rank % 2 == 0, rank // 2, count - 1 - rank // 2)


def ring_send(block, count, direction):
    order = list(range(0, count, 2)) + list(range(count - 1, 0, -2))
    route = [(order[i], order[(i + direction) % count]) for i in range(count)]
    return lax.ppermute(block, "wide", route)


def after(value, *others):
    return lax.optimization_barrier((value,) + others)[0] if others else value


class Order:
    def __init__(self):
        self.marks = ()

    def tie(self, value):
        return after(value, *self.marks)

    def at(self, *marks):
        self.marks = tuple(marks)

    def land(self, *arrived):
        self.marks = self.marks + tuple(arrived)


PLAN = {'r1': 'wd', 'r2': 'split', 'r3': 'da2', 'r4': 'wu', 'e1': 'wu', 'e2': 'far3', 'e3': 'both3', 'e4': 'back2', 'u1': 'wqkv', 'u2': 'da1', 'u3': 'norm4', 'o1': '@q3', 'g1': '@o3', 'd1': '@g3', 'O': 'da1', 'P6': 1, 'W': 'wqkv', 'f1': 'wo', 'f2': 'da1', 'f3': 'norm4', 'f4': 'deal'}
LAND = {'r1': 'da2', 'r2': 'wg', 'r3': 'yf', 'r4': 'norm3', 'e1': 'norm3', 'e2': 'mixed', 'e3': 'back1', 'e4': 'da1', 'u1': 'sum4', 'u3': 'unpack', 'f1': 'sum4', 'f2': 'norm4', 'f3': 'unpack'}
MADE = {'e4': 'back1', 'e2': 'gather3'}


class Plan:
    def __init__(self, order):
        self.order, self.rings, self.sent = order, {}, {}
        self.passed = set()

    def add(self, name, ring):
        self.rings[name], self.sent[name] = ring, 0
        self.push(())

    def push(self, marks):
        for name, ring in self.rings.items():
            while self.sent[name] < ring.count // 2:
                step = PLAN.get(name + str(self.sent[name] + 1))
                if step is not None and step[0] == "@":
                    if self.sent.get(step[1], 0) < int(step[2]):
                        break
                    self.order.at(*self.hop(step[1:]))
                elif step is not None and step not in self.passed:
                    break
                else:
                    self.order.at(*(marks if step is not None else ()))
                ring.send(self.order)
                self.sent[name] += 1
        self.order.at()

    def hop(self, name):
        hops = self.rings[name[0]].hops
        return hops[int(name[1]) - 1] if hops else ()

    def done(self, step, *marks):
        self.passed.add(step)
        self.push(marks)

    def before(self, step, value):
        marks = []
        for name, ready in LAND.items():
            if ready == step and self.sent.get(name[0], 0) >= int(name[1]):
                marks += self.hop(name)
        for name, ready in MADE.items():
            if ready == step and self.sent.get(name[0], 0) >= int(name[1]):
                marks += self.rings[name[0]].messages[int(name[1]) - 1 :][:1] and list(
                    self.rings[name[0]].messages[int(name[1]) - 1]
                )
        return after(value, *marks)


class RingGather:
    def __init__(self, group, count):
        self.group, self.count, self.hops, self.messages = group, count, [], []
        self.block = jnp.concatenate(group, axis=0) if len(group) > 1 else group[0]

    def send(self, order):
        if self.count > RING_MAX:
            return
        up, down = self.hops[-1] if self.hops else (self.block, self.block)
        if len(self.hops) == self.count // 2 - 1:
            half = self.block.shape[0] // 16 * 8
            up, down = up[:half], down[half:]
            order.land(up, down)
        up, down = order.tie(up), order.tie(down)
        self.messages.append((up, down))
        self.hops.append((ring_send(up, self.count, 1), ring_send(down, self.count, -1)))

    def arrived(self):
        return self.hops[-1] if self.hops else ()

    def hop(self, index):
        return self.hops[index] if self.hops else ()

    def all(self, order):
        for _ in range(self.count // 2):
            self.send(order)
            order.at()

    def gathered(self):
        rows = self.group[0].shape[0]
        if not self.hops:
            fulls = [lax.all_gather(one, "wide", axis=0, tiled=True) for one in self.group]
            return [([full], [(0, 0, full.shape[0], None, 0)], rows) for full in fulls]
        far = self.count // 2
        found = []
        for step, (up, down) in enumerate(self.hops[:-1], 1):
            found += [(-step, 0, up), (step, 0, down)]
        up, down = self.hops[-1]
        found += [(far, 0, up), (far, up.shape[0], down)]
        out = []
        for index, own in enumerate(self.group):
            arrays, moves = [own], [(0, 0, rows, 0, 0)]
            first = index * rows
            for shift, start, piece in found:
                low = max(first, start)
                high = min(first + rows, start + piece.shape[0])
                if low < high:
                    arrays.append(piece)
                    moves.append((len(arrays) - 1, low - start, high - low, shift, low - first))
            out.append((arrays, moves, rows))
        return out


class RingSum:
    def __init__(self, fulls, count, where):
        self.fulls, self.count, self.where = fulls, count, where
        self.rows = fulls[0].shape[0] // count
        self.last = ()
        self.hops, self.messages = [], []
        self.hop = 0
        self.place = ring_place(lax.axis_index("wide"), count)
        self.half = self.rows * len(fulls) // 16 * 8

    def arrived(self):
        return self.last

    def local(self, shift):
        owner = ring_rank(self.place + shift, self.count)
        return jnp.concatenate(
            [
                lax.dynamic_slice_in_dim(full, owner * self.rows, self.rows, axis=0)
                for full in self.fulls
            ],
            axis=0,
        )

    def send(self, order):
        if self.count > RING_MAX:
            return
        self.hop += 1
        far, half = self.count // 2, self.half
        if self.hop == 1:
            both = self.local(far)
            up, down = order.tie(both[:half]), order.tie(both[half:])
        else:
            up, down = ring_add(
                self.where, self.count, far - self.hop + 1, self.fulls,
                order.tie(self.last[0]), self.last[1],
            )
        self.messages.append((up, down))
        self.last = (ring_send(up, self.count, 1), ring_send(down, self.count, -1))
        self.hops.append(self.last)

    def finish(self):
        if self.count > RING_MAX:
            return [
                lax.psum_scatter(full, "wide", scatter_dimension=0, tiled=True).astype(jnp.float32)
                for full in self.fulls
            ]
        up, down = self.last
        done = (
            self.local(0).astype(jnp.float32) + up.astype(jnp.float32) + down.astype(jnp.float32)
        )
        return [done[i * self.rows : (i + 1) * self.rows] for i in range(len(self.fulls))]


def swap_chip(block):
    return lax.ppermute(block, "narrow", [(0, 2), (1, 3), (2, 0), (3, 1)])


def swap_core(block):
    return lax.ppermute(block, "narrow", [(0, 1), (1, 0), (2, 3), (3, 2)])


class LaneGather:
    def __init__(self, block, order):
        self.block = order.tie(block)
        self.chip = swap_chip(self.block)
        self.core = swap_core(self.block)

    def finish(self, order):
        self.pieces = [self.block, self.core, self.chip, swap_core(order.tie(self.chip))]
        return self.pieces

    def whole(self):
        lane = lax.axis_index("narrow")
        full = jnp.zeros((4,) + self.block.shape, self.block.dtype)
        for index, piece in enumerate(self.pieces):
            full = lax.dynamic_update_slice(
                full, piece[None], (lane ^ index,) + (0,) * self.block.ndim
            )
        return full


class LaneSum:
    def __init__(self, own, across, pair, order):
        self.own, self.across = own, across
        self.got = swap_core(order.tie(pair))

    def cross(self, order):
        both = self.across.astype(jnp.float32) + self.got[0].astype(jnp.float32)
        both = order.tie(both.astype(jnp.bfloat16))
        order.land(both)
        self.far = swap_chip(both)

    def finish(self):
        return (
            self.own.astype(jnp.float32)
            + self.got[1].astype(jnp.float32)
            + self.far.astype(jnp.float32)
        )


def sum_over(value, axis, count):
    step = 1
    while step < count:
        value = value + lax.ppermute(value, axis, [(i, i ^ step) for i in range(count)])
        step *= 2
    return value


def angles(position):
    lane = jnp.arange(2 * HEAD_DIM, dtype=jnp.int32) % HEAD_DIM
    counter = (lane % (HEAD_DIM // 2)).astype(jnp.float32)
    frequency = jnp.exp(counter * (-2.0 * math.log(10000.0) / HEAD_DIM))
    phase_angle = position.astype(jnp.float32)[:, None] * frequency[None, :]
    sign = jnp.where(lane < HEAD_DIM // 2, -1.0, 1.0)
    return jnp.cos(phase_angle), jnp.sin(phase_angle) * sign[None, :]


def turn(field_in, cosine, sine, direction):
    rows, width = field_in.shape
    parts = []
    for low in range(0, width, 2 * HEAD_DIM):
        size = min(2 * HEAD_DIM, width - low)
        piece = field_in[:, low : low + size]
        if size < 2 * HEAD_DIM:
            piece = jnp.concatenate([piece, piece], axis=1)
        lane = lax.broadcasted_iota(jnp.int32, piece.shape, 1)
        swapped = jnp.where(
            lane % HEAD_DIM < HEAD_DIM // 2,
            pltpu.roll(piece, 2 * HEAD_DIM - HEAD_DIM // 2, 1),
            pltpu.roll(piece, HEAD_DIM // 2, 1),
        )
        parts.append((piece * cosine + direction * (swapped * sine))[:, :size])
    return jnp.concatenate(parts, axis=1)


def row_major(value):
    return with_layout_constraint(value, Layout(major_to_minor=tuple(range(value.ndim))))


def contract_rows(left, right):
    product = lax.dot_general(
        left, right, (((0,), (0,)), ((), ())), preferred_element_type=jnp.float32
    )
    return row_major(product.astype(jnp.bfloat16))


def times(left, right):
    return jnp.dot(left, right, preferred_element_type=jnp.float32)


def times_transpose(left, right):
    return lax.dot_general(
        left, right, (((1,), (1,)), ((), ())), preferred_element_type=jnp.float32
    )


def norm_rate(resid):
    return lax.rsqrt(jnp.mean(resid * resid, axis=1, keepdims=True) + EPSILON)


def norm_backward(grad_in, resid, rate, gain):
    scaled_grad = grad_in * gain[None, :]
    return rate * scaled_grad - resid * rate**3 * jnp.mean(
        scaled_grad * resid, axis=1, keepdims=True
    )


def invert_order(placing):
    counter = jnp.arange(placing.shape[0], dtype=jnp.int32)
    return jnp.sum(jnp.where(placing[None, :] == counter[:, None], counter[None, :], 0), axis=1)


def deal_routes(deal, my_rank, my_lane, rank_count, lane_count, block_count):
    per_pair = block_count // rank_count
    base_block = (my_rank * lane_count + my_lane) * block_count
    counter = jnp.arange(block_count, dtype=jnp.int32)
    every_block = jnp.arange(deal.shape[0], dtype=jnp.int32)
    owned = base_block + counter
    target = jnp.sum(jnp.where(deal[None, :] == owned[:, None], every_block[None, :], 0), axis=1)
    target_rank = target // (lane_count * block_count)
    target_slot = target % block_count
    earlier = (target_rank[None, :] == target_rank[:, None]) & (
        target_slot[None, :] < target_slot[:, None]
    )
    send_place = target_rank * per_pair + jnp.sum(earlier.astype(jnp.int32), axis=1)
    mine = lax.dynamic_slice_in_dim(deal, base_block, block_count)
    source_rank = mine // (lane_count * block_count)
    before = (source_rank[None, :] == source_rank[:, None]) & (counter[None, :] < counter[:, None])
    recv_place = source_rank * per_pair + jnp.sum(before.astype(jnp.int32), axis=1)
    return (send_place, recv_place)


def stream_layout(length_row, my_rank, slot_rows):
    extent = (length_row + UNIT - 1) // UNIT * UNIT
    begin = jnp.cumsum(extent) - extent
    places = my_rank * slot_rows - slot_rows + jnp.arange(2 * slot_rows, dtype=jnp.int32)
    ending = begin + length_row
    inside = (places[:, None] >= begin[None, :]) & (places[:, None] < ending[None, :])
    number = jnp.arange(length_row.shape[0], dtype=jnp.int32) + 1
    segment = jnp.sum(jnp.where(inside, number[None, :], 0), axis=1) - 1
    position = places - jnp.sum(jnp.where(inside, begin[None, :], 0), axis=1)
    return (segment, position)


VMEM_LIMIT = 60 * 1024 * 1024


def dot_nn(left, right):
    return jnp.dot(left, right, preferred_element_type=jnp.float32)


def dot_nt(left, right):
    return times_transpose(left, right)


def dot_tn(left, right):
    return lax.dot_general(
        left, right, (((0,), (0,)), ((), ())), preferred_element_type=jnp.float32
    )


def params():
    return pltpu.CompilerParams(vmem_limit_bytes=VMEM_LIMIT)


def cost(flops, bytes_accessed, transcendentals=0):
    return pl.CostEstimate(
        flops=flops, bytes_accessed=bytes_accessed, transcendentals=transcendentals
    )


ANY = pl.BlockSpec(memory_space=pl.ANY)


class Collector:
    def __init__(self, gathered):
        self.arrays, self.moves, self.rows = gathered
        self.height = self.rows * lax.axis_size("wide")
        self.width = self.arrays[0].shape[1]
        self.shape = jax.ShapeDtypeStruct((self.height, self.width), jnp.bfloat16)

    def scratch(self):
        return [
            pltpu.VMEM((self.height, self.width), jnp.bfloat16),
            pltpu.SemaphoreType.DMA((len(self.moves) + 1,)),
        ]

    def copies(self, where, refs, whole, sems):
        count = self.height // self.rows
        for index, (array, start, rows, shift, offset) in enumerate(self.moves):
            row = offset
            if shift is not None:
                owner = ring_rank(ring_place(where[2], count) + shift, count)
                row = pl.multiple_of(owner * self.rows + offset, 16)
            yield pltpu.make_async_copy(
                refs[array].at[pl.ds(start, rows), :], whole.at[pl.ds(row, rows), :], sems.at[index]
            )

    def start(self, *args):
        for copy in self.copies(*args):
            copy.start()

    def wait(self, *args):
        for copy in self.copies(*args):
            copy.wait()

    def out(self, whole, out_ref, sems):
        return pltpu.make_async_copy(whole, out_ref, sems.at[len(self.moves)])


class Lanes:
    def __init__(self, pieces):
        self.pieces = list(pieces)
        self.block = pieces[0].shape
        self.shape = jax.ShapeDtypeStruct((4,) + self.block, jnp.bfloat16)

    def scratch(self):
        return [pltpu.VMEM((4,) + self.block, jnp.bfloat16), pltpu.SemaphoreType.DMA((4,))]

    def start(self, refs, rows, sems):
        for index in range(4):
            pltpu.make_async_copy(refs[index], rows.at[index], sems.at[index]).start()

    def wait(self, step, refs, rows, sems):
        pltpu.make_async_copy(refs[0], rows.at[step], sems.at[step]).wait()


def by_lane(rows, width):
    return pl.BlockSpec((None, rows, width), lambda i, where: (where[0] ^ i, 0, 0))


def fixed(*shape):
    return pl.BlockSpec(shape, lambda i, where: (0,) * len(shape))


def whole(*shape):
    return pl.BlockSpec(
        shape, lambda i, where: (0,) * len(shape), pipeline_mode=pl.Buffered(1)
    )


def by_parity(parity, both):
    half = both.shape[0] // 2
    low, high = both[:half], both[half:]
    return jnp.where(parity == 0, low, high), jnp.where(parity == 0, high, low)


def project_kernel(weight, lanes, where, *refs):
    count = len(weight.arrays)
    weights, refs = refs[:count], refs[count:]
    pieces, refs = refs[:4], refs[4:]
    cos_ref, sin_ref, q_ref, send_ref, keep_ref, w_out, rows_out, w, w_sems, rows, r_sems, o_sems = refs
    skip = weight.width - 3 * q_ref.shape[-1]
    step = pl.program_id(0)

    @pl.when(step == 0)
    def _():
        lanes.start(pieces, rows, r_sems)
        weight.start(where, weights, w, w_sems)
        weight.wait(where, weights, w, w_sems)
        weight.out(w, w_out, w_sems).start()

    lanes.wait(step, pieces, rows, r_sems)
    pltpu.make_async_copy(rows.at[step], rows_out.at[where[0] ^ step], o_sems.at[step]).start()
    width = q_ref.shape[-1]
    z = dot_nn(rows[step], w[:, skip:])
    turned = turn(z[:, : 2 * width], cos_ref[...], sin_ref[...], 1.0)
    first, second = by_parity(where[1], turned[:, :width])
    q_ref[0], q_ref[1] = first.astype(jnp.bfloat16), second.astype(jnp.bfloat16)
    first, second = by_parity(where[1], pack_pair(turned[:, width:], z[:, 2 * width :]))
    send_ref[...], keep_ref[...] = first.astype(jnp.bfloat16), second.astype(jnp.bfloat16)

    @pl.when(step == 3)
    def _():
        weight.out(w, w_out, w_sems).wait()
        for index in range(4):
            pltpu.make_async_copy(rows.at[index], rows_out.at[index], o_sems.at[index]).wait()


def project(where, gathered, width, pieces, cosine, sine):
    weight, lanes = Collector(gathered), Lanes(pieces)
    count, depth = lanes.block
    angle = by_lane(count, 2 * HEAD_DIM)
    pair = pl.BlockSpec((2, None, count // 2, width), lambda i, where: (0, where[0] ^ i, 0, 0))
    out = jax.ShapeDtypeStruct((2, 4, count // 2, width), jnp.bfloat16)
    both = jax.ShapeDtypeStruct((4, count // 2, 2 * width), jnp.bfloat16)
    both_spec = by_lane(count // 2, 2 * width)
    return pl.pallas_call(
        lambda *refs: project_kernel(weight, lanes, *refs),
        out_shape=(out, both, both, weight.shape, lanes.shape),
        grid_spec=pltpu.PrefetchScalarGridSpec(
            num_scalar_prefetch=1,
            grid=(4,),
            in_specs=[ANY] * (len(weight.arrays) + 4) + [angle, angle],
            out_specs=(pair, both_spec, both_spec, ANY, ANY),
            scratch_shapes=weight.scratch() + lanes.scratch() + [pltpu.SemaphoreType.DMA((4,))],
        ),
        compiler_params=params(),
        cost_estimate=cost(8 * count * depth * 3 * width, 40 * count * depth),
        name="project",
    )(where, *weight.arrays, *lanes.pieces, cosine, sine)


def put_relative(step, value, own_ref, across_ref, pair_ref):
    @pl.when(step == 0)
    def _():
        own_ref[...] = value

    @pl.when(step == 2)
    def _():
        across_ref[...] = value

    @pl.when(step == 3)
    def _():
        pair_ref[0] = value

    @pl.when(step == 1)
    def _():
        pair_ref[1] = value


def relative_out(rows, width):
    shapes = (
        jax.ShapeDtypeStruct((rows, width), jnp.bfloat16),
        jax.ShapeDtypeStruct((rows, width), jnp.bfloat16),
        jax.ShapeDtypeStruct((2, rows, width), jnp.bfloat16),
    )
    specs = (whole(rows, width), whole(rows, width), whole(2, rows, width))
    return shapes, specs


def part_of(weight, width):
    columns = width if weight.shape[1] == width else (width + 127) // 128 * 128
    return pl.BlockSpec(
        (weight.shape[0], columns), lambda i, where: (0, 0), pipeline_mode=pl.Buffered(1)
    )


def merge_kernel(weight, where, *refs):
    count = len(weight.arrays)
    weights, refs = refs[:count], refs[count:]
    a_ref, b_ref, own_ref, across_ref, pair_ref, o_ref, w_out, w, w_sems = refs
    step = pl.program_id(0)

    @pl.when(step == 0)
    def _():
        weight.start(where, weights, w, w_sems)
        weight.wait(where, weights, w, w_sems)
        weight.out(w, w_out, w_sems).start()

    low, high = by_parity(where[1], jnp.concatenate([a_ref[...], b_ref[...]], axis=0))
    rows = jnp.concatenate([low, high], axis=0)
    o_ref[...] = rows
    put_relative(step, dot_nt(rows, w[...]).astype(jnp.bfloat16), own_ref, across_ref, pair_ref)

    @pl.when(step == 3)
    def _():
        weight.out(w, w_out, w_sems).wait()


def merge(where, gathered, first, second):
    weight = Collector(gathered)
    lanes, rows, width = first.shape
    shapes, specs = relative_out(2 * rows, weight.height)
    return pl.pallas_call(
        lambda *refs: merge_kernel(weight, *refs),
        out_shape=shapes + (jax.ShapeDtypeStruct((lanes, 2 * rows, width), jnp.bfloat16), weight.shape),
        grid_spec=pltpu.PrefetchScalarGridSpec(
            num_scalar_prefetch=1,
            grid=(4,),
            in_specs=[ANY] * len(weight.arrays) + [by_lane(rows, width)] * 2,
            out_specs=specs + (by_lane(2 * rows, width), ANY),
            scratch_shapes=weight.scratch(),
        ),
        compiler_params=params(),
        cost_estimate=cost(16 * rows * width * weight.height, 20 * rows * weight.height),
        name="merge",
    )(where, *weight.arrays, first, second)


def hidden_kernel(gate_w, up_w, lanes, where, *refs):
    gates, refs = refs[: len(gate_w.arrays)], refs[len(gate_w.arrays) :]
    ups, refs = refs[: len(up_w.arrays)], refs[len(up_w.arrays) :]
    pieces, refs = refs[:4], refs[4:]
    gate_ref, up_ref, hidden_ref, g_out, u_out, rows_out, g, g_sems, u, u_sems, rows, r_sems, o_sems = refs
    step = pl.program_id(0)

    @pl.when(step == 0)
    def _():
        lanes.start(pieces, rows, r_sems)
        gate_w.start(where, gates, g, g_sems)
        up_w.start(where, ups, u, u_sems)
        gate_w.wait(where, gates, g, g_sems)
        gate_w.out(g, g_out, g_sems).start()

    lanes.wait(step, pieces, rows, r_sems)
    pltpu.make_async_copy(rows.at[step], rows_out.at[where[0] ^ step], o_sems.at[step]).start()
    gate = dot_nn(rows[step], g[...])
    gate_ref[...] = gate

    @pl.when(step == 0)
    def _():
        up_w.wait(where, ups, u, u_sems)
        up_w.out(u, u_out, u_sems).start()

    up = dot_nn(rows[step], u[...])
    up_ref[...] = up
    hidden_ref[...] = (gate * jax.nn.sigmoid(gate) * up).astype(jnp.bfloat16)

    @pl.when(step == 3)
    def _():
        gate_w.out(g, g_out, g_sems).wait()
        up_w.out(u, u_out, u_sems).wait()
        for index in range(4):
            pltpu.make_async_copy(rows.at[index], rows_out.at[index], o_sems.at[index]).wait()


def hidden_units(where, gathered_gate, gathered_up, pieces):
    gate_w, up_w, lanes = Collector(gathered_gate), Collector(gathered_up), Lanes(pieces)
    rows, depth = lanes.block
    width = gate_w.width
    wide = jax.ShapeDtypeStruct((4, rows, width), jnp.float32)
    return pl.pallas_call(
        lambda *refs: hidden_kernel(gate_w, up_w, lanes, *refs),
        out_shape=(
            wide, wide, jax.ShapeDtypeStruct((4, rows, width), jnp.bfloat16),
            gate_w.shape, up_w.shape, lanes.shape,
        ),
        grid_spec=pltpu.PrefetchScalarGridSpec(
            num_scalar_prefetch=1,
            grid=(4,),
            in_specs=[ANY] * (len(gate_w.arrays) + len(up_w.arrays) + 4),
            out_specs=(by_lane(rows, width),) * 3 + (ANY,) * 3,
            scratch_shapes=gate_w.scratch() + up_w.scratch() + lanes.scratch()
            + [pltpu.SemaphoreType.DMA((4,))],
        ),
        compiler_params=params(),
        cost_estimate=cost(16 * rows * depth * width, 60 * rows * width, 4 * rows * width),
        name="hidden_units",
    )(where, *gate_w.arrays, *up_w.arrays, *lanes.pieces)


def split_kernel(down_w, where, *refs):
    downs, refs = refs[: len(down_w.arrays)], refs[len(down_w.arrays) :]
    cot_ref, gate_ref, up_ref, dg_ref, du_ref, d_out, d, d_sems = refs
    step = pl.program_id(0)

    @pl.when(step == 0)
    def _():
        down_w.start(where, downs, d, d_sems)
        down_w.wait(where, downs, d, d_sems)
        down_w.out(d, d_out, d_sems).start()

    grad = dot_nn(cot_ref[...], d[...])
    gate, up = gate_ref[...], up_ref[...]
    sigma = jax.nn.sigmoid(gate)
    part = grad * sigma
    dg_ref[...] = (part * up * (1.0 + gate * (1.0 - sigma))).astype(jnp.bfloat16)
    du_ref[...] = (part * gate).astype(jnp.bfloat16)

    @pl.when(step == 3)
    def _():
        down_w.out(d, d_out, d_sems).wait()


def split_grads(where, gathered, cot, gate, up):
    down_w = Collector(gathered)
    lanes, rows, width = gate.shape
    depth = cot.shape[2]
    narrow = jax.ShapeDtypeStruct(gate.shape, jnp.bfloat16)
    block = by_lane(rows, width)
    return pl.pallas_call(
        lambda *refs: split_kernel(down_w, *refs),
        out_shape=(narrow, narrow, down_w.shape),
        grid_spec=pltpu.PrefetchScalarGridSpec(
            num_scalar_prefetch=1,
            grid=(4,),
            in_specs=[ANY] * len(down_w.arrays) + [by_lane(rows, depth), block, block],
            out_specs=(block, block, ANY),
            scratch_shapes=down_w.scratch(),
        ),
        compiler_params=params(),
        cost_estimate=cost(8 * rows * depth * width, 60 * rows * width, 4 * rows * width),
        name="split_grads",
    )(where, *down_w.arrays, cot, gate, up)


def terms_kernel(count, where, *refs):
    total = None
    for index in range(count):
        rows, weight = refs[index][...], refs[count + index]
        term = dot_nt(rows, weight[:, weight.shape[1] - rows.shape[1] :])
        total = term if total is None else total + term
    put_relative(pl.program_id(0), total.astype(jnp.bfloat16), *refs[2 * count :])


def terms(where, pairs):
    rows = pairs[0][0].shape[1]
    height = pairs[0][1].shape[0]
    shapes, specs = relative_out(rows, height)
    depth = sum(weight.shape[1] for _, weight in pairs)
    return pl.pallas_call(
        lambda *refs: terms_kernel(len(pairs), *refs),
        out_shape=shapes,
        grid_spec=pltpu.PrefetchScalarGridSpec(
            num_scalar_prefetch=1,
            grid=(4,),
            in_specs=[by_lane(rows, one.shape[2]) for one, _ in pairs]
            + [whole(*weight.shape) for _, weight in pairs],
            out_specs=specs,
        ),
        compiler_params=params(),
        cost_estimate=cost(8 * rows * height * depth, 2 * (4 * rows + height) * depth),
        name="terms",
    )(where, *[one for one, _ in pairs], *[weight for _, weight in pairs])


def mixed_kernel(lanes, where, *refs):
    pieces, refs = refs[:4], refs[4:]
    w_ref, out_ref, rows_out, rows, r_sems, o_sems = refs
    step = pl.program_id(0)

    @pl.when(step == 0)
    def _():
        lanes.start(pieces, rows, r_sems)

    lanes.wait(step, pieces, rows, r_sems)
    pltpu.make_async_copy(rows.at[step], rows_out.at[where[0] ^ step], o_sems.at[step]).start()
    out = dot_nn(rows[step], w_ref[:, : out_ref.shape[-1]])
    first, second = by_parity(where[1], out)
    out_ref[0], out_ref[1] = first.astype(jnp.bfloat16), second.astype(jnp.bfloat16)

    @pl.when(step == 3)
    def _():
        for index in range(4):
            pltpu.make_async_copy(rows.at[index], rows_out.at[index], o_sems.at[index]).wait()


def mixed_grads(where, weight, width, pieces):
    lanes = Lanes(pieces)
    count, depth = lanes.block
    return pl.pallas_call(
        lambda *refs: mixed_kernel(lanes, *refs),
        out_shape=(jax.ShapeDtypeStruct((2, 4, count // 2, width), jnp.bfloat16), lanes.shape),
        grid_spec=pltpu.PrefetchScalarGridSpec(
            num_scalar_prefetch=1,
            grid=(4,),
            in_specs=[ANY] * 4 + [part_of(weight, width)],
            out_specs=(
                pl.BlockSpec((2, None, count // 2, width), lambda i, where: (0, where[0] ^ i, 0, 0)),
                ANY,
            ),
            scratch_shapes=lanes.scratch() + [pltpu.SemaphoreType.DMA((4,))],
        ),
        compiler_params=params(),
        cost_estimate=cost(8 * count * depth * width, 20 * count * depth),
        name="mixed_grads",
    )(where, *lanes.pieces, weight)


def ring_add_kernel(count, split, where, *refs):
    ups, downs, refs = refs[:count], refs[count : 2 * count], refs[2 * count :]
    up_in, down_in, up_out, down_out = refs
    step = pl.program_id(0)
    for index in range(count):

        @pl.when(step // 2 == index)
        def _():
            up = ups[index][...].astype(jnp.float32)
            down = downs[index][...].astype(jnp.float32)
            if split:
                up = jnp.where(step < count, up + up_in[...].astype(jnp.float32), up)
                down = jnp.where(step < count, down, down + down_in[...].astype(jnp.float32))
            else:
                up = up + up_in[...].astype(jnp.float32)
                down = down + down_in[...].astype(jnp.float32)
            up_out[...] = up.astype(jnp.bfloat16)
            down_out[...] = down.astype(jnp.bfloat16)


def ring_add(where, ranks, shift, fulls, up, down):
    count = len(fulls)
    rows, width = fulls[0].shape[0] // ranks, fulls[0].shape[1]
    part = rows // 2
    split = up.shape[0] < rows * count

    def local(index, direction):
        def at(i, where):
            owner = ring_rank(ring_place(where[2], ranks) + direction * shift, ranks)
            return (owner * 2 + jnp.clip(i - 2 * index, 0, 1), 0)

        return pl.BlockSpec((part, width), at)

    block = pl.BlockSpec((part, width), lambda i, where: (i, 0))
    upper, lower = block, block
    if split:
        upper = pl.BlockSpec((part, width), lambda i, where: (jnp.minimum(i, count - 1), 0))
        lower = pl.BlockSpec((part, width), lambda i, where: (jnp.maximum(i - count, 0), 0))
    out = jax.ShapeDtypeStruct((rows * count, width), jnp.bfloat16)
    return pl.pallas_call(
        lambda *refs: ring_add_kernel(count, split, *refs),
        out_shape=(out, out),
        grid_spec=pltpu.PrefetchScalarGridSpec(
            num_scalar_prefetch=1,
            grid=(2 * count,),
            in_specs=[local(index, 1) for index in range(count)]
            + [local(index, -1) for index in range(count)]
            + [upper, lower],
            out_specs=(block, block),
        ),
        compiler_params=params(),
        cost_estimate=cost(4 * rows * count * width, 12 * rows * count * width),
        name="ring_add",
    )(where, *fulls, *fulls, up, down)


def fill_bias(seg_col_ref, seg_row_ref, bias_own, bias_prev):
    slot = bias_own.shape[0]
    query = seg_row_ref[...]
    key = lax.broadcasted_iota(jnp.int32, (slot, slot), 0)
    place = lax.broadcasted_iota(jnp.int32, (slot, slot), 1)
    own = seg_col_ref[slot:, :]
    allowed = (own == query) & (query >= 0) & (key <= place) | (key == place)
    bias_own[...] = jnp.where(allowed, 0.0, NEGATIVE)
    if bias_prev is not None:
        before = seg_col_ref[:slot, :]
        bias_prev[...] = jnp.where((before == query) & (query >= 0), 0.0, NEGATIVE)


def over_pairs(width, body):
    pairs = width // (2 * HEAD_DIM)

    def step(index, carry):
        body(pl.multiple_of(index * 2 * HEAD_DIM, 2 * HEAD_DIM), index * 2, 2)
        return carry

    lax.fori_loop(0, pairs, step, 0)
    if width % (2 * HEAD_DIM):
        body(pairs * 2 * HEAD_DIM, pairs * 2, 1)


def head_mask(lanes, head, value):
    lane = lax.broadcasted_iota(jnp.int32, (1, lanes), 1)
    return jnp.where(lane // HEAD_DIM == head, value, 0.0).astype(jnp.bfloat16)


def flat(ref, low, lanes):
    value = ref[:, :, pl.ds(low, lanes)]
    return value.reshape(value.shape[0] * value.shape[1], lanes)


def pack_pair(keys, values):
    even = keys.shape[1] // (2 * HEAD_DIM) * 2 * HEAD_DIM
    return jnp.concatenate(
        [keys[:, :even], values[:, :even], keys[:, even:], values[:, even:]], axis=1
    )


def split_pair(both):
    width = both.shape[1] // 2
    even = width // (2 * HEAD_DIM) * 2 * HEAD_DIM
    odd = width - even
    return (
        jnp.concatenate([both[:, :even], both[:, 2 * even : 2 * even + odd]], axis=1),
        jnp.concatenate([both[:, even : 2 * even], both[:, 2 * even + odd :]], axis=1),
    )


def pair_lane(low, heads, which, width):
    even = width // (2 * HEAD_DIM) * 2 * HEAD_DIM
    if heads == 2:
        return pl.multiple_of(low + which * even, 2 * HEAD_DIM)
    return 2 * even + which * HEAD_DIM


def attend_kernel(with_prev, seg_col_ref, seg_row_ref, q_ref, kv_ref, *refs):
    if with_prev:
        before_ref, o_ref, lse_ref, bias_own, bias_prev = refs
    else:
        o_ref, lse_ref, bias_own = refs
        bias_prev = None
    fill_bias(seg_col_ref, seg_row_ref, bias_own, bias_prev)
    slot = bias_own.shape[0]
    part = slot // 2

    def pair(low, head, heads):
        lanes = heads * HEAD_DIM
        q = flat(q_ref, low, lanes)
        at_k, at_v = (pair_lane(low, heads, which, q_ref.shape[2]) for which in range(2))
        k, v = flat(kv_ref, at_k, lanes), flat(kv_ref, at_v, lanes)
        if with_prev:
            kp, vp = flat(before_ref, at_k, lanes), flat(before_ref, at_v, lanes)
        for half in range(2):
            first, keys = half * part, (half + 1) * part
            mixed = []
            for one in range(heads):
                qm = q[first : first + part] * head_mask(lanes, one, 1.0 / math.sqrt(HEAD_DIM))
                s = dot_nt(k[:keys], qm) + bias_own[:keys, first : first + part]
                top = jnp.max(s, axis=0, keepdims=True)
                if with_prev:
                    sp = dot_nt(kp, qm) + bias_prev[:, first : first + part]
                    top = jnp.maximum(top, jnp.max(sp, axis=0, keepdims=True))
                p = jnp.exp(s - top)
                total = jnp.sum(p, axis=0, keepdims=True)
                o = dot_tn(v[:keys], p.astype(jnp.bfloat16))
                if with_prev:
                    pp = jnp.exp(sp - top)
                    total = total + jnp.sum(pp, axis=0, keepdims=True)
                    o = o + dot_tn(vp, pp.astype(jnp.bfloat16))
                mixed.append(o[one * HEAD_DIM : (one + 1) * HEAD_DIM] / total)
                lse_ref[pl.ds(head + one, 1), first : first + part] = top + jnp.log(total)
            o = jnp.concatenate(mixed, axis=0).T
            quarter = o_ref.shape[1]
            o_ref[first // quarter : (first + part) // quarter, :, pl.ds(low, lanes)] = (
                o.astype(jnp.bfloat16).reshape(part // quarter, quarter, lanes)
            )

    over_pairs(q_ref.shape[2], pair)


def attend(slot, seg_col, seg_row, q, kv, before=None):
    _, lanes, rows, width = q.shape
    count = lanes * rows
    heads = width // HEAD_DIM
    with_prev = before is not None
    both = pl.BlockSpec((lanes, rows, 2 * width), lambda i: (0, 0, 0))
    return pl.pallas_call(
        lambda *refs: attend_kernel(with_prev, *refs),
        out_shape=(
            jax.ShapeDtypeStruct((lanes, rows, width), jnp.bfloat16),
            jax.ShapeDtypeStruct((16, count), jnp.float32),
        ),
        grid=(1,),
        in_specs=slot_specs(slot, lanes, rows, width) + [both] * (2 if with_prev else 1),
        out_specs=(
            pl.BlockSpec((lanes, rows, width), lambda i: (0, 0, 0)),
            pl.BlockSpec((16, count), lambda i: (0, 0)),
        ),
        scratch_shapes=[pltpu.VMEM((count, count), jnp.float32)] * (2 if with_prev else 1),
        compiler_params=params(),
        cost_estimate=cost(
            (5 if with_prev else 2) * heads * count * count * 256,
            12 * count * width,
            heads * count * count,
        ),
        name="attend",
    )(seg_col, seg_row, q, kv, *([before] if with_prev else []))


def slot_specs(slot, lanes, rows, width):
    count = lanes * rows
    return [
        pl.BlockSpec((None, 2 * count, 1), lambda i: (slot, 0, 0)),
        pl.BlockSpec((None, 1, count), lambda i: (slot, 0, 0)),
        pl.BlockSpec((None, lanes, rows, width), lambda i: (slot, 0, 0, 0)),
    ]


def attend_back_kernel(
    with_prev, seg_col_ref, seg_row_ref, q_ref, kv_ref, o_ref, do_ref, lse_ref, *refs
):
    if with_prev:
        before_ref, dq_ref, dk_ref, dv_ref, back_ref, bias_own, bias_prev = refs
    else:
        dq_ref, dk_ref, dv_ref, bias_own = refs
        bias_prev = None
    fill_bias(seg_col_ref, seg_row_ref, bias_own, bias_prev)
    slot = bias_own.shape[0]
    part = slot // 2
    quarter = q_ref.shape[1]
    scale = 1.0 / math.sqrt(HEAD_DIM)

    def pair(low, head, heads):
        lanes = heads * HEAD_DIM
        q, o, do = (flat(ref, low, lanes) for ref in (q_ref, o_ref, do_ref))
        at_k, at_v = (pair_lane(low, heads, which, q_ref.shape[2]) for which in range(2))
        k, v = flat(kv_ref, at_k, lanes), flat(kv_ref, at_v, lanes)
        if with_prev:
            kp, vp = flat(before_ref, at_k, lanes), flat(before_ref, at_v, lanes)
        product = (do.astype(jnp.float32) * o.astype(jnp.float32)).T
        dk = [0.0, 0.0]
        dv = [0.0, 0.0]
        dkp = dvp = 0.0
        for half in range(2):
            first, keys = half * part, (half + 1) * part
            turned = []
            for one in range(heads):
                span = slice(one * HEAD_DIM, (one + 1) * HEAD_DIM)
                delta = jnp.sum(product[span, first : first + part], axis=0, keepdims=True)
                lse = lse_ref[pl.ds(head + one, 1), first : first + part]
                qm = q[first : first + part] * head_mask(lanes, one, scale)
                dm = do[first : first + part] * head_mask(lanes, one, 1.0)
                p = jnp.exp(dot_nt(k[:keys], qm) + bias_own[:keys, first : first + part] - lse)
                ds = (p * (dot_nt(v[:keys], dm) - delta)).astype(jnp.bfloat16)
                new_dv = dot_nn(p.astype(jnp.bfloat16), dm)
                new_dk = dot_nn(ds, qm)
                for index in range(half + 1):
                    rows = slice(index * part, (index + 1) * part)
                    dv[index] = dv[index] + new_dv[rows]
                    dk[index] = dk[index] + new_dk[rows]
                dq = dot_tn(k[:keys], ds)
                if with_prev:
                    p = jnp.exp(dot_nt(kp, qm) + bias_prev[:, first : first + part] - lse)
                    ds = (p * (dot_nt(vp, dm) - delta)).astype(jnp.bfloat16)
                    dvp = dvp + dot_nn(p.astype(jnp.bfloat16), dm)
                    dkp = dkp + dot_nn(ds, qm)
                    dq = dq + dot_tn(kp, ds)
                turned.append(dq[span])
            dq = jnp.concatenate(turned, axis=0).T * scale
            dq_ref[first // quarter : (first + part) // quarter, :, pl.ds(low, lanes)] = dq.reshape(
                part // quarter, quarter, lanes
            )
        for index in range(2):
            span = slice(index * part // quarter, (index + 1) * part // quarter)
            shape = (part // quarter, quarter, lanes)
            dk_ref[span, :, pl.ds(low, lanes)] = dk[index].reshape(shape)
            dv_ref[span, :, pl.ds(low, lanes)] = dv[index].reshape(shape)
        if with_prev:
            shape = (slot // quarter, quarter, lanes)
            back_ref[:, :, pl.ds(at_k, lanes)] = dkp.astype(jnp.bfloat16).reshape(shape)
            back_ref[:, :, pl.ds(at_v, lanes)] = dvp.astype(jnp.bfloat16).reshape(shape)

    over_pairs(q_ref.shape[2], pair)


def attend_back(slot, seg_col, seg_row, q, kv, o, do, lse_in, before=None):
    _, lanes, rows, width = q.shape
    count = lanes * rows
    heads = width // HEAD_DIM
    with_prev = before is not None
    both = pl.BlockSpec((lanes, rows, 2 * width), lambda i: (0, 0, 0))
    one = pl.BlockSpec((lanes, rows, width), lambda i: (0, 0, 0))
    specs = slot_specs(slot, lanes, rows, width)
    wide = jax.ShapeDtypeStruct((lanes, rows, width), jnp.float32)
    sent = jax.ShapeDtypeStruct((lanes, rows, 2 * width), jnp.bfloat16)
    return pl.pallas_call(
        lambda *refs: attend_back_kernel(with_prev, *refs),
        out_shape=(wide, wide, wide) + ((sent,) if with_prev else ()),
        grid=(1,),
        in_specs=specs
        + [both, one, specs[2], pl.BlockSpec((16, count), lambda i: (0, 0))]
        + ([both] if with_prev else []),
        out_specs=(one, one, one) + ((both,) if with_prev else ()),
        scratch_shapes=[pltpu.VMEM((count, count), jnp.float32)] * (2 if with_prev else 1),
        compiler_params=params(),
        cost_estimate=cost(
            (12 if with_prev else 5) * heads * count * count * 256,
            30 * count * width,
            heads * count * count,
        ),
        name="attend_back",
    )(seg_col, seg_row, q, kv, o, do, lse_in, *([before] if with_prev else []))


def join_kernel(where, *refs):
    dq_a, dk_a, dv_a, dq_b, dk_b, dv_b, back_ref, cos_ref, sin_ref, out_ref = refs
    cos_a, cos_b = by_parity(where[1], cos_ref[...])
    sin_a, sin_b = by_parity(where[1], sin_ref[...])
    dk_back, dv_back = split_pair(back_ref[...])
    dk = dk_a[...] + dk_back.astype(jnp.float32)
    dv = dv_a[...] + dv_back.astype(jnp.float32)
    first = jnp.concatenate(
        [turn(dq_a[...], cos_a, sin_a, -1.0), turn(dk, cos_a, sin_a, -1.0), dv], axis=1
    )
    second = jnp.concatenate(
        [turn(dq_b[...], cos_b, sin_b, -1.0), turn(dk_b[...], cos_b, sin_b, -1.0), dv_b[...]], axis=1
    )
    half = first.shape[0]
    out_ref[:half] = jnp.where(where[1] == 0, first, second).astype(jnp.bfloat16)
    out_ref[half:] = jnp.where(where[1] == 0, second, first).astype(jnp.bfloat16)


def join_grads(where, first, second, back, cosine, sine):
    lanes, rows, width = first[0].shape
    block = by_lane(rows, width)
    both = by_lane(rows, 2 * width)
    angle = by_lane(2 * rows, 2 * HEAD_DIM)
    return pl.pallas_call(
        join_kernel,
        out_shape=jax.ShapeDtypeStruct((lanes, 2 * rows, 3 * width), jnp.bfloat16),
        grid_spec=pltpu.PrefetchScalarGridSpec(
            num_scalar_prefetch=1,
            grid=(lanes,),
            in_specs=[block] * 6 + [both, angle, angle],
            out_specs=by_lane(2 * rows, 3 * width),
        ),
        compiler_params=params(),
        cost_estimate=cost(16 * lanes * rows * width, 44 * lanes * rows * width),
        name="join_grads",
    )(where, *first, *second, back, cosine, sine)


def to_next(block, count, direction):
    route = [(low, low + 1) for low in range(count - 1)]
    return lax.ppermute(block, "wide", [(b, a) for a, b in route] if direction < 0 else route)


def body(
    tokens,
    norm_attn,
    norm_ffn,
    w_query,
    w_key,
    w_value,
    w_out,
    w_gate,
    w_up,
    w_down,
    cotangent,
    lengths,
    deal,
):
    rank_count = lax.axis_size("wide")
    lane_count = lax.axis_size("narrow")
    my_rank = lax.axis_index("wide")
    my_lane = lax.axis_index("narrow")
    row_count = tokens.shape[0]
    width = tokens.shape[1]
    block_count = row_count // BLK
    per_pair = block_count // rank_count
    micro_rows = row_count // MB
    slot_rows = lane_count * micro_rows
    all_rows = lane_count * row_count
    features = w_query.shape[1]
    shard = w_query.shape[0]
    send_place, recv_place = deal_routes(
        deal, my_rank, my_lane, rank_count, lane_count, block_count
    )
    send_order = invert_order(send_place)
    back_order = invert_order(recv_place)

    def exchange(flat_rows, order_of, extra=None):
        packed = flat_rows.reshape(block_count, BLK, width)[order_of].reshape(
            rank_count, per_pair * BLK, width
        )
        if extra is not None:
            extra = jnp.broadcast_to(extra[None], (rank_count,) + extra.shape)
            packed = jnp.concatenate([packed, extra], axis=1)
        return lax.all_to_all(order.tie(packed), "wide", split_axis=0, concat_axis=0, tiled=True)

    def unpack(got, placing):
        rows = got[:, : per_pair * BLK]
        return rows.reshape(block_count, BLK, width)[placing].reshape(row_count, width)

    def rows_of(array):
        return array.reshape(all_rows, array.shape[-1])

    order = Order()
    plan = Plan(order)
    ring_qkv = RingGather([jnp.concatenate([w_query, w_key, w_value], axis=1)], rank_count)
    ring_out = RingGather([w_out.T], rank_count)
    ring_ffn = RingGather([w_gate, w_up], rank_count)
    ring_down = RingGather([w_down.T], rank_count)
    for name, ring in (("q", ring_qkv), ("o", ring_out), ("g", ring_ffn), ("d", ring_down)):
        plan.add(name, ring)

    got_x = exchange(tokens, send_order)
    plan.done("start")
    if "C" not in PLAN:
        got_cot = exchange(cotangent, send_order)

    gain_attn = norm_attn.astype(jnp.float32)
    gain_ffn = norm_ffn.astype(jnp.float32)
    parity = my_rank % 2
    where = jnp.stack([my_lane, parity, my_rank]).astype(jnp.int32)
    layouts = [stream_layout(lengths[micro], my_rank, slot_rows) for micro in range(MB)]
    own_segment = jnp.concatenate(
        [
            lax.dynamic_slice_in_dim(one[0], slot_rows + my_lane * micro_rows, micro_rows)
            for one in layouts
        ]
    )
    validity = (own_segment >= 0).astype(jnp.float32)[:, None]
    row_position = jnp.stack(
        [one[1][slot_rows:].reshape(lane_count, micro_rows) for one in layouts], axis=1
    ).reshape(all_rows)
    cosine, sine = (
        one.reshape(lane_count, row_count, 2 * HEAD_DIM) for one in angles(row_position)
    )
    segments = [one[0] for one in layouts]
    by_slot = jnp.where(parity == 0, jnp.stack(segments), jnp.stack(segments[::-1]))
    seg_col = by_slot[:, :, None]
    seg_row = by_slot[:, None, slot_rows:]

    dealt_x = unpack(got_x, recv_place)
    resid = dealt_x.astype(jnp.float32) * validity
    rate_attn = norm_rate(resid)
    attn_in = (resid * rate_attn * gain_attn[None, :]).astype(jnp.bfloat16)
    attn_in = plan.before("norm1", attn_in)
    rows_attn = LaneGather(attn_in, order).finish(order)
    plan.done("norm1", attn_in)
    (got_qkv,) = ring_qkv.gathered()
    rows_attn[0] = plan.before("project", rows_attn[0])
    queries, sent_kv, kept_kv, wqkv, attn_rows = project(
        where, got_qkv, features, rows_attn, cosine, sine
    )
    before = to_next(sent_kv, rank_count, 1)
    plan.done("project", queries)
    out_first, lse_first = attend(
        0, seg_col, seg_row, plan.before("attend1", queries), sent_kv
    )
    plan.done("attend1", out_first)
    if PLAN.get("C") == "attend1":
        got_cot = exchange(after(cotangent, out_first), send_order)
    out_second, lse_second = attend(
        1, seg_col, seg_row, queries, plan.before("attend2", after(kept_kv, out_first)), before
    )
    plan.done("attend2", out_second)
    (got_out,) = ring_out.gathered()
    own, across, pair, attn_out, w_out_full = merge(
        where, got_out, out_first, plan.before("merge", out_second)
    )
    plan.done("merge", pair)
    if PLAN.get("C") == "merge":
        got_cot = exchange(after(cotangent, pair), send_order)
    sum_attn = LaneSum(own, across, pair, order)
    sum_attn.got = plan.before("cross1", sum_attn.got)
    sum_attn.cross(order)
    plan.done("cross1", sum_attn.got)
    if PLAN.get("C") == "cross1":
        got_cot = exchange(after(cotangent, sum_attn.got), send_order)
    order.at()
    middle = resid + BRANCH * sum_attn.finish()
    rate_ffn = norm_rate(middle)
    ffn_in = (middle * rate_ffn * gain_ffn[None, :]).astype(jnp.bfloat16)
    ffn_in = plan.before("norm2", ffn_in)
    gather_ffn = LaneGather(ffn_in, order)
    plan.done("norm2", ffn_in)
    gather_ffn.chip = plan.before("both2", gather_ffn.chip)
    rows_ffn = gather_ffn.finish(order)
    plan.done("both2", gather_ffn.chip)
    dealt_cot = unpack(got_cot, recv_place)
    cot_in = (BRANCH * dealt_cot.astype(jnp.float32)).astype(jnp.bfloat16)
    if PLAN.get("X"):
        cot_in = after(cot_in, {"norm2": ffn_in, "both2": gather_ffn.chip, "merge": pair}[PLAN["X"]])
    gather_cot = LaneGather(cot_in, order)
    gather_cot.finish(order)
    cot_branch = gather_cot.whole()
    (got_gate, got_up) = ring_ffn.gathered()
    rows_ffn[0] = plan.before("hidden", rows_ffn[0])
    gate, upward, hidden, wg, wu, ffn_rows = hidden_units(
        where, got_gate, got_up, rows_ffn
    )
    plan.done("hidden", hidden)
    grad_wd = contract_rows(rows_of(cot_branch), rows_of(plan.before("wd", hidden)))
    plan.add("r", RingSum([grad_wd], rank_count, where))
    plan.done("wd", grad_wd)
    (got_down,) = ring_down.gathered()
    grad_gate, grad_upward, wd = split_grads(
        where, got_down, plan.before("split", after(cot_branch, grad_wd)), gate, upward
    )
    plan.done("split", grad_gate)
    own, across, pair = terms(
        where, [(plan.before("da2", grad_gate), wg), (grad_upward, wu)]
    )
    plan.done("da2", pair)
    sum_grad_ffn = LaneSum(own, across, pair, order)
    grad_wg = contract_rows(
        rows_of(ffn_rows), rows_of(plan.before("wg", after(grad_gate, pair)))
    )
    plan.done("wg", grad_wg)
    sum_grad_ffn.got = plan.before("cross2", after(sum_grad_ffn.got, grad_wg))
    sum_grad_ffn.cross(order)
    order.at()
    grad_wu = contract_rows(
        rows_of(ffn_rows),
        rows_of(plan.before("wu", after(grad_upward, grad_wg, sum_grad_ffn.got))),
    )
    plan.add("e", RingSum([grad_wg, grad_wu], rank_count, where))
    plan.done("wu", grad_wu)
    own, across, pair = terms(where, [(plan.before("yf", after(hidden, grad_wu)), wd)])
    plan.done("yf", pair)
    sum_grad_ffn.far = plan.before("norm3", after(sum_grad_ffn.far, pair))
    plan.done("far3", sum_grad_ffn.far)
    grad_ffn_in = sum_grad_ffn.finish()
    grad_middle = dealt_cot.astype(jnp.float32) + norm_backward(
        grad_ffn_in, middle, rate_ffn, gain_ffn
    )
    grad_branch_in = (BRANCH * grad_middle).astype(jnp.bfloat16)
    gather_branch = LaneGather(plan.before("gather3", grad_branch_in), order)
    plan.done("norm3", gather_branch.block)
    gain_total_ffn = jnp.sum(grad_ffn_in * middle * rate_ffn, axis=0)
    sum_down_out = LaneSum(own, across, after(pair, gather_branch.block), order)
    gather_branch.chip = plan.before("both3", after(gather_branch.chip, sum_down_out.got))
    rows_branch = gather_branch.finish(order)
    plan.done("both3", gather_branch.chip)
    order.at(gather_branch.chip)
    sum_down_out.cross(order)
    order.at()
    rows_branch[0] = plan.before("mixed", rows_branch[0])
    grad_mixed, grad_branch = mixed_grads(where, w_out_full, features, rows_branch)
    plan.done("mixed", grad_mixed)
    late = PLAN.get("W", "wqkv")
    if late == "mixed":
        grad_wo = contract_rows(rows_of(grad_branch), rows_of(after(attn_out, grad_mixed)))
        plan.add("f", RingSum([grad_wo], rank_count, where))
        plan.done("wo", grad_wo)
        grad_mixed = after(grad_mixed, grad_wo)
    *grads_second, shared = attend_back(
        1, seg_col, seg_row, queries, kept_kv, out_second,
        plan.before("back2", grad_mixed), lse_second, before
    )
    back = to_next(shared, rank_count, -1)
    plan.done("back2", shared)
    grads_first = attend_back(
        0, seg_col, seg_row, queries, sent_kv, out_first,
        plan.before(
            "back1", after(grad_mixed, shared, *((sum_down_out.far,) if PLAN.get("P6") else ()))
        ),
        lse_first
    )
    plan.done("back1", grads_first[0])
    if late == "back1":
        grad_wo = contract_rows(rows_of(grad_branch), rows_of(after(attn_out, grads_first[0])))
        plan.add("f", RingSum([grad_wo], rank_count, where))
        plan.done("wo", grad_wo)
        back = after(back, grad_wo)
    output_rows = (middle + BRANCH * sum_down_out.finish()).astype(jnp.bfloat16)
    ready = PLAN.get("O")
    if ready in ("back1", "back2"):
        output_rows = after(output_rows, grads_first[0] if ready == "back1" else shared)
        got_output = exchange(output_rows, back_order)
    grad_qkv = join_grads(
        where, grads_first, grads_second,
        plan.before("join", after(back, grads_first[0])), cosine, sine
    )
    plan.done("join", grad_qkv)
    grad_wqkv = contract_rows(rows_of(attn_rows), rows_of(plan.before("wqkv", grad_qkv)))
    plan.add("u", RingSum([grad_wqkv], rank_count, where))
    plan.done("wqkv", grad_wqkv)
    tail = grad_wqkv
    if late == "wqkv":
        grad_wo = contract_rows(rows_of(grad_branch), rows_of(after(attn_out, grad_wqkv)))
        plan.add("f", RingSum([grad_wo], rank_count, where))
        plan.done("wo", grad_wo)
        tail = grad_wo
    if ready not in ("back1", "back2", "da1"):
        got_output = exchange(after(output_rows, tail), back_order)
    own, across, pair = terms(
        where,
        [
            (
                plan.before(
                    "da1", after(grad_qkv, tail, *((got_output,) if PLAN.get("OL") == "da1" else ()))
                ),
                wqkv,
            )
        ],
    )
    if ready == "da1":
        got_output = exchange(after(output_rows, pair), back_order)
    pair = plan.before("sum4", pair)
    if PLAN.get("OL") == "sum4":
        pair = after(pair, got_output)
    plan.done("da1", pair)
    sum_grad_attn = LaneSum(own, across, pair, order)
    sum_grad_attn.got = plan.before("cross4", sum_grad_attn.got)
    sum_grad_attn.cross(order)
    plan.done("cross4", sum_grad_attn.got)
    sum_grad_attn.far = plan.before("norm4", sum_grad_attn.far)
    grad_attn_in = sum_grad_attn.finish()
    gain_total_attn = jnp.sum(grad_attn_in * resid * rate_attn, axis=0)
    grad_resid = grad_middle + norm_backward(grad_attn_in, resid, rate_attn, gain_attn)
    gains = jnp.stack([gain_total_attn, gain_total_ffn])
    main = gains.astype(jnp.bfloat16)
    rest = (gains - main.astype(jnp.float32)).astype(jnp.bfloat16)
    extra = jnp.concatenate([main, rest, jnp.zeros((BLK - 4, width), jnp.bfloat16)], axis=0)
    got_grad = exchange((validity * grad_resid).astype(jnp.bfloat16), back_order, extra)
    plan.done("norm4", sum_grad_attn.far)
    plan.done("deal", got_grad)
    got_grad = plan.before("unpack", got_grad)
    extra = got_grad[:, per_pair * BLK :].astype(jnp.float32)
    gains = sum_over(jnp.sum(extra[:, :2] + extra[:, 2:4], axis=0), "narrow", lane_count)
    output = unpack(got_output, send_place)
    grad_tokens = unpack(got_grad, send_place)
    (sum_wd,) = plan.rings["r"].finish()
    sum_wg, sum_wu = plan.rings["e"].finish()
    (sum_wo,) = plan.rings["f"].finish()
    (sum_wqkv,) = plan.rings["u"].finish()
    return (
        output,
        grad_tokens,
        gains[0],
        gains[1],
        sum_wqkv[:, :features],
        sum_wqkv[:, features : 2 * features],
        sum_wqkv[:, 2 * features :],
        sum_wo.T,
        sum_wg,
        sum_wu,
        sum_wd.T,
    )


def solution(mesh):
    placed = (
        P(("wide", "narrow"), None),
        P(),
        P(),
        P("wide", "narrow"),
        P("wide", "narrow"),
        P("wide", "narrow"),
        P("narrow", "wide"),
        P("wide", "narrow"),
        P("wide", "narrow"),
        P("narrow", "wide"),
        P(("wide", "narrow"), None),
        P(),
        P(),
    )
    return jax.shard_map(
        body,
        mesh=mesh,
        in_specs=placed,
        out_specs=(
            P(("wide", "narrow"), None),
            P(("wide", "narrow"), None),
            P(),
            P(),
            P("wide", "narrow"),
            P("wide", "narrow"),
            P("wide", "narrow"),
            P("narrow", "wide"),
            P("wide", "narrow"),
            P("wide", "narrow"),
            P("narrow", "wide"),
        ),
        check_vma=False,
    )
```

time: 1050 us -> 956 us (0.910)
  Pallas kernels: 61.8 us -> 247 us
  matrix products: 159 us -> 52.1 us
  local copies, waits for them, and re-layouts: 153 us -> 51.3 us
  blocking collectives: 50.9 us -> 0 us
  other arithmetic: 104 us -> 63.2 us
  waiting for transfers between devices: 351 us -> 387 us
    pallas_call x4 -> x25, Pallas kernels: 61.8 us -> 247 us  [the longest x3 55.6 us: terms(): pl.pallas_call(lambda *refs: terms_kernel(len(pairs), *refs), out_shape=s...]
    dot_general x9 -> x0, matrix products: 109 us -> none  [the longest x5 64.1 us: times_transpose(): lax.dot_general(left, right, (((1,), (1,)), ((), ())), preferred_element_...]
    dynamic_update_slice x49 -> x3, local copies, waits for them, and re-layouts: 55.9 us -> 4.6 us  [whole(): lax.dynamic_update_slice(full, piece[None], (lane ^ index,) + (0,) * self...]
    psum x1 -> x0, blocking collectives: 50.9 us -> none  [body(): lax.psum((gain_total_attn, gain_total_ffn), ('wide', 'narrow'))]
    ppermute x4, waiting for transfers between devices: 0.01 us -> 34.6 us  [the longest x2 34.6 us: to_next(): lax.ppermute(block, 'wide', [(b, a) for a, b in route] if direction < 0 e...]
    ppermute x8, waiting for transfers between devices: 13.8 us -> 40.7 us  [swap_chip(): return lax.ppermute(block, 'narrow', [(0, 2), (1, 3), (2, 0), (3, 1)])]
    ppermute x64, waiting for transfers between devices: 322 us -> 300 us  [ring_send(): return lax.ppermute(block, 'wide', route)]
    convert_element_type x17 -> x11, other arithmetic: 39.2 us -> 20.1 us  [the longest x4 11.3 us: cross(): both = order.tie(both.astype(jnp.bfloat16))]
  transfers between devices with their start and end apart: 96 -> 92, of which waited for: 33 -> 42; matrix products, arithmetic and copies ran while one was open for 30% -> 15% of each run, Pallas kernels for 6% -> 25%
where the time goes in v2:
time: 956 us; the launch traced here: 948 us
  waiting for transfers between devices  387 us (40%)
  Pallas kernels  247 us (26%)
  starting transfers between devices  145 us (15%)
  other arithmetic  63.2 us (7%)
  matrix products  52.1 us (5%)
  local copies, waits for them, and re-layouts  51.3 us (5%)
    ppermute x64, waiting for transfers between devices, ring_send(): return lax.ppermute(block, 'wide', route)  300 us
    ppermute x64, starting transfers between devices, ring_send(): return lax.ppermute(block, 'wide', route)  111 us
    pallas_call x3, Pallas kernels, terms(): pl.pallas_call(lambda *refs: terms_kernel(len(pairs), *refs), out_shape=s...  55.6 us
    dot_general x5, matrix products, contract_rows(): lax.dot_general(left, right, (((0,), (0,)), ((), ())), preferred_element_...  52.1 us
    pallas_call x12, Pallas kernels, ring_add(): pl.pallas_call(lambda *refs: ring_add_kernel(count, split, *refs), out_sh...  51.4 us
    ppermute x8, waiting for transfers between devices, swap_chip(): return lax.ppermute(block, 'narrow', [(0, 2), (1, 3), (2, 0), (3, 1)])  40.7 us
    ppermute x2, waiting for transfers between devices, to_next(): lax.ppermute(block, 'wide', [(b, a) for a, b in route] if direction < 0 e...  34.6 us
    pallas_call x2, Pallas kernels, attend_back(): pl.pallas_call(lambda *refs: attend_back_kernel(with_prev, *refs), out_sh...  27.2 us
  transfers between devices with their start and end apart: 92, of which 42 were waited for; matrix products, arithmetic and copies ran while one was open for 15% of the time, Pallas kernels for 25%

profile of v2, /device:TPU:0, one launch (start us, length us, event | category | flops | bytes accessed | tf_op | source)
XLA Modules:
  0.0 948.0 jit_solution(13073378851023271407)
XLA Ops:
  17.0 38.4 %collective-permute-done.refs_2_ = bf16[288,1728]{1,0:T(8,128)(2,1)S(1)} collective-permute-done((bf16[288,1728]{1,0:T(8,128)(2,1)S(1)}, bf16[288,1728]{1,0:T(8,128)(2,1)S(1)}, u32[]{:S(2)}, u32[]{:S(2)}) %collective-permute-start) | collective-permute-done | bytes 995360 | tf_op jit(solution)/shard_map/ppermute | solution.py:36
  64.9 20.5 %collective-permute-done.1.refs_4_ = bf16[288,1728]{1,0:T(8,128)(2,1)} collective-permute-done((bf16[288,1728]{1,0:T(8,128)(2,1)S(1)}, bf16[288,1728]{1,0:T(8,128)(2,1)}, u32[]{:S(2)}, u32[]{:S(2)}) %collective-permute-start.1) | collective-permute-done | bytes 995360 | tf_op jit(solution)/shard_map/ppermute | solution.py:36
  92.7 17.6 %collective-permute-done.2.refs_6_ = bf16[288,1728]{1,0:T(8,128)(2,1)} collective-permute-done((bf16[288,1728]{1,0:T(8,128)(2,1)}, bf16[288,1728]{1,0:T(8,128)(2,1)}, u32[]{:S(2)}, u32[]{:S(2)}) %collective-permute-start.2) | collective-permute-done | bytes 995360 | tf_op jit(solution)/shard_map/ppermute | solution.py:36
  145.4 11.3 %collective-permute-done.11.refs_7_ = bf16[288,576]{1,0:T(8,128)(2,1)S(1)} collective-permute-done((bf16[288,576]{1,0:T(8,128)(2,1)}, bf16[288,576]{1,0:T(8,128)(2,1)S(1)}, u32[]{:S(2)}, u32[]{:S(2)}) %collective-permute-start.11) | collective-permute-done | bytes 331808 | tf_op jit(solution)/shard_map/ppermute | solution.py:36
  158.8 17.9 %project.1 = (bf16[2,4,128,576]{3,2,1,0:T(8,128)(2,1)}, bf16[4,128,1152]{2,1,0:T(8,128)(2,1)}, bf16[4,128,1152]{2,1,0:T(8,128)(2,1)}, bf16[2304,1728]{1,0:T(8,128)(2,1)}, bf16[4,256,2304]{2,1,0:T(8,128)(2,1)}) custom-call(s32[3]{0:T(128)} %pad_add_fusion.2.refs_0_.where, bf16[288,1728]{1,0:T(8,128)(2,1)} %copy-done.33, bf16[288,1728]{1,0:T(8,128)(2,1)} %copy-done.69, ...), custom_call_target="tpu_custom_call" | custom-call | flops 8153726976 | bytes 23592960 | tf_op jit(solution)/shard_map/project/pallas_call | solution.py:508
  200.3 30.4 %collective-permute-done.19.refs_4_.refs_7_ = bf16[4,128,1152]{2,1,0:T(8,128)(2,1)} collective-permute-done((bf16[4,128,1152]{2,1,0:T(8,128)(2,1)}, bf16[4,128,1152]{2,1,0:T(8,128)(2,1)}, u32[]{:S(2)}, u32[]{:S(2)}) %collective-permute-start.19) | collective-permute-done | bytes 1179680 | tf_op jit(solution)/shard_map/ppermute | solution.py:1115
  230.7 13.6 %attend.3 = (bf16[4,128,576]{2,1,0:T(8,128)(2,1)}, f32[16,512]{1,0:T(8,128)}) custom-call(s32[2,1024,1]{2,1,0:T(8,128)} %add_select_fusion.refs_0_, s32[2,1,512]{2,1,0:T(1,128)} %broadcast_in_dim.151.refs_1_, bf16[2,4,128,576]{3,2,1,0:T(8,128)(2,1)} %get-tuple-element.137.refs_2_, bf16[4,128,1152]{2,1,0:T(8,128)(2,1)} %get-tuple-element.141.refs_3_, ...), custom_call_target="tpu_custom_call" | custom-call | flops 3019898880 | bytes 3538944 | tf_op jit(solution)/shard_map/attend/pallas_call | solution.py:947
  259.5 24.1 %collective-permute-done.24.refs_4_.refs_12_ = bf16[576,1440]{1,0:T(8,128)(2,1)} collective-permute-done((bf16[576,1440]{1,0:T(8,128)(2,1)}, bf16[576,1440]{1,0:T(8,128)(2,1)}, u32[]{:S(2)}, u32[]{:S(2)}) %collective-permute-start.24) | collective-permute-done | bytes 1658912 | tf_op jit(solution)/shard_map/ppermute | solution.py:36
  291.3 25.0 %collective-permute-done.26.refs_6_.refs_14_ = bf16[576,1440]{1,0:T(8,128)(2,1)} collective-permute-done((bf16[576,1440]{1,0:T(8,128)(2,1)}, bf16[576,1440]{1,0:T(8,128)(2,1)}, u32[]{:S(2)}, u32[]{:S(2)}) %collective-permute-start.26) | collective-permute-done | bytes 1658912 | tf_op jit(solution)/shard_map/ppermute | solution.py:36
  372.3 12.6 %collective-permute-done.37.refs_6_ = bf16[288,1440]{1,0:T(8,128)(2,1)S(1)} collective-permute-done((bf16[288,1440]{1,0:T(8,128)(2,1)S(1)}, bf16[288,1440]{1,0:T(8,128)(2,1)S(1)}, u32[]{:S(2)}, u32[]{:S(2)}) %collective-permute-start.37) | collective-permute-done | bytes 829472 | tf_op jit(solution)/shard_map/ppermute | solution.py:36
  391.6 15.0 %collective-permute-done.38.refs_7_ = bf16[288,1440]{1,0:T(8,128)(2,1)S(1)} collective-permute-done((bf16[288,1440]{1,0:T(8,128)(2,1)S(1)}, bf16[288,1440]{1,0:T(8,128)(2,1)S(1)}, u32[]{:S(2)}, u32[]{:S(2)}) %collective-permute-start.38) | collective-permute-done | bytes 829472 | tf_op jit(solution)/shard_map/ppermute | solution.py:36
  412.8 25.1 %hidden_units.1 = (f32[4,256,1440]{2,1,0:T(8,128)}, f32[4,256,1440]{2,1,0:T(8,128)}, bf16[4,256,1440]{2,1,0:T(8,128)(2,1)}, bf16[2304,1440]{1,0:T(8,128)(2,1)}, ...) custom-call(s32[3]{0:T(128)} %pad_add_fusion.2.refs_0_.where, bf16[288,1440]{1,0:T(8,128)(2,1)} %refs_1_.1, ...), custom_call_target="tpu_custom_call" | custom-call | flops 13589544960 | bytes 22118400 | tf_op jit(solution)/shard_map/hidden_units/pallas_call | solution.py:643
  455.0 17.2 %split_grads.1 = (bf16[4,256,1440]{2,1,0:T(8,128)(2,1)}, bf16[4,256,1440]{2,1,0:T(8,128)(2,1)}, bf16[2304,1440]{1,0:T(8,128)(2,1)}) custom-call(s32[3]{0:T(128)} %pad_add_fusion.2.refs_0_.where, bf16[288,1440]{1,0:T(8,128)(2,1)} %bitcast.24.refs_1_, bf16[288,1440]{1,0:T(8,128)(2,1)} %collective-permute-done.33.refs_2_, bf16[288,1440]{1,0:T(8,128)(2,1)} %copy-done.70, ...), custom_call_target="tpu_custom_call" | custom-call | flops 6794772480 | bytes 22118400 | tf_op jit(solution)/shard_map/split_grads/pallas_call | solution.py:692
  478.5 24.4 %terms.3 = (bf16[256,2304]{1,0:T(8,128)(2,1)}, bf16[256,2304]{1,0:T(8,128)(2,1)}, bf16[2,256,2304]{2,1,0:T(8,128)(2,1)}) custom-call(s32[3]{0:T(128)} %pad_add_fusion.2.refs_0_.where, bf16[4,256,1440]{2,1,0:T(8,128)(2,1)} %get-tuple-element.169.refs_1_, bf16[4,256,1440]{2,1,0:T(8,128)(2,1)} %get-tuple-element.171.refs_2_, ...), custom_call_target="tpu_custom_call" | custom-call | flops 13589544960 | bytes 19169280 | tf_op jit(solution)/shard_map/terms/pallas_call | solution.py:722
  548.7 14.7 %terms.4 = (bf16[256,2304]{1,0:T(8,128)(2,1)}, bf16[256,2304]{1,0:T(8,128)(2,1)}, bf16[2,256,2304]{2,1,0:T(8,128)(2,1)}) custom-call(s32[3]{0:T(128)} %pad_add_fusion.2.refs_0_.where, bf16[4,256,1440]{2,1,0:T(8,128)(2,1)} %get-tuple-element.176.refs_1_, bf16[2304,1440]{1,0:T(8,128)(2,1)} %get-tuple-element.177.refs_2_), custom_call_target="tpu_custom_call" | custom-call | flops 6794772480 | bytes 9584640 | tf_op jit(solution)/shard_map/terms/pallas_call | solution.py:722
  566.4 16.2 %collective-permute-done.54.refs_5_ = bf16[288,1440]{1,0:T(8,128)(2,1)} collective-permute-done((bf16[288,1440]{1,0:T(8,128)(2,1)}, bf16[288,1440]{1,0:T(8,128)(2,1)}, u32[]{:S(2)}, u32[]{:S(2)}) %collective-permute-start.54) | collective-permute-done | bytes 829472 | tf_op jit(solution)/shard_map/ppermute | solution.py:36
  601.8 27.5 %collective-permute-done.57.refs_3_ = bf16[256,2304]{1,0:T(8,128)(2,1)} collective-permute-done((bf16[256,2304]{1,0:T(8,128)(2,1)S(1)}, bf16[256,2304]{1,0:T(8,128)(2,1)}, u32[]{:S(2)}, u32[]{:S(2)}) %collective-permute-start.57) | collective-permute-done | bytes 1179680 | tf_op jit(solution)/shard_map/ppermute | solution.py:215
  661.3 16.6 %attend_back.2 = (f32[4,128,576]{2,1,0:T(8,128)}, f32[4,128,576]{2,1,0:T(8,128)}, f32[4,128,576]{2,1,0:T(8,128)}, bf16[4,128,1152]{2,1,0:T(8,128)(2,1)}) custom-call(s32[2,1024,1]{2,1,0:T(8,128)} %add_select_fusion.refs_0_, s32[2,1,512]{2,1,0:T(1,128)} %broadcast_in_dim.151.refs_1_, bf16[2,4,128,576]{3,2,1,0:T(8,128)(2,1)} %get-tuple-element.137.refs_2_, ...), custom_call_target="tpu_custom_call" | custom-call | flops 7247757312 | bytes 8847360 | tf_op jit(solution)/shard_map/attend_back/pallas_call | solution.py:1056
  679.2 12.7 %collective-permute-done.63.refs_5_ = bf16[576,1440]{1,0:T(8,128)(2,1)S(1)} collective-permute-done((bf16[576,1440]{1,0:T(8,128)(2,1)}, bf16[576,1440]{1,0:T(8,128)(2,1)S(1)}, u32[]{:S(2)}, u32[]{:S(2)}) %collective-permute-start.63) | collective-permute-done | bytes 1658912 | tf_op jit(solution)/shard_map/ppermute | solution.py:36
  727.6 11.9 %bitcast_convert_fusion.refs_1_.refs_2_ = bf16[2304,1728]{1,0:T(8,128)(2,1)S(1)} fusion(bf16[4,256,2304]{2,1,0:T(8,128)(2,1)} %get-tuple-element.220, bf16[4,256,1728]{2,1,0:T(8,128)(2,1)} %join_grads.1.refs_1_), kind=kOutput, calls=%fused_computation.8 | convolution fusion | flops 8157708288 | bytes 16220160 | tf_op jit(solution)/shard_map/dot_general | solution.py:301
  757.0 16.5 %terms.5 = (bf16[256,2304]{1,0:T(8,128)(2,1)}, bf16[256,2304]{1,0:T(8,128)(2,1)}, bf16[2,256,2304]{2,1,0:T(8,128)(2,1)}) custom-call(s32[3]{0:T(128)} %pad_add_fusion.2.refs_0_.where, bf16[4,256,1728]{2,1,0:T(8,128)(2,1)} %join_grads.1.refs_1_, bf16[2304,1728]{1,0:T(8,128)(2,1)} %get-tuple-element.224.refs_2_), custom_call_target="tpu_custom_call" | custom-call | flops 8153726976 | bytes 11501568 | tf_op jit(solution)/shard_map/terms/pallas_call | solution.py:722
  845.8 12.8 %collective-permute-start.78 = (bf16[288,1728]{1,0:T(8,128)(2,1)}, bf16[288,1728]{1,0:T(8,128)(2,1)}, u32[]{:S(2)}, u32[]{:S(2)}) collective-permute-start(bf16[288,1728]{1,0:T(8,128)(2,1)} %get-tuple-element.242), channel_id=1, source_target_pairs={{0,8},{8,16},{16,24},{24,28},{28,20},{20,12},{12,4},{4,0},{1,9},{9... | collective-permute-start | bytes 2985992 | tf_op jit(solution)/shard_map/ppermute | solution.py:36
  874.2 11.1 %collective-permute-done.78.refs_3_ = bf16[288,1728]{1,0:T(8,128)(2,1)} collective-permute-done((bf16[288,1728]{1,0:T(8,128)(2,1)}, bf16[288,1728]{1,0:T(8,128)(2,1)}, u32[]{:S(2)}, u32[]{:S(2)}) %collective-permute-start.78) | collective-permute-done | bytes 995360 | tf_op jit(solution)/shard_map/ppermute | solution.py:36
  914.8 12.8 %collective-permute-done.85 = bf16[288,1728]{1,0:T(8,128)(2,1)} collective-permute-done((bf16[288,1728]{1,0:T(8,128)(2,1)}, bf16[288,1728]{1,0:T(8,128)(2,1)}, u32[]{:S(2)}, u32[]{:S(2)}) %collective-permute-start.85) | collective-permute-done | bytes 995360 | tf_op jit(solution)/shard_map/ppermute | solution.py:36
  (475 shorter events, 499.9 us)
Async XLA Ops:
  6.4 82.3 %all-to-all-start = ((bf16[8,32,2304]{2,1,0:T(8,128)(2,1)}), bf16[8,32,2304]{2,1,0:T(8,128)(2,1)S(1)}, u32[]{:S(2)}, u32[]{:S(2)}) async-start(bf16[8,32,2304]{2,1,0:T(8,128)(2,1)} %bitcast.3), calls=%async_computation | async-start | bytes 2359296 | tf_op jit(solution)/shard_map/all_to_all | solution.py:1159
  16.5 46.7 %collective-permute-start.3 = (bf16[288,1728]{1,0:T(8,128)(2,1)S(1)}, bf16[288,1728]{1,0:T(8,128)(2,1)}, u32[]{:S(2)}, u32[]{:S(2)}) collective-permute-start(bf16[288,1728]{1,0:T(8,128)(2,1)S(1)} %concatenate.43.refs_1_), channel_id=1, source_target_pairs={{0,4},{8,0},{16,8},{24,16},{28,24},{20,28},{12,20},{4,12},{1,5},{9... | collective-permute-start | bytes 2985992 | tf_op jit(solution)/shard_map/ppermute | solution.py:36
  114.9 42.7 %collective-permute-start.16 = (bf16[256,2304]{1,0:T(8,128)(2,1)S(1)}, bf16[256,2304]{1,0:T(8,128)(2,1)}, u32[]{:S(2)}, u32[]{:S(2)}) collective-permute-start(bf16[256,2304]{1,0:T(8,128)(2,1)S(1)} %fusion.11.refs_10_), channel_id=1, source_target_pairs={{0,1},{1,0},{2,3},{3,2},{4,5},{5,4},{6,7},{7,6},{8,9},{9,8},{10,11... | collective-permute-start | bytes 3538952 | tf_op jit(solution)/shard_map/ppermute | solution.py:219
  156.7 87.6 %collective-permute-start.22 = (bf16[576,1440]{1,0:T(8,128)(2,1)}, bf16[576,1440]{1,0:T(8,128)(2,1)}, u32[]{:S(2)}, u32[]{:S(2)}) collective-permute-start(bf16[576,1440]{1,0:T(8,128)(2,1)} %pad_maximum_fusion), channel_id=1, source_target_pairs={{0,8},{8,16},{16,24},{24,28},{28,20},{20,12},{12,4},{4,0},{1,9},{9... | collective-permute-start | bytes 4976648 | tf_op jit(solution)/shard_map/ppermute | solution.py:36
  157.6 86.7 %collective-permute-start.23 = (bf16[576,1440]{1,0:T(8,128)(2,1)}, bf16[576,1440]{1,0:T(8,128)(2,1)}, u32[]{:S(2)}, u32[]{:S(2)}) collective-permute-start(bf16[576,1440]{1,0:T(8,128)(2,1)} %pad_maximum_fusion), channel_id=1, source_target_pairs={{0,4},{8,0},{16,8},{24,16},{28,24},{20,28},{12,20},{4,12},{1,5},{9... | collective-permute-start | bytes 4976648 | tf_op jit(solution)/shard_map/ppermute | solution.py:36
  176.7 54.1 %collective-permute-start.19 = (bf16[4,128,1152]{2,1,0:T(8,128)(2,1)}, bf16[4,128,1152]{2,1,0:T(8,128)(2,1)}, u32[]{:S(2)}, u32[]{:S(2)}) collective-permute-start(bf16[4,128,1152]{2,1,0:T(8,128)(2,1)} %get-tuple-element.138.refs_3_), channel_id=1, source_target_pairs={{0,4},{4,8},{8,12},{12,16},{16,20},{20,24},{24,28},{1,5},{5,9},{9,... | collective-permute-start | bytes 3538952 | tf_op jit(solution)/shard_map/ppermute | solution.py:1115
  181.6 77.1 %all-to-all-start.1 = ((bf16[8,32,2304]{2,1,0:T(8,128)(2,1)}), bf16[8,32,2304]{2,1,0:T(8,128)(2,1)S(1)}, u32[]{:S(2)}, u32[]{:S(2)}) async-start(bf16[8,32,2304]{2,1,0:T(8,128)(2,1)} %bitcast.26), calls=%async_computation.1 | async-start | bytes 2359296 | tf_op jit(solution)/shard_map/all_to_all | solution.py:1159
  188.3 58.6 %collective-permute-start.12 = (bf16[144,576]{1,0:T(8,128)(2,1)S(1)}, bf16[144,576]{1,0:T(8,128)(2,1)S(1)}, u32[]{:S(2)}, u32[]{:S(2)}) collective-permute-start(bf16[144,576]{1,0:T(8,128)(2,1)S(1)} %slice.170), channel_id=1, source_target_pairs={{0,8},{8,16},{16,24},{24,28},{28,20},{20,12},{12,4},{4,0},{1,9},{9... | collective-permute-start | bytes 497672 | tf_op jit(solution)/shard_map/ppermute | solution.py:36
  190.2 56.7 %collective-permute-start.13 = (bf16[144,576]{1,0:T(8,128)(2,1)S(1)}, bf16[144,576]{1,0:T(8,128)(2,1)S(1)}, u32[]{:S(2)}, u32[]{:S(2)}) collective-permute-start(bf16[144,576]{1,0:T(8,128)(2,1)S(1)} %slice.171), channel_id=1, source_target_pairs={{0,4},{8,0},{16,8},{24,16},{28,24},{20,28},{12,20},{4,12},{1,5},{9... | collective-permute-start | bytes 497672 | tf_op jit(solution)/shard_map/ppermute | solution.py:36
  319.5 42.3 %collective-permute-start.41 = (bf16[256,2304]{1,0:T(8,128)(2,1)}, bf16[256,2304]{1,0:T(8,128)(2,1)S(1)}, u32[]{:S(2)}, u32[]{:S(2)}) collective-permute-start(bf16[256,2304]{1,0:T(8,128)(2,1)} %fusion.2), channel_id=1, source_target_pairs={{0,1},{1,0},{2,3},{3,2},{4,5},{5,4},{6,7},{7,6},{8,9},{9,8},{10,11... | collective-permute-start | bytes 3538952 | tf_op jit(solution)/shard_map/ppermute | solution.py:219
  319.5 46.0 %collective-permute-start.43 = (bf16[256,2304]{1,0:T(8,128)(2,1)}, bf16[256,2304]{1,0:T(8,128)(2,1)S(1)}, u32[]{:S(2)}, u32[]{:S(2)}) collective-permute-start(bf16[256,2304]{1,0:T(8,128)(2,1)} %collective-permute-done.42), channel_id=1, source_target_pairs={{0,1},{1,0},{2,3},{3,2},{4,5},{5,4},{6,7},{7,6},{8,9},{9,8},{10,11... | collective-permute-start | bytes 3538952 | tf_op jit(solution)/shard_map/ppermute | solution.py:219
  365.4 44.0 %collective-permute-start.28 = (bf16[288,1440]{1,0:T(8,128)(2,1)S(1)}, bf16[288,1440]{1,0:T(8,128)(2,1)S(1)}, u32[]{:S(2)}, u32[]{:S(2)}) collective-permute-start(bf16[288,1440]{1,0:T(8,128)(2,1)S(1)} %slice.180), channel_id=1, source_target_pairs={{0,8},{8,16},{16,24},{24,28},{28,20},{20,12},{12,4},{4,0},{1,9},{9... | collective-permute-start | bytes 2488328 | tf_op jit(solution)/shard_map/ppermute | solution.py:36
  365.4 45.3 %collective-permute-start.29 = (bf16[288,1440]{1,0:T(8,128)(2,1)S(1)}, bf16[288,1440]{1,0:T(8,128)(2,1)S(1)}, u32[]{:S(2)}, u32[]{:S(2)}) collective-permute-start(bf16[288,1440]{1,0:T(8,128)(2,1)S(1)} %slice.181), channel_id=1, source_target_pairs={{0,4},{8,0},{16,8},{24,16},{28,24},{20,28},{12,20},{4,12},{1,5},{9... | collective-permute-start | bytes 2488328 | tf_op jit(solution)/shard_map/ppermute | solution.py:36
  407.5 47.5 %collective-permute-start.39 = (bf16[144,1440]{1,0:T(8,128)(2,1)S(1)}, bf16[144,1440]{1,0:T(8,128)(2,1)}, u32[]{:S(2)}, u32[]{:S(2)}) collective-permute-start(bf16[144,1440]{1,0:T(8,128)(2,1)S(1)} %slice.182), channel_id=1, source_target_pairs={{0,8},{8,16},{16,24},{24,28},{28,20},{20,12},{12,4},{4,0},{1,9},{9... | collective-permute-start | bytes 1244168 | tf_op jit(solution)/shard_map/ppermute | solution.py:36
  409.4 45.7 %collective-permute-start.40 = (bf16[144,1440]{1,0:T(8,128)(2,1)}, bf16[144,1440]{1,0:T(8,128)(2,1)}, u32[]{:S(2)}, u32[]{:S(2)}) collective-permute-start(bf16[144,1440]{1,0:T(8,128)(2,1)} %slice.183), channel_id=1, source_target_pairs={{0,4},{8,0},{16,8},{24,16},{28,24},{20,28},{12,20},{4,12},{1,5},{9... | collective-permute-start | bytes 1244168 | tf_op jit(solution)/shard_map/ppermute | solution.py:36
  599.1 41.2 %collective-permute-start.59 = (bf16[576,1440]{1,0:T(8,128)(2,1)}, bf16[576,1440]{1,0:T(8,128)(2,1)S(1)}, u32[]{:S(2)}, u32[]{:S(2)}) collective-permute-start(bf16[576,1440]{1,0:T(8,128)(2,1)} %get-tuple-element.190), channel_id=1, source_target_pairs={{0,8},{8,16},{16,24},{24,28},{28,20},{20,12},{12,4},{4,0},{1,9},{9... | collective-permute-start | bytes 4976648 | tf_op jit(solution)/shard_map/ppermute | solution.py:36
  601.8 50.4 %collective-permute-start.61 = (bf16[256,2304]{1,0:T(8,128)(2,1)S(1)}, bf16[256,2304]{1,0:T(8,128)(2,1)}, u32[]{:S(2)}, u32[]{:S(2)}) collective-permute-start(bf16[256,2304]{1,0:T(8,128)(2,1)S(1)} %copy-done.24), channel_id=1, source_target_pairs={{0,1},{1,0},{2,3},{3,2},{4,5},{5,4},{6,7},{7,6},{8,9},{9,8},{10,11... | collective-permute-start | bytes 3538952 | tf_op jit(solution)/shard_map/ppermute | solution.py:219
  650.1 41.8 %collective-permute-start.63 = (bf16[576,1440]{1,0:T(8,128)(2,1)}, bf16[576,1440]{1,0:T(8,128)(2,1)S(1)}, u32[]{:S(2)}, u32[]{:S(2)}) collective-permute-start(bf16[576,1440]{1,0:T(8,128)(2,1)} %get-tuple-element.204), channel_id=1, source_target_pairs={{0,8},{8,16},{16,24},{24,28},{28,20},{20,12},{12,4},{4,0},{1,9},{9... | collective-permute-start | bytes 4976648 | tf_op jit(solution)/shard_map/ppermute | solution.py:36
  651.9 41.9 %collective-permute-start.64 = (bf16[576,1440]{1,0:T(8,128)(2,1)}, bf16[576,1440]{1,0:T(8,128)(2,1)}, u32[]{:S(2)}, u32[]{:S(2)}) collective-permute-start(bf16[576,1440]{1,0:T(8,128)(2,1)} %get-tuple-element.205), channel_id=1, source_target_pairs={{0,4},{8,0},{16,8},{24,16},{28,24},{20,28},{12,20},{4,12},{1,5},{9... | collective-permute-start | bytes 4976648 | tf_op jit(solution)/shard_map/ppermute | solution.py:36
  699.9 55.3 %collective-permute-start.66 = (bf16[576,1440]{1,0:T(8,128)(2,1)}, bf16[576,1440]{1,0:T(8,128)(2,1)}, u32[]{:S(2)}, u32[]{:S(2)}) collective-permute-start(bf16[576,1440]{1,0:T(8,128)(2,1)} %get-tuple-element.207), channel_id=1, source_target_pairs={{0,8},{8,16},{16,24},{24,28},{28,20},{20,12},{12,4},{4,0},{1,9},{9... | collective-permute-start | bytes 4976648 | tf_op jit(solution)/shard_map/ppermute | solution.py:36
  701.7 55.3 %collective-permute-start.67 = (bf16[576,1440]{1,0:T(8,128)(2,1)}, bf16[576,1440]{1,0:T(8,128)(2,1)}, u32[]{:S(2)}, u32[]{:S(2)}) collective-permute-start(bf16[576,1440]{1,0:T(8,128)(2,1)} %get-tuple-element.208), channel_id=1, source_target_pairs={{0,4},{8,0},{16,8},{24,16},{28,24},{20,28},{12,20},{4,12},{1,5},{9... | collective-permute-start | bytes 4976648 | tf_op jit(solution)/shard_map/ppermute | solution.py:36
  827.0 87.6 %all-to-all-start.3 = ((bf16[8,40,2304]{2,1,0:T(8,128)(2,1)}), bf16[8,40,2304]{2,1,0:T(8,128)(2,1)S(1)}, u32[]{:S(2)}, u32[]{:S(2)}) async-start(bf16[8,40,2304]{2,1,0:T(8,128)(2,1)} %pad_maximum_fusion.1), calls=%async_computation.3 | async-start | bytes 2949120 | tf_op jit(solution)/shard_map/all_to_all | solution.py:1159
  869.3 45.2 %collective-permute-start.80 = (bf16[288,576]{1,0:T(8,128)(2,1)}, bf16[288,576]{1,0:T(8,128)(2,1)S(1)}, u32[]{:S(2)}, u32[]{:S(2)}) collective-permute-start(bf16[288,576]{1,0:T(8,128)(2,1)} %get-tuple-element.245), channel_id=1, source_target_pairs={{0,8},{8,16},{16,24},{24,28},{28,20},{20,12},{12,4},{4,0},{1,9},{9... | collective-permute-start | bytes 995336 | tf_op jit(solution)/shard_map/ppermute | solution.py:36
  871.3 43.2 %collective-permute-start.81 = (bf16[288,576]{1,0:T(8,128)(2,1)}, bf16[288,576]{1,0:T(8,128)(2,1)S(1)}, u32[]{:S(2)}, u32[]{:S(2)}) collective-permute-start(bf16[288,576]{1,0:T(8,128)(2,1)} %get-tuple-element.246), channel_id=1, source_target_pairs={{0,4},{8,0},{16,8},{24,16},{28,24},{20,28},{12,20},{4,12},{1,5},{9... | collective-permute-start | bytes 995336 | tf_op jit(solution)/shard_map/ppermute | solution.py:36
  (153 other events, 3561.5 us)

commit v3 on v2

--- a/solution.py
+++ b/solution.py
@@ -54,8 +54,8 @@
         self.marks = self.marks + tuple(arrived)
 
 
-PLAN = {'r1': 'wd', 'r2': 'split', 'r3': 'da2', 'r4': 'wu', 'e1': 'wu', 'e2': 'far3', 'e3': 'both3', 'e4': 'back2', 'u1': 'wqkv', 'u2': 'da1', 'u3': 'norm4', 'o1': '@q3', 'g1': '@o3', 'd1': '@g3', 'O': 'da1', 'P6': 1, 'W': 'wqkv', 'f1': 'wo', 'f2': 'da1', 'f3': 'norm4', 'f4': 'deal'}
-LAND = {'r1': 'da2', 'r2': 'wg', 'r3': 'yf', 'r4': 'norm3', 'e1': 'norm3', 'e2': 'mixed', 'e3': 'back1', 'e4': 'da1', 'u1': 'sum4', 'u3': 'unpack', 'f1': 'sum4', 'f2': 'norm4', 'f3': 'unpack'}
+PLAN = {'r1': 'wd', 'r2': 'split', 'r3': 'da2', 'r4': 'wu', 'e1': 'wu', 'e2': 'far3', 'e3': 'both3', 'e4': 'back2', 'u1': 'wqkv', 'u2': 'da1', 'u3': 'norm4', 'o1': '@q3', 'g1': '@o3', 'd1': '@g3', 'C': 'attend1', 'O': 'da1', 'P6': 1, 'W': 'wqkv', 'f1': 'wo', 'f2': 'da1', 'f3': 'norm4', 'f4': 'deal'}
+LAND = {'r1': 'da2', 'r2': 'wg', 'r3': 'yf', 'r4': 'both3', 'e1': 'both3', 'e2': 'mixed', 'e3': 'back1', 'e4': 'da1', 'u1': 'sum4', 'u3': 'unpack', 'f1': 'sum4', 'f2': 'norm4', 'f3': 'unpack'}
 MADE = {'e4': 'back1', 'e2': 'gather3'}
 
 
@@ -99,9 +99,8 @@
                 marks += self.hop(name)
         for name, ready in MADE.items():
             if ready == step and self.sent.get(name[0], 0) >= int(name[1]):
-                marks += self.rings[name[0]].messages[int(name[1]) - 1 :][:1] and list(
-                    self.rings[name[0]].messages[int(name[1]) - 1]
-                )
+                messages = self.rings[name[0]].messages
+                marks += messages[int(name[1]) - 1] if messages else ()
         return after(value, *marks)
 
 

time: 956 us -> 945 us (0.988)
  transfers between devices with their start and end apart: 92 -> 92, of which waited for: 42 -> 38; matrix products, arithmetic and copies ran while one was open for 15% -> 15% of each run, Pallas kernels for 25% -> 25%
where the time goes in v3:
time: 945 us; the launch traced here: 936 us
  waiting for transfers between devices  378 us (40%)
  Pallas kernels  247 us (26%)
  starting transfers between devices  147 us (16%)
  other arithmetic  62.8 us (7%)
  matrix products  50.7 us (5%)
  local copies, waits for them, and re-layouts  48.6 us (5%)
    ppermute x64, waiting for transfers between devices, ring_send(): return lax.ppermute(block, 'wide', route)  291 us
    ppermute x64, starting transfers between devices, ring_send(): return lax.ppermute(block, 'wide', route)  110 us
    pallas_call x3, Pallas kernels, terms(): pl.pallas_call(lambda *refs: terms_kernel(len(pairs), *refs), out_shape=s...  55.6 us
    pallas_call x12, Pallas kernels, ring_add(): pl.pallas_call(lambda *refs: ring_add_kernel(count, split, *refs), out_sh...  51.4 us
    dot_general x5, matrix products, contract_rows(): lax.dot_general(left, right, (((0,), (0,)), ((), ())), preferred_element_...  50.7 us
    ppermute x8, waiting for transfers between devices, swap_chip(): return lax.ppermute(block, 'narrow', [(0, 2), (1, 3), (2, 0), (3, 1)])  41.4 us
    ppermute x2, waiting for transfers between devices, to_next(): lax.ppermute(block, 'wide', [(b, a) for a, b in route] if direction < 0 e...  32.5 us
    pallas_call x2, Pallas kernels, attend_back(): pl.pallas_call(lambda *refs: attend_back_kernel(with_prev, *refs), out_sh...  27.3 us
  transfers between devices with their start and end apart: 92, of which 38 were waited for; matrix products, arithmetic and copies ran while one was open for 15% of the time, Pallas kernels for 25%

profile of v3, /device:TPU:0, one launch (start us, length us, event | category | flops | bytes accessed | tf_op | source)
XLA Modules:
  0.0 936.2 jit_solution(4842717712601721535)
XLA Ops:
  17.0 38.4 %collective-permute-done.refs_2_ = bf16[288,1728]{1,0:T(8,128)(2,1)S(1)} collective-permute-done((bf16[288,1728]{1,0:T(8,128)(2,1)S(1)}, bf16[288,1728]{1,0:T(8,128)(2,1)S(1)}, u32[]{:S(2)}, u32[]{:S(2)}) %collective-permute-start) | collective-permute-done | bytes 995360 | tf_op jit(solution)/shard_map/ppermute | solution.py:36
  63.8 21.7 %collective-permute-done.1.refs_4_ = bf16[288,1728]{1,0:T(8,128)(2,1)} collective-permute-done((bf16[288,1728]{1,0:T(8,128)(2,1)S(1)}, bf16[288,1728]{1,0:T(8,128)(2,1)}, u32[]{:S(2)}, u32[]{:S(2)}) %collective-permute-start.1) | collective-permute-done | bytes 995360 | tf_op jit(solution)/shard_map/ppermute | solution.py:36
  92.0 18.4 %collective-permute-done.2.refs_6_ = bf16[288,1728]{1,0:T(8,128)(2,1)} collective-permute-done((bf16[288,1728]{1,0:T(8,128)(2,1)}, bf16[288,1728]{1,0:T(8,128)(2,1)}, u32[]{:S(2)}, u32[]{:S(2)}) %collective-permute-start.2) | collective-permute-done | bytes 995360 | tf_op jit(solution)/shard_map/ppermute | solution.py:36
  155.7 17.8 %project.1 = (bf16[2,4,128,576]{3,2,1,0:T(8,128)(2,1)}, bf16[4,128,1152]{2,1,0:T(8,128)(2,1)}, bf16[4,128,1152]{2,1,0:T(8,128)(2,1)}, bf16[2304,1728]{1,0:T(8,128)(2,1)}, bf16[4,256,2304]{2,1,0:T(8,128)(2,1)}) custom-call(s32[3]{0:T(128)} %pad_add_fusion.2.refs_0_.where, bf16[288,1728]{1,0:T(8,128)(2,1)} %copy-done.31, bf16[288,1728]{1,0:T(8,128)(2,1)} %copy-done.62, ...), custom_call_target="tpu_custom_call" | custom-call | flops 8153726976 | bytes 23592960 | tf_op jit(solution)/shard_map/project/pallas_call | solution.py:507
  198.4 27.8 %collective-permute-done.19.refs_4_.refs_7_ = bf16[4,128,1152]{2,1,0:T(8,128)(2,1)} collective-permute-done((bf16[4,128,1152]{2,1,0:T(8,128)(2,1)}, bf16[4,128,1152]{2,1,0:T(8,128)(2,1)}, u32[]{:S(2)}, u32[]{:S(2)}) %collective-permute-start.19) | collective-permute-done | bytes 1179680 | tf_op jit(solution)/shard_map/ppermute | solution.py:1114
  226.2 13.6 %attend.3 = (bf16[4,128,576]{2,1,0:T(8,128)(2,1)}, f32[16,512]{1,0:T(8,128)}) custom-call(s32[2,1024,1]{2,1,0:T(8,128)} %add_select_fusion.refs_0_, s32[2,1,512]{2,1,0:T(1,128)} %broadcast_in_dim.151.refs_1_, bf16[2,4,128,576]{3,2,1,0:T(8,128)(2,1)} %get-tuple-element.138.refs_2_, bf16[4,128,1152]{2,1,0:T(8,128)(2,1)} %get-tuple-element.142.refs_3_, ...), custom_call_target="tpu_custom_call" | custom-call | flops 3019898880 | bytes 3538944 | tf_op jit(solution)/shard_map/attend/pallas_call | solution.py:946
  254.1 24.9 %collective-permute-done.24.refs_4_.refs_12_ = bf16[576,1440]{1,0:T(8,128)(2,1)} collective-permute-done((bf16[576,1440]{1,0:T(8,128)(2,1)}, bf16[576,1440]{1,0:T(8,128)(2,1)}, u32[]{:S(2)}, u32[]{:S(2)}) %collective-permute-start.24) | collective-permute-done | bytes 1658912 | tf_op jit(solution)/shard_map/ppermute | solution.py:36
  286.1 21.0 %collective-permute-done.26.refs_6_.refs_14_ = bf16[576,1440]{1,0:T(8,128)(2,1)} collective-permute-done((bf16[576,1440]{1,0:T(8,128)(2,1)}, bf16[576,1440]{1,0:T(8,128)(2,1)}, u32[]{:S(2)}, u32[]{:S(2)}) %collective-permute-start.26) | collective-permute-done | bytes 1658912 | tf_op jit(solution)/shard_map/ppermute | solution.py:36
  318.9 11.1 %collective-permute-done.21 = bf16[256,2304]{1,0:T(8,128)(2,1)} collective-permute-done((bf16[256,2304]{1,0:T(8,128)(2,1)S(1)}, bf16[256,2304]{1,0:T(8,128)(2,1)}, u32[]{:S(2)}, u32[]{:S(2)}) %collective-permute-start.21) | collective-permute-done | bytes 1179680 | tf_op jit(solution)/shard_map/ppermute | solution.py:214
  342.5 11.8 %collective-permute-done.35.refs_4_ = bf16[288,1440]{1,0:T(8,128)(2,1)S(1)} collective-permute-done((bf16[288,1440]{1,0:T(8,128)(2,1)}, bf16[288,1440]{1,0:T(8,128)(2,1)S(1)}, u32[]{:S(2)}, u32[]{:S(2)}) %collective-permute-start.35) | collective-permute-done | bytes 829472 | tf_op jit(solution)/shard_map/ppermute | solution.py:36
  366.9 11.7 %collective-permute-done.37.refs_6_ = bf16[288,1440]{1,0:T(8,128)(2,1)S(1)} collective-permute-done((bf16[288,1440]{1,0:T(8,128)(2,1)S(1)}, bf16[288,1440]{1,0:T(8,128)(2,1)S(1)}, u32[]{:S(2)}, u32[]{:S(2)}) %collective-permute-start.37) | collective-permute-done | bytes 829472 | tf_op jit(solution)/shard_map/ppermute | solution.py:36
  385.9 15.4 %collective-permute-done.38.refs_7_ = bf16[288,1440]{1,0:T(8,128)(2,1)S(1)} collective-permute-done((bf16[288,1440]{1,0:T(8,128)(2,1)S(1)}, bf16[288,1440]{1,0:T(8,128)(2,1)S(1)}, u32[]{:S(2)}, u32[]{:S(2)}) %collective-permute-start.38) | collective-permute-done | bytes 829472 | tf_op jit(solution)/shard_map/ppermute | solution.py:36
  407.3 25.1 %hidden_units.1 = (f32[4,256,1440]{2,1,0:T(8,128)}, f32[4,256,1440]{2,1,0:T(8,128)}, bf16[4,256,1440]{2,1,0:T(8,128)(2,1)}, bf16[2304,1440]{1,0:T(8,128)(2,1)}, ...) custom-call(s32[3]{0:T(128)} %pad_add_fusion.2.refs_0_.where, bf16[288,1440]{1,0:T(8,128)(2,1)} %refs_1_.1, ...), custom_call_target="tpu_custom_call" | custom-call | flops 13589544960 | bytes 22118400 | tf_op jit(solution)/shard_map/hidden_units/pallas_call | solution.py:642
  449.6 17.2 %split_grads.1 = (bf16[4,256,1440]{2,1,0:T(8,128)(2,1)}, bf16[4,256,1440]{2,1,0:T(8,128)(2,1)}, bf16[2304,1440]{1,0:T(8,128)(2,1)}) custom-call(s32[3]{0:T(128)} %pad_add_fusion.2.refs_0_.where, bf16[288,1440]{1,0:T(8,128)(2,1)} %bitcast.24.refs_1_, bf16[288,1440]{1,0:T(8,128)(2,1)} %collective-permute-done.33.refs_2_, bf16[288,1440]{1,0:T(8,128)(2,1)} %copy-done.63, ...), custom_call_target="tpu_custom_call" | custom-call | flops 6794772480 | bytes 22118400 | tf_op jit(solution)/shard_map/split_grads/pallas_call | solution.py:691
  473.1 24.4 %terms.3 = (bf16[256,2304]{1,0:T(8,128)(2,1)}, bf16[256,2304]{1,0:T(8,128)(2,1)}, bf16[2,256,2304]{2,1,0:T(8,128)(2,1)}) custom-call(s32[3]{0:T(128)} %pad_add_fusion.2.refs_0_.where, bf16[4,256,1440]{2,1,0:T(8,128)(2,1)} %get-tuple-element.171.refs_1_, bf16[4,256,1440]{2,1,0:T(8,128)(2,1)} %get-tuple-element.173.refs_2_, ...), custom_call_target="tpu_custom_call" | custom-call | flops 13589544960 | bytes 19169280 | tf_op jit(solution)/shard_map/terms/pallas_call | solution.py:721
  537.3 14.7 %terms.4 = (bf16[256,2304]{1,0:T(8,128)(2,1)}, bf16[256,2304]{1,0:T(8,128)(2,1)}, bf16[2,256,2304]{2,1,0:T(8,128)(2,1)}) custom-call(s32[3]{0:T(128)} %pad_add_fusion.2.refs_0_.where, bf16[4,256,1440]{2,1,0:T(8,128)(2,1)} %get-tuple-element.178.refs_1_, bf16[2304,1440]{1,0:T(8,128)(2,1)} %get-tuple-element.179.refs_2_), custom_call_target="tpu_custom_call" | custom-call | flops 6794772480 | bytes 9584640 | tf_op jit(solution)/shard_map/terms/pallas_call | solution.py:721
  574.0 21.4 %collective-permute-done.55.refs_3_ = bf16[256,2304]{1,0:T(8,128)(2,1)} collective-permute-done((bf16[256,2304]{1,0:T(8,128)(2,1)S(1)}, bf16[256,2304]{1,0:T(8,128)(2,1)}, u32[]{:S(2)}, u32[]{:S(2)}) %collective-permute-start.55) | collective-permute-done | bytes 1179680 | tf_op jit(solution)/shard_map/ppermute | solution.py:214
  597.3 30.3 %collective-permute-done.56 = bf16[288,1440]{1,0:T(8,128)(2,1)} collective-permute-done((bf16[288,1440]{1,0:T(8,128)(2,1)}, bf16[288,1440]{1,0:T(8,128)(2,1)}, u32[]{:S(2)}, u32[]{:S(2)}) %collective-permute-start.56) | collective-permute-done | bytes 829472 | tf_op jit(solution)/shard_map/ppermute | solution.py:36
  649.1 16.6 %attend_back.2 = (f32[4,128,576]{2,1,0:T(8,128)}, f32[4,128,576]{2,1,0:T(8,128)}, f32[4,128,576]{2,1,0:T(8,128)}, bf16[4,128,1152]{2,1,0:T(8,128)(2,1)}) custom-call(s32[2,1024,1]{2,1,0:T(8,128)} %add_select_fusion.refs_0_, s32[2,1,512]{2,1,0:T(1,128)} %broadcast_in_dim.151.refs_1_, bf16[2,4,128,576]{3,2,1,0:T(8,128)(2,1)} %get-tuple-element.138.refs_2_, ...), custom_call_target="tpu_custom_call" | custom-call | flops 7247757312 | bytes 8847360 | tf_op jit(solution)/shard_map/attend_back/pallas_call | solution.py:1055
  667.4 12.1 %collective-permute-done.63.refs_5_ = bf16[576,1440]{1,0:T(8,128)(2,1)S(1)} collective-permute-done((bf16[576,1440]{1,0:T(8,128)(2,1)}, bf16[576,1440]{1,0:T(8,128)(2,1)S(1)}, u32[]{:S(2)}, u32[]{:S(2)}) %collective-permute-start.63) | collective-permute-done | bytes 1658912 | tf_op jit(solution)/shard_map/ppermute | solution.py:36
  715.2 11.9 %bitcast_convert_fusion.refs_1_.refs_2_ = bf16[2304,1728]{1,0:T(8,128)(2,1)S(1)} fusion(bf16[4,256,2304]{2,1,0:T(8,128)(2,1)} %get-tuple-element.222, bf16[4,256,1728]{2,1,0:T(8,128)(2,1)} %join_grads.1.refs_1_), kind=kOutput, calls=%fused_computation.8 | convolution fusion | flops 8157708288 | bytes 16220160 | tf_op jit(solution)/shard_map/dot_general | solution.py:300
  744.6 16.5 %terms.5 = (bf16[256,2304]{1,0:T(8,128)(2,1)}, bf16[256,2304]{1,0:T(8,128)(2,1)}, bf16[2,256,2304]{2,1,0:T(8,128)(2,1)}) custom-call(s32[3]{0:T(128)} %pad_add_fusion.2.refs_0_.where, bf16[4,256,1728]{2,1,0:T(8,128)(2,1)} %join_grads.1.refs_1_, bf16[2304,1728]{1,0:T(8,128)(2,1)} %get-tuple-element.226.refs_2_), custom_call_target="tpu_custom_call" | custom-call | flops 8153726976 | bytes 11501568 | tf_op jit(solution)/shard_map/terms/pallas_call | solution.py:721
  834.1 13.3 %collective-permute-start.78 = (bf16[288,1728]{1,0:T(8,128)(2,1)}, bf16[288,1728]{1,0:T(8,128)(2,1)}, u32[]{:S(2)}, u32[]{:S(2)}) collective-permute-start(bf16[288,1728]{1,0:T(8,128)(2,1)} %get-tuple-element.244), channel_id=1, source_target_pairs={{0,8},{8,16},{16,24},{24,28},{28,20},{20,12},{12,4},{4,0},{1,9},{9... | collective-permute-start | bytes 2985992 | tf_op jit(solution)/shard_map/ppermute | solution.py:36
  903.2 12.6 %collective-permute-done.85 = bf16[288,1728]{1,0:T(8,128)(2,1)} collective-permute-done((bf16[288,1728]{1,0:T(8,128)(2,1)}, bf16[288,1728]{1,0:T(8,128)(2,1)}, u32[]{:S(2)}, u32[]{:S(2)}) %collective-permute-start.85) | collective-permute-done | bytes 995360 | tf_op jit(solution)/shard_map/ppermute | solution.py:36
  (457 shorter events, 484.3 us)
Async XLA Ops:
  6.4 82.3 %all-to-all-start = ((bf16[8,32,2304]{2,1,0:T(8,128)(2,1)}), bf16[8,32,2304]{2,1,0:T(8,128)(2,1)S(1)}, u32[]{:S(2)}, u32[]{:S(2)}) async-start(bf16[8,32,2304]{2,1,0:T(8,128)(2,1)} %bitcast.3), calls=%async_computation | async-start | bytes 2359296 | tf_op jit(solution)/shard_map/all_to_all | solution.py:1158
  16.5 46.7 %collective-permute-start.3 = (bf16[288,1728]{1,0:T(8,128)(2,1)S(1)}, bf16[288,1728]{1,0:T(8,128)(2,1)}, u32[]{:S(2)}, u32[]{:S(2)}) collective-permute-start(bf16[288,1728]{1,0:T(8,128)(2,1)S(1)} %concatenate.43.refs_1_), channel_id=1, source_target_pairs={{0,4},{8,0},{16,8},{24,16},{28,24},{20,28},{12,20},{4,12},{1,5},{9... | collective-permute-start | bytes 2985992 | tf_op jit(solution)/shard_map/ppermute | solution.py:36
  153.6 86.2 %collective-permute-start.22 = (bf16[576,1440]{1,0:T(8,128)(2,1)}, bf16[576,1440]{1,0:T(8,128)(2,1)}, u32[]{:S(2)}, u32[]{:S(2)}) collective-permute-start(bf16[576,1440]{1,0:T(8,128)(2,1)} %pad_maximum_fusion), channel_id=1, source_target_pairs={{0,8},{8,16},{16,24},{24,28},{28,20},{20,12},{12,4},{4,0},{1,9},{9... | collective-permute-start | bytes 4976648 | tf_op jit(solution)/shard_map/ppermute | solution.py:36
  154.2 86.4 %collective-permute-start.23 = (bf16[576,1440]{1,0:T(8,128)(2,1)}, bf16[576,1440]{1,0:T(8,128)(2,1)}, u32[]{:S(2)}, u32[]{:S(2)}) collective-permute-start(bf16[576,1440]{1,0:T(8,128)(2,1)} %pad_maximum_fusion), channel_id=1, source_target_pairs={{0,4},{8,0},{16,8},{24,16},{28,24},{20,28},{12,20},{4,12},{1,5},{9... | collective-permute-start | bytes 4976648 | tf_op jit(solution)/shard_map/ppermute | solution.py:36
  173.5 52.7 %collective-permute-start.19 = (bf16[4,128,1152]{2,1,0:T(8,128)(2,1)}, bf16[4,128,1152]{2,1,0:T(8,128)(2,1)}, u32[]{:S(2)}, u32[]{:S(2)}) collective-permute-start(bf16[4,128,1152]{2,1,0:T(8,128)(2,1)} %get-tuple-element.139.refs_3_), channel_id=1, source_target_pairs={{0,4},{4,8},{8,12},{12,16},{16,20},{20,24},{24,28},{1,5},{5,9},{9,... | collective-permute-start | bytes 3538952 | tf_op jit(solution)/shard_map/ppermute | solution.py:1114
  181.1 61.3 %collective-permute-start.12 = (bf16[144,576]{1,0:T(8,128)(2,1)}, bf16[144,576]{1,0:T(8,128)(2,1)}, u32[]{:S(2)}, u32[]{:S(2)}) collective-permute-start(bf16[144,576]{1,0:T(8,128)(2,1)} %slice.170), channel_id=1, source_target_pairs={{0,8},{8,16},{16,24},{24,28},{28,20},{20,12},{12,4},{4,0},{1,9},{9... | collective-permute-start | bytes 497672 | tf_op jit(solution)/shard_map/ppermute | solution.py:36
  181.1 61.3 %collective-permute-start.13 = (bf16[144,576]{1,0:T(8,128)(2,1)}, bf16[144,576]{1,0:T(8,128)(2,1)}, u32[]{:S(2)}, u32[]{:S(2)}) collective-permute-start(bf16[144,576]{1,0:T(8,128)(2,1)} %slice.171), channel_id=1, source_target_pairs={{0,4},{8,0},{16,8},{24,16},{28,24},{20,28},{12,20},{4,12},{1,5},{9... | collective-permute-start | bytes 497672 | tf_op jit(solution)/shard_map/ppermute | solution.py:36
  194.6 58.8 %all-to-all-start.1 = ((bf16[8,32,2304]{2,1,0:T(8,128)(2,1)}), bf16[8,32,2304]{2,1,0:T(8,128)(2,1)S(1)}, u32[]{:S(2)}, u32[]{:S(2)}) async-start(bf16[8,32,2304]{2,1,0:T(8,128)(2,1)} %bitcast.26), calls=%async_computation.1 | async-start | bytes 2359296 | tf_op jit(solution)/shard_map/all_to_all | solution.py:1158
  285.5 44.5 %collective-permute-start.21 = (bf16[256,2304]{1,0:T(8,128)(2,1)S(1)}, bf16[256,2304]{1,0:T(8,128)(2,1)}, u32[]{:S(2)}, u32[]{:S(2)}) collective-permute-start(bf16[256,2304]{1,0:T(8,128)(2,1)S(1)} %fusion.31), channel_id=1, source_target_pairs={{0,2},{1,3},{2,0},{3,1},{4,6},{5,7},{6,4},{7,5},{8,10},{9,11},{10,... | collective-permute-start | bytes 3538952 | tf_op jit(solution)/shard_map/ppermute | solution.py:214
  312.8 45.2 %collective-permute-start.41 = (bf16[256,2304]{1,0:T(8,128)(2,1)}, bf16[256,2304]{1,0:T(8,128)(2,1)S(1)}, u32[]{:S(2)}, u32[]{:S(2)}) collective-permute-start(bf16[256,2304]{1,0:T(8,128)(2,1)} %fusion.2), channel_id=1, source_target_pairs={{0,1},{1,0},{2,3},{3,2},{4,5},{5,4},{6,7},{7,6},{8,9},{9,8},{10,11... | collective-permute-start | bytes 3538952 | tf_op jit(solution)/shard_map/ppermute | solution.py:218
  312.8 48.9 %collective-permute-start.43 = (bf16[256,2304]{1,0:T(8,128)(2,1)}, bf16[256,2304]{1,0:T(8,128)(2,1)S(1)}, u32[]{:S(2)}, u32[]{:S(2)}) collective-permute-start(bf16[256,2304]{1,0:T(8,128)(2,1)} %collective-permute-done.42), channel_id=1, source_target_pairs={{0,1},{1,0},{2,3},{3,2},{4,5},{5,4},{6,7},{7,6},{8,9},{9,8},{10,11... | collective-permute-start | bytes 3538952 | tf_op jit(solution)/shard_map/ppermute | solution.py:218
  361.7 43.7 %collective-permute-start.29 = (bf16[288,1440]{1,0:T(8,128)(2,1)S(1)}, bf16[288,1440]{1,0:T(8,128)(2,1)S(1)}, u32[]{:S(2)}, u32[]{:S(2)}) collective-permute-start(bf16[288,1440]{1,0:T(8,128)(2,1)S(1)} %slice.181), channel_id=1, source_target_pairs={{0,4},{8,0},{16,8},{24,16},{28,24},{20,28},{12,20},{4,12},{1,5},{9... | collective-permute-start | bytes 2488328 | tf_op jit(solution)/shard_map/ppermute | solution.py:36
  402.1 47.4 %collective-permute-start.39 = (bf16[144,1440]{1,0:T(8,128)(2,1)S(1)}, bf16[144,1440]{1,0:T(8,128)(2,1)}, u32[]{:S(2)}, u32[]{:S(2)}) collective-permute-start(bf16[144,1440]{1,0:T(8,128)(2,1)S(1)} %slice.182), channel_id=1, source_target_pairs={{0,8},{8,16},{16,24},{24,28},{28,20},{20,12},{12,4},{4,0},{1,9},{9... | collective-permute-start | bytes 1244168 | tf_op jit(solution)/shard_map/ppermute | solution.py:36
  402.4 47.1 %collective-permute-start.40 = (bf16[144,1440]{1,0:T(8,128)(2,1)}, bf16[144,1440]{1,0:T(8,128)(2,1)}, u32[]{:S(2)}, u32[]{:S(2)}) collective-permute-start(bf16[144,1440]{1,0:T(8,128)(2,1)} %slice.183), channel_id=1, source_target_pairs={{0,4},{8,0},{16,8},{24,16},{28,24},{20,28},{12,20},{4,12},{1,5},{9... | collective-permute-start | bytes 1244168 | tf_op jit(solution)/shard_map/ppermute | solution.py:36
  567.5 60.6 %collective-permute-start.59 = (bf16[576,1440]{1,0:T(8,128)(2,1)}, bf16[576,1440]{1,0:T(8,128)(2,1)}, u32[]{:S(2)}, u32[]{:S(2)}) collective-permute-start(bf16[576,1440]{1,0:T(8,128)(2,1)} %get-tuple-element.188), channel_id=1, source_target_pairs={{0,8},{8,16},{16,24},{24,28},{28,20},{20,12},{12,4},{4,0},{1,9},{9... | collective-permute-start | bytes 4976648 | tf_op jit(solution)/shard_map/ppermute | solution.py:36
  568.1 59.9 %collective-permute-start.60 = (bf16[576,1440]{1,0:T(8,128)(2,1)}, bf16[576,1440]{1,0:T(8,128)(2,1)}, u32[]{:S(2)}, u32[]{:S(2)}) collective-permute-start(bf16[576,1440]{1,0:T(8,128)(2,1)} %get-tuple-element.189), channel_id=1, source_target_pairs={{0,4},{8,0},{16,8},{24,16},{28,24},{20,28},{12,20},{4,12},{1,5},{9... | collective-permute-start | bytes 4976648 | tf_op jit(solution)/shard_map/ppermute | solution.py:36
  573.3 54.3 %collective-permute-start.56 = (bf16[288,1440]{1,0:T(8,128)(2,1)}, bf16[288,1440]{1,0:T(8,128)(2,1)}, u32[]{:S(2)}, u32[]{:S(2)}) collective-permute-start(bf16[288,1440]{1,0:T(8,128)(2,1)} %get-tuple-element.195), channel_id=1, source_target_pairs={{0,8},{8,16},{16,24},{24,28},{28,20},{20,12},{12,4},{4,0},{1,9},{9... | collective-permute-start | bytes 2488328 | tf_op jit(solution)/shard_map/ppermute | solution.py:36
  597.3 42.6 %collective-permute-start.61 = (bf16[256,2304]{1,0:T(8,128)(2,1)S(1)}, bf16[256,2304]{1,0:T(8,128)(2,1)}, u32[]{:S(2)}, u32[]{:S(2)}) collective-permute-start(bf16[256,2304]{1,0:T(8,128)(2,1)S(1)} %copy-done.24), channel_id=1, source_target_pairs={{0,1},{1,0},{2,3},{3,2},{4,5},{5,4},{6,7},{7,6},{8,9},{9,8},{10,11... | collective-permute-start | bytes 3538952 | tf_op jit(solution)/shard_map/ppermute | solution.py:218
  639.6 41.8 %collective-permute-start.64 = (bf16[576,1440]{1,0:T(8,128)(2,1)}, bf16[576,1440]{1,0:T(8,128)(2,1)}, u32[]{:S(2)}, u32[]{:S(2)}) collective-permute-start(bf16[576,1440]{1,0:T(8,128)(2,1)} %get-tuple-element.207), channel_id=1, source_target_pairs={{0,4},{8,0},{16,8},{24,16},{28,24},{20,28},{12,20},{4,12},{1,5},{9... | collective-permute-start | bytes 4976648 | tf_op jit(solution)/shard_map/ppermute | solution.py:36
  687.5 55.4 %collective-permute-start.66 = (bf16[576,1440]{1,0:T(8,128)(2,1)}, bf16[576,1440]{1,0:T(8,128)(2,1)}, u32[]{:S(2)}, u32[]{:S(2)}) collective-permute-start(bf16[576,1440]{1,0:T(8,128)(2,1)} %get-tuple-element.209), channel_id=1, source_target_pairs={{0,8},{8,16},{16,24},{24,28},{28,20},{20,12},{12,4},{4,0},{1,9},{9... | collective-permute-start | bytes 4976648 | tf_op jit(solution)/shard_map/ppermute | solution.py:36
  689.5 55.1 %collective-permute-start.67 = (bf16[576,1440]{1,0:T(8,128)(2,1)}, bf16[576,1440]{1,0:T(8,128)(2,1)}, u32[]{:S(2)}, u32[]{:S(2)}) collective-permute-start(bf16[576,1440]{1,0:T(8,128)(2,1)} %get-tuple-element.210), channel_id=1, source_target_pairs={{0,4},{8,0},{16,8},{24,16},{28,24},{20,28},{12,20},{4,12},{1,5},{9... | collective-permute-start | bytes 4976648 | tf_op jit(solution)/shard_map/ppermute | solution.py:36
  815.4 87.5 %all-to-all-start.3 = ((bf16[8,40,2304]{2,1,0:T(8,128)(2,1)}), bf16[8,40,2304]{2,1,0:T(8,128)(2,1)S(1)}, u32[]{:S(2)}, u32[]{:S(2)}) async-start(bf16[8,40,2304]{2,1,0:T(8,128)(2,1)} %pad_maximum_fusion.1), calls=%async_computation.3 | async-start | bytes 2949120 | tf_op jit(solution)/shard_map/all_to_all | solution.py:1158
  858.1 44.8 %collective-permute-start.80 = (bf16[288,576]{1,0:T(8,128)(2,1)}, bf16[288,576]{1,0:T(8,128)(2,1)S(1)}, u32[]{:S(2)}, u32[]{:S(2)}) collective-permute-start(bf16[288,576]{1,0:T(8,128)(2,1)} %get-tuple-element.247), channel_id=1, source_target_pairs={{0,8},{8,16},{16,24},{24,28},{28,20},{20,12},{12,4},{4,0},{1,9},{9... | collective-permute-start | bytes 995336 | tf_op jit(solution)/shard_map/ppermute | solution.py:36
  860.2 42.7 %collective-permute-start.81 = (bf16[288,576]{1,0:T(8,128)(2,1)}, bf16[288,576]{1,0:T(8,128)(2,1)S(1)}, u32[]{:S(2)}, u32[]{:S(2)}) collective-permute-start(bf16[288,576]{1,0:T(8,128)(2,1)} %get-tuple-element.248), channel_id=1, source_target_pairs={{0,4},{8,0},{16,8},{24,16},{28,24},{20,28},{12,20},{4,12},{1,5},{9... | collective-permute-start | bytes 995336 | tf_op jit(solution)/shard_map/ppermute | solution.py:36
  (144 other events, 3511.2 us)
